TPU v7x, 32 devices: a whole 2x2x4 slice. The times are simulated.
32 devices in a mesh: section: 2 (over x), expert: 8 (over z, y), replica: 2 (over core).
Axes of the slice: x: 2, y: 2, z: 4, core: 2. Of those that a mesh axis runs over, the one named last changes fastest.
Arguments:
- token_grads: bfloat16 [2, 512, 3584], P('section', 'expert', 'replica'), may hold values from -6 to 6
- routing: int32 [2, 512, 1], P('section', 'expert'), may hold values from 0 to 1; in each aligned block of 64 rows (0 to 63, 64 to 127, ..., all dimensions but the last counted through in order) at most 34 rows name the same one
- gate_weights: float32 [2, 512, 1], P('section', 'expert'), may hold values from 0.1 to 1
- layer_inputs: bfloat16 [2, 512, 3584], P('section', 'expert', 'replica'), may hold values from -6 to 6
- w_gate: bfloat16 [2, 3584, 2048], P('section', 'replica', 'expert'), may hold values from -0.09375 to 0.09375
- w_up: bfloat16 [2, 3584, 2048], P('section', 'replica', 'expert'), may hold values from -0.09375 to 0.09375
- w_down: bfloat16 [2, 3584, 2048], P('section', 'replica', 'expert'), may hold values from -0.09375 to 0.09375
Outputs:
- upstream: bfloat16 [2, 512, 3584], P('section', 'expert', 'replica')
- grad_gate: bfloat16 [2, 3584, 2048], P('section', 'replica', 'expert')
- grad_up: bfloat16 [2, 3584, 2048], P('section', 'replica', 'expert')
- grad_down: bfloat16 [2, 3584, 2048], P('section', 'replica', 'expert')
Inputs may be any that keep to these rules, and one draw needn't show every extreme that they name: `routing`: each token names 1 different experts. Among the 64 tokens of one group no expert is named more than 34 times, and in every draw some group names some expert exactly 34 times.
All inputs are finite; a program needn't handle non-finite values.
Results may differ from a plain program's by a relative error of at most 0.0064.
Values may be sent and summed in bfloat16 or wider, within the bound.
No kernel may reach another device: no remote copies, remote signals or barrier semaphores. Data moves between devices by JAX's collectives and lax.ppermute only.
A program may use at most 64 MiB of HBM per device.

v0:
```python
import jax
import jax.numpy as jnp
from jax import lax
from jax.sharding import PartitionSpec as P

SHARES = 4


def shifted(value, axis, steps):
    count = lax.axis_size(axis)
    first, last = (max(0, -steps), min(count, count - steps))
    return lax.ppermute(value, axis, [(source, source + steps) for source in range(first, last)])


def slot_index(routes, n_experts, capacity):
    flat_route = routes.reshape(-1)
    one_hot = (flat_route[:, None] == jnp.arange(n_experts, dtype=jnp.int32)[None, :]).astype(
        jnp.int32
    )
    before = jnp.cumsum(one_hot, axis=0) - one_hot
    rank_in = jnp.sum(before * one_hot, axis=1)
    return flat_route * capacity + rank_in


def dispatch_rows(grad_rows, routes, weights, n_experts, capacity):
    feature_width = grad_rows.shape[1]
    scaled = (grad_rows.astype(jnp.float32)[:, None, :] * weights[:, :, None]).reshape(
        -1, feature_width
    )
    positions = slot_index(routes, n_experts, capacity)
    blank_rows = jnp.zeros((n_experts * capacity, feature_width), jnp.float32)
    return blank_rows.at[positions].set(scaled).astype(jnp.bfloat16)


def place_rows(inputs, routes, n_experts, capacity):
    feature_width = inputs.shape[1]
    chosen = routes.shape[1]
    copies = jnp.broadcast_to(inputs[:, None, :], (inputs.shape[0], chosen, feature_width)).reshape(
        -1, feature_width
    )
    positions = slot_index(routes, n_experts, capacity)
    blank_rows = jnp.zeros((n_experts * capacity, feature_width), inputs.dtype)
    return blank_rows.at[positions].set(copies)


def activations(gate_pre, up_pre, grad_hidden):
    sigmoid_gate = jax.nn.sigmoid(gate_pre)
    activated = gate_pre * sigmoid_gate
    hidden = (activated * up_pre).astype(jnp.bfloat16)
    slope_term = sigmoid_gate * (1.0 + gate_pre * (1.0 - sigmoid_gate))
    d_gate = (grad_hidden * up_pre * slope_term).astype(jnp.bfloat16)
    d_up = (grad_hidden * activated).astype(jnp.bfloat16)
    return (hidden, d_gate, d_up)


def contract_rows(left, right):
    return lax.dot_general(
        left, right, (((0,), (0,)), ((), ())), preferred_element_type=jnp.float32
    )


def contract_cols(left, right):
    return lax.dot_general(
        left, right, (((1,), (1,)), ((), ())), preferred_element_type=jnp.float32
    )


def per_device(token_grads, routing, gate_weights, layer_inputs, w_gate, w_up, w_down):
    n_groups = lax.axis_size("expert")
    n_experts = n_groups // SHARES
    grad_rows = token_grads[0]
    routes = routing[0]
    weights = gate_weights[0]
    inputs = layer_inputs[0]
    gate_cols = w_gate[0]
    up_cols = w_up[0]
    down_cols = w_down[0]
    n_tokens = routes.shape[0]
    chosen = routes.shape[1]
    columns = grad_rows.shape[1]
    capacity = min(n_tokens, 17 * n_tokens * chosen // (16 * n_experts))
    outgoing = dispatch_rows(grad_rows, routes, weights, n_experts, capacity).reshape(
        n_experts, capacity, columns
    )
    outgoing = jnp.repeat(outgoing, SHARES, axis=0)
    placed = place_rows(inputs, routes, n_experts, capacity).reshape(n_experts, capacity, columns)
    placed = jnp.repeat(placed, SHARES, axis=0)
    received, saved = (
        lax.all_to_all(outgoing, "expert", split_axis=0, concat_axis=0, tiled=True),
        lax.all_to_all(placed, "expert", split_axis=0, concat_axis=0, tiled=True),
    )
    received = received.reshape(n_groups * capacity, columns)
    saved = saved.reshape(n_groups * capacity, columns)
    gate_part = jnp.dot(saved, gate_cols, preferred_element_type=jnp.float32)
    up_part = jnp.dot(saved, up_cols, preferred_element_type=jnp.float32)
    down_part = jnp.dot(received, down_cols, preferred_element_type=jnp.float32)
    gate_share, up_share, grad_share = (
        lax.psum_scatter(gate_part, "replica", scatter_dimension=0, tiled=True),
        lax.psum_scatter(up_part, "replica", scatter_dimension=0, tiled=True),
        lax.psum_scatter(down_part, "replica", scatter_dimension=0, tiled=True),
    )
    hidden_share, d_gate_share, d_up_share = activations(gate_share, up_share, grad_share)
    hidden, d_gate, d_up = (
        lax.all_gather(hidden_share, "replica", axis=0, tiled=True),
        lax.all_gather(d_gate_share, "replica", axis=0, tiled=True),
        lax.all_gather(d_up_share, "replica", axis=0, tiled=True),
    )
    back_rows = (contract_cols(d_gate, gate_cols) + contract_cols(d_up, up_cols)).astype(
        jnp.bfloat16
    )
    returned = lax.all_to_all(
        back_rows.reshape(n_groups, capacity, columns),
        "expert",
        split_axis=0,
        concat_axis=0,
        tiled=True,
    )
    merged = jnp.sum(
        returned.reshape(n_experts, SHARES, capacity, columns).astype(jnp.float32), axis=1
    )
    merged = merged.reshape(n_experts * capacity, columns)
    positions = slot_index(routes, n_experts, capacity)
    picked = merged[positions].reshape(n_tokens, chosen, columns)
    boundary = jnp.sum(picked, axis=1).astype(jnp.bfloat16)
    upstream = shifted(boundary[None], "section", -1)
    grad_gate = contract_rows(saved, d_gate).astype(jnp.bfloat16)
    grad_up = contract_rows(saved, d_up).astype(jnp.bfloat16)
    grad_down = contract_rows(received, hidden).astype(jnp.bfloat16)
    return (upstream, grad_gate[None], grad_up[None], grad_down[None])


def solution(mesh):
    placed = (
        P("section", "expert", "replica"),
        P("section", "expert", None),
        P("section", "expert", None),
        P("section", "expert", "replica"),
        P("section", "replica", "expert"),
        P("section", "replica", "expert"),
        P("section", "replica", "expert"),
    )
    return jax.shard_map(
        per_device,
        mesh=mesh,
        in_specs=placed,
        out_specs=(
            P("section", "expert", "replica"),
            P("section", "replica", "expert"),
            P("section", "replica", "expert"),
            P("section", "replica", "expert"),
        ),
        check_vma=False,
    )
```

profile of v0, /device:TPU:0, one launch (start us, length us, event | category | flops | bytes accessed | tf_op | source)
XLA Modules:
  0.0 149.3 jit_solution(3669221726009222780)
XLA Ops:
  7.2 0.0 copy-start
  7.2 0.8 fusion.21
  8.0 0.1 reduce_window_sum.13
  8.1 0.8 select_reduce_fusion
  8.9 0.7 fusion.22
  9.6 1.4 scatter_custom_fusion.1
  11.0 0.1 reshape.93
  11.1 0.0 copy-start.3
  11.1 0.0 copy-start.4
  11.1 1.1 broadcast_in_dim.32
  12.2 7.3 %all-to-all-start.1 = ((bf16[8,34,1792]{2,1,0:T(8,128)(2,1)}), bf16[8,34,1792]{2,1,0:T(8,128)(2,1)S(1)}, u32[]{:S(2)}, u32[]{:S(2)}) async-start(bf16[8,34,1792]{2,1,0:T(8,128)(2,1)} %bitcast.58), calls=%async_computation.2 | async-start | bytes 2293760 | tf_op jit(solution)/shard_map/all_to_all | solution.py:90
  19.5 0.0 copy-done.3
  19.5 0.0 copy-done.4
  19.5 1.1 scatter_custom_fusion
  20.6 0.1 reshape.90
  20.7 26.7 %all-to-all-done.1 = bf16[8,34,1792]{2,1,0:T(8,128)(2,1)S(1)} async-done(((bf16[8,34,1792]{2,1,0:T(8,128)(2,1)}), bf16[8,34,1792]{2,1,0:T(8,128)(2,1)S(1)}, u32[]{:S(2)}, u32[]{:S(2)}) %all-to-all-start.1) | async-done | bytes 974880 | tf_op jit(solution)/shard_map/all_to_all | solution.py:90
  47.4 0.0 copy-start.1
  47.4 1.2 broadcast_in_dim.30
  48.6 0.2 copy-done.1
  48.8 3.6 %all-to-all-start = ((bf16[8,34,1792]{2,1,0:T(8,128)(2,1)}), bf16[8,34,1792]{2,1,0:T(8,128)(2,1)S(1)}, u32[]{:S(2)}, u32[]{:S(2)}) async-start(bf16[8,34,1792]{2,1,0:T(8,128)(2,1)} %bitcast.57), calls=%async_computation | async-start | bytes 2293760 | tf_op jit(solution)/shard_map/all_to_all | solution.py:89
  52.4 0.0 reduce-scatter.6.cloned.1.call-start
  52.5 1.4 reshape.95
  53.9 2.3 %fusion.9 = f32[272,256]{1,0:T(8,128)} fusion(bf16[272,1792]{1,0:T(8,128)(2,1)S(1)} %reshape.95, bf16[1,1792,256]{2,1,0:T(8,128)(2,1)} %param.12), kind=kOutput, calls=%fused_computation.17 | convolution fusion | flops 249561088 | bytes 2170880 | tf_op jit(solution)/shard_map/dot_general | solution.py:95
  56.2 0.0 reduce-scatter.6.cloned.1.call-update
  56.2 0.0 reduce-scatter.8.cloned.1.call-start
  56.2 0.0 copy-done
  56.3 1.1 fusion.6
  57.4 0.0 reduce-scatter.8.cloned.1.call-update
  57.4 0.0 reduce-scatter.4.cloned.1.call-start
  57.5 23.0 %all-to-all-done = bf16[8,34,1792]{2,1,0:T(8,128)(2,1)S(1)} async-done(((bf16[8,34,1792]{2,1,0:T(8,128)(2,1)}), bf16[8,34,1792]{2,1,0:T(8,128)(2,1)S(1)}, u32[]{:S(2)}, u32[]{:S(2)}) %all-to-all-start) | async-done | bytes 974880 | tf_op jit(solution)/shard_map/all_to_all | solution.py:89
  80.5 1.1 reshape.92
  81.6 2.6 %fusion.11 = f32[272,256]{1,0:T(8,128)} fusion(bf16[272,1792]{1,0:T(8,128)(2,1)} %reshape.92, bf16[1,1792,256]{2,1,0:T(8,128)(2,1)} %param.13), kind=kOutput, calls=%fused_computation.19 | convolution fusion | flops 249561088 | bytes 2170880 | tf_op jit(solution)/shard_map/dot_general | solution.py:96
  84.2 0.0 reduce-scatter.4.cloned.1.call-update
  84.2 0.0 reduce-scatter.6.cloned.1.call-done
  84.3 0.0 reduce-scatter.8.cloned.1.call-done
  84.3 6.9 %reduce-scatter.4.cloned.1.call-done = f32[136,256]{1,0:T(8,128)} async-done(((f32[272,256]{1,0:T(8,128)}), f32[136,256]{1,0:T(8,128)}) %reduce-scatter.4.cloned.1.call-update) | async-done | bytes 139280 | tf_op jit(solution)/shard_map/reduce_scatter | solution.py:100
  91.2 1.1 multiply_convert_fusion
  92.3 0.0 copy-start.2
  92.3 2.0 %all_gather.9 = bf16[272,256]{1,0:T(8,128)(2,1)S(1)} all-gather(bf16[136,256]{1,0:T(8,128)(2,1)S(1)} %get-tuple-element.5), channel_id=1, replica_groups=mesh['section'=2,'expert'=8,'replica'=2] {'replica'}, dimensions={0}, use_global_device_ids=true | all-gather | bytes 208896 | tf_op jit(solution)/shard_map/all_gather | solution.py:105
  94.4 0.4 fusion.4
  94.8 1.9 %all_gather.10 = bf16[272,256]{1,0:T(8,128)(2,1)S(1)} all-gather(bf16[136,256]{1,0:T(8,128)(2,1)S(1)} %get-tuple-element.6), channel_id=1, replica_groups=mesh['section'=2,'expert'=8,'replica'=2] {'replica'}, dimensions={0}, use_global_device_ids=true | all-gather | bytes 208896 | tf_op jit(solution)/shard_map/all_gather | solution.py:106
  96.7 0.0 copy-done.2
  96.7 0.5 fusion
  97.2 1.2 reshape.96
  98.4 5.7 %all-to-all-start.2 = ((bf16[8,34,1792]{2,1,0:T(8,128)(2,1)}), bf16[8,34,1792]{2,1,0:T(8,128)(2,1)S(1)}, u32[]{:S(2)}, u32[]{:S(2)}) async-start(bf16[8,34,1792]{2,1,0:T(8,128)(2,1)} %reshape.96), calls=%async_computation.5 | async-start | bytes 2293760 | tf_op jit(solution)/shard_map/all_to_all | solution.py:111
  104.1 1.6 %fusion.1 = bf16[1,1792,256]{2,1,0:T(8,128)(2,1)} fusion(bf16[272,1792]{1,0:T(8,128)(2,1)S(1)} %reshape.95, bf16[272,256]{1,0:T(8,128)(2,1)S(1)} %all_gather.9), kind=kOutput, calls=%fused_computation.8 | convolution fusion | flops 250019840 | bytes 2031616 | tf_op jit(solution)/shard_map/dot_general | solution.py:57
  105.7 1.6 %fusion.2 = bf16[1,1792,256]{2,1,0:T(8,128)(2,1)} fusion(bf16[272,1792]{1,0:T(8,128)(2,1)S(1)} %reshape.95, bf16[272,256]{1,0:T(8,128)(2,1)S(1)} %all_gather.10), kind=kOutput, calls=%fused_computation.9 | convolution fusion | flops 250019840 | bytes 2031616 | tf_op jit(solution)/shard_map/dot_general | solution.py:57
  107.3 25.2 %all-to-all-done.2 = bf16[8,34,1792]{2,1,0:T(8,128)(2,1)S(1)} async-done(((bf16[8,34,1792]{2,1,0:T(8,128)(2,1)}), bf16[8,34,1792]{2,1,0:T(8,128)(2,1)S(1)}, u32[]{:S(2)}, u32[]{:S(2)}) %all-to-all-start.2) | async-done | bytes 974880 | tf_op jit(solution)/shard_map/all_to_all | solution.py:111
  132.5 0.2 convert_reduce_fusion
  132.7 0.1 reshape.97
  132.7 0.7 gather_fusion
  133.5 1.3 collective-permute-start
  134.8 1.9 %all_gather.11 = bf16[272,256]{1,0:T(8,128)(2,1)S(1)} all-gather(bf16[136,256]{1,0:T(8,128)(2,1)S(1)} %get-tuple-element.4), channel_id=1, replica_groups=mesh['section'=2,'expert'=8,'replica'=2] {'replica'}, dimensions={0}, use_global_device_ids=true | all-gather | bytes 208896 | tf_op jit(solution)/shard_map/all_gather | solution.py:104
  136.7 2.8 %fusion.3 = bf16[1,1792,256]{2,1,0:T(8,128)(2,1)} fusion(bf16[272,1792]{1,0:T(8,128)(2,1)} %reshape.92, bf16[272,256]{1,0:T(8,128)(2,1)S(1)} %all_gather.11), kind=kOutput, calls=%fused_computation.10 | convolution fusion | flops 250019840 | bytes 2031616 | tf_op jit(solution)/shard_map/dot_general | solution.py:57
  139.5 2.6 %collective-permute-done = bf16[1,64,1792]{2,1,0:T(8,128)(2,1)S(1)} collective-permute-done((bf16[1,64,1792]{2,1,0:T(8,128)(2,1)S(1)}, bf16[1,64,1792]{2,1,0:T(8,128)(2,1)S(1)}, u32[]{:S(2)}, u32[]{:S(2)}) %collective-permute-start) | collective-permute-done | bytes 229408 | tf_op jit(solution)/shard_map/ppermute | solution.py:12
  142.1 0.7 copy.12
  (2 shorter events, 0.0 us)
Async XLA Ops:
  7.2 49.1 %copy-start = (bf16[1,1792,256]{2,1,0:T(8,128)(2,1)S(1)}, bf16[1,1792,256]{2,1,0:T(8,128)(2,1)}, u32[]{:S(2)}) copy-start(bf16[1,1792,256]{2,1,0:T(8,128)(2,1)} %param.11) | copy-start | bytes 2752516
  11.1 8.4 %copy-start.3 = (bf16[1,64,1792]{2,1,0:T(8,128)(2,1)S(1)}, bf16[1,64,1792]{2,1,0:T(8,128)(2,1)}, u32[]{:S(2)}) copy-start(bf16[1,64,1792]{2,1,0:T(8,128)(2,1)} %param.7) | copy-start | bytes 688132
  11.1 8.4 %copy-start.4 = (f32[1,64,1]{1,2,0:T(1,128)S(1)}, f32[1,64,1]{1,2,0:T(1,128)}, u32[]{:S(2)}) copy-start(f32[1,64,1]{1,2,0:T(1,128)} %param.9) | copy-start | bytes 772
  12.2 35.2 %all-to-all-start.1 = ((bf16[8,34,1792]{2,1,0:T(8,128)(2,1)}), bf16[8,34,1792]{2,1,0:T(8,128)(2,1)S(1)}, u32[]{:S(2)}, u32[]{:S(2)}) async-start(bf16[8,34,1792]{2,1,0:T(8,128)(2,1)} %bitcast.58), calls=%async_computation.2 | async-start | bytes 2293760 | tf_op jit(solution)/shard_map/all_to_all | solution.py:90
  47.4 1.4 copy-start.1
  48.8 31.7 %all-to-all-start = ((bf16[8,34,1792]{2,1,0:T(8,128)(2,1)}), bf16[8,34,1792]{2,1,0:T(8,128)(2,1)S(1)}, u32[]{:S(2)}, u32[]{:S(2)}) async-start(bf16[8,34,1792]{2,1,0:T(8,128)(2,1)} %bitcast.57), calls=%async_computation | async-start | bytes 2293760 | tf_op jit(solution)/shard_map/all_to_all | solution.py:89
  52.4 31.9 %reduce-scatter.6.cloned.1.call-start = ((), (), s32[]{:S(2)}) async-start(), calls=%async_computation.7 | async-start | bytes 417792 | tf_op jit(solution)/shard_map/reduce_scatter | solution.py:99
  56.2 28.1 %reduce-scatter.8.cloned.1.call-start = ((), (), s32[]{:S(2)}) async-start(), calls=%async_computation.8 | async-start | bytes 417792 | tf_op jit(solution)/shard_map/reduce_scatter | solution.py:98
  57.4 33.8 %reduce-scatter.4.cloned.1.call-start = ((), (), s32[]{:S(2)}) async-start(), calls=%async_computation.6 | async-start | bytes 417792 | tf_op jit(solution)/shard_map/reduce_scatter | solution.py:100
  92.3 4.4 %copy-start.2 = (bf16[1,1792,256]{2,1,0:T(8,128)(2,1)S(1)}, bf16[1,1792,256]{2,1,0:T(8,128)(2,1)}, u32[]{:S(2)}) copy-start(bf16[1,1792,256]{2,1,0:T(8,128)(2,1)} %param.12) | copy-start | bytes 2752516
  98.4 34.1 %all-to-all-start.2 = ((bf16[8,34,1792]{2,1,0:T(8,128)(2,1)}), bf16[8,34,1792]{2,1,0:T(8,128)(2,1)S(1)}, u32[]{:S(2)}, u32[]{:S(2)}) async-start(bf16[8,34,1792]{2,1,0:T(8,128)(2,1)} %reshape.96), calls=%async_computation.5 | async-start | bytes 2293760 | tf_op jit(solution)/shard_map/all_to_all | solution.py:111
  133.5 8.6 %collective-permute-start = (bf16[1,64,1792]{2,1,0:T(8,128)(2,1)S(1)}, bf16[1,64,1792]{2,1,0:T(8,128)(2,1)S(1)}, u32[]{:S(2)}, u32[]{:S(2)}) collective-permute-start(bf16[1,64,1792]{2,1,0:T(8,128)(2,1)S(1)} %bitcast.59), channel_id=1, source_target_pairs={{16,0},{17,1},{18,2},{19,3},{20,4},{21,5},{22,6},{23,7},{24,8},{25... | collective-permute-start | bytes 688136 | tf_op jit(solution)/shard_map/ppermute | solution.py:12
Sparse Core Ops, SparseCore 0:
  56.3 9.1 reduce-scatter.5
  68.3 8.8 reduce-scatter.7
  84.4 6.7 reduce-scatter.3
where the time goes:
time: 150 us; the launch traced here: 149 us
  waiting for transfers between devices  84.4 us (56%)
  starting transfers between devices  18.1 us (12%)
  between operations  13.9 us (9%)
  matrix products  13 us (9%)
  local copies, waits for them, and re-layouts  9.24 us (6%)
  blocking collectives  5.85 us (4%)
  other arithmetic  4.82 us (3%)
    all_to_all x1, waiting for transfers between devices, per_device(): lax.all_to_all(placed, 'expert', split_axis=0, concat_axis=0, tiled=True)  26.7 us
    all_to_all x1, waiting for transfers between devices, per_device(): lax.all_to_all(back_rows.reshape(n_groups, capacity, columns), 'expert',...  25.2 us
    all_to_all x1, waiting for transfers between devices, per_device(): lax.all_to_all(outgoing, 'expert', split_axis=0, concat_axis=0, tiled=True)  23 us
    all_to_all x1, starting transfers between devices, per_device(): lax.all_to_all(placed, 'expert', split_axis=0, concat_axis=0, tiled=True)  7.31 us
    reduce_scatter x1, waiting for transfers between devices, per_device(): lax.psum_scatter(down_part, 'replica', scatter_dimension=0, tiled=True)  6.9 us
    dot_general x3, matrix products, contract_rows(): lax.dot_general(left, right, (((0,), (0,)), ((), ())), preferred_element_...  5.99 us
    all_to_all x1, starting transfers between devices, per_device(): lax.all_to_all(back_rows.reshape(n_groups, capacity, columns), 'expert',...  5.74 us
    all_to_all x1, starting transfers between devices, per_device(): lax.all_to_all(outgoing, 'expert', split_axis=0, concat_axis=0, tiled=True)  3.64 us
  transfers between devices with their start and end apart: 7, of which 5 were waited for; matrix products, arithmetic and copies ran while one was open for 11% of the time, Pallas kernels for 0%

commit v1 on v0

v1 whole, which is shorter than its diff:
```python
import functools

import jax
import jax.numpy as jnp
from jax import lax
from jax.experimental import pallas as pl
from jax.experimental.pallas import tpu as pltpu
from jax.sharding import PartitionSpec as P

SHARES = 4
F32 = jnp.float32
BF16 = jnp.bfloat16
VMEM_BYTES = 16 * 1024 * 1024


def round_up(value, multiple):
    return -(-value // multiple) * multiple


def call(body, out_shape, flops, n_bytes, scratch=()):
    return functools.partial(
        pl.pallas_call,
        out_shape=out_shape,
        scratch_shapes=list(scratch),
        compiler_params=pltpu.CompilerParams(vmem_limit_bytes=VMEM_BYTES),
        cost_estimate=pl.CostEstimate(flops=flops, bytes_accessed=n_bytes, transcendentals=0),
    )(body)


def dot(left, right, left_dim=1, right_dim=0):
    return lax.dot_general(
        left, right, (((left_dim,), (right_dim,)), ((), ())), preferred_element_type=F32
    )


def slots(routes, n_experts):
    chosen, n_tokens = routes.shape
    shift = lax.axis_index("expert") // SHARES
    relative = routes - shift
    relative = jnp.where(relative < 0, relative + n_experts, relative)
    experts = lax.broadcasted_iota(jnp.int32, (round_up(n_experts, 8), n_tokens), 0)
    named = [relative[k : k + 1] == experts for k in range(chosen)]
    count = sum(one.astype(F32) for one in named)
    earlier = (
        lax.broadcasted_iota(jnp.int32, (n_tokens, n_tokens), 0)
        < lax.broadcasted_iota(jnp.int32, (n_tokens, n_tokens), 1)
    ).astype(BF16)
    before = dot(count.astype(BF16), earlier)
    slot_rows = []
    for k in range(chosen):
        rank = jnp.sum(jnp.where(named[k], before, 0.0), axis=0, keepdims=True).astype(jnp.int32)
        for other in range(k):
            rank = rank + (relative[other : other + 1] == relative[k : k + 1]).astype(jnp.int32)
        slot_rows.append(rank)
    return relative, slot_rows


def dispatch_block(routes, weights, grad_rows, inputs, which, n_experts, capacity, split):
    chosen, n_tokens = routes.shape
    columns = inputs.shape[1]
    rows = round_up(2 * capacity, 8)

    def body(routes_ref, weights_ref, grads_ref, inputs_ref, lo_ref, hi_ref):
        relative, slot_rows = slots(routes_ref[...], n_experts)
        row = lax.broadcasted_iota(jnp.int32, (rows, n_tokens), 0)
        pick_input = jnp.zeros((rows, n_tokens), F32)
        pick_grad = jnp.zeros((rows, n_tokens), F32)
        scale = jnp.zeros((rows, n_tokens), F32)
        for k in range(chosen):
            target = jnp.where(relative[k : k + 1] == which, slot_rows[k], -2 * rows)
            pick_input = pick_input + (row == target).astype(F32)
            hit = (row == target + capacity).astype(F32)
            pick_grad = pick_grad + hit
            scale = scale + hit * weights_ref[k : k + 1, :]
        scale = jnp.sum(scale, axis=1, keepdims=True)
        pick_input = pick_input.astype(BF16)
        pick_grad = pick_grad.astype(BF16)
        for out_ref, begin, end in ((lo_ref, 0, split), (hi_ref, split, columns)):
            block = dot(pick_input, inputs_ref[:, begin:end])
            block = block + dot(pick_grad, grads_ref[:, begin:end]) * scale
            out_ref[...] = block.astype(BF16)

    return call(
        body,
        (
            jax.ShapeDtypeStruct((rows, split), BF16),
            jax.ShapeDtypeStruct((rows, columns - split), BF16),
        ),
        2 * 2 * rows * n_tokens * columns,
        2 * n_tokens * columns * 2 + rows * columns * 2,
    )(routes, weights, grad_rows, inputs)


def partial_products(blocks, gate_cols, up_cols, down_cols, capacity, split):
    rows = round_up(2 * capacity, 8)
    kept = round_up(capacity, 8)
    n_blocks = len(blocks)
    columns, width = gate_cols.shape

    def body(*refs):
        block_refs = refs[: 2 * n_blocks]
        gate_ref, up_ref, down_ref, out_ref, packed_ref = refs[2 * n_blocks :]
        for i in range(n_blocks):
            packed_ref[i * rows : (i + 1) * rows, :split] = block_refs[2 * i][...]
            packed_ref[i * rows : (i + 1) * rows, split:] = block_refs[2 * i + 1][...]
        packed = packed_ref[...]
        gate = dot(packed, gate_ref[...])
        up = dot(packed, up_ref[...])
        down = dot(packed, down_ref[...])
        for i in range(n_blocks):
            at = i * rows
            out_ref[i, :, :width] = gate[at : at + kept]
            out_ref[i, :, width : 2 * width] = up[at : at + kept]
            out_ref[i, :capacity, 2 * width :] = down[at + capacity : at + 2 * capacity]
            if kept > capacity:
                out_ref[i, capacity:, 2 * width :] = jnp.zeros((kept - capacity, width), F32)

    return call(
        body,
        (
            jax.ShapeDtypeStruct((n_blocks, kept, 3 * width), F32),
            jax.ShapeDtypeStruct((n_blocks * rows, columns), BF16),
        ),
        2 * 3 * n_blocks * rows * columns * width,
        3 * columns * width * 2 + n_blocks * rows * columns * 4,
    )(*[half for block in blocks for half in block], gate_cols, up_cols, down_cols)


def hidden_backward(partials, gate_cols, up_cols, capacity):
    n_blocks, kept, width3 = partials[0].shape
    columns, width = gate_cols.shape
    rows = round_up(2 * capacity, 8)
    n_parts = len(partials)

    def body(*refs):
        part_refs = refs[:n_parts]
        gate_ref, up_ref = refs[n_parts : n_parts + 2]
        back_refs = refs[n_parts + 2 : n_parts + 2 + n_blocks]
        slope_ref = refs[n_parts + 2 + n_blocks]
        valid = lax.broadcasted_iota(jnp.int32, (kept, width), 0) < capacity
        d_gates, d_ups = [], []
        slope_ref[...] = jnp.zeros(slope_ref.shape, BF16)
        for i in range(n_blocks):
            total = part_refs[0][i]
            for ref in part_refs[1:]:
                total = total + ref[i]
            gate = jnp.where(valid, total[:, :width], 0.0)
            up = jnp.where(valid, total[:, width : 2 * width], 0.0)
            grad_hidden = total[:, 2 * width :]
            sigmoid_gate = jax.nn.sigmoid(gate)
            activated = gate * sigmoid_gate
            hidden = (activated * up).astype(BF16)
            slope_term = sigmoid_gate * (1.0 + gate * (1.0 - sigmoid_gate))
            d_gate = (grad_hidden * up * slope_term).astype(BF16)
            d_up = (grad_hidden * activated).astype(BF16)
            at = i * rows
            slope_ref[at : at + capacity, :width] = d_gate[:capacity]
            slope_ref[at : at + capacity, width : 2 * width] = d_up[:capacity]
            slope_ref[at + capacity : at + 2 * capacity, 2 * width :] = hidden[:capacity]
            d_gates.append(d_gate)
            d_ups.append(d_up)
        back = dot(jnp.concatenate(d_gates, axis=0), gate_ref[...], 1, 1)
        back = back + dot(jnp.concatenate(d_ups, axis=0), up_ref[...], 1, 1)
        for i in range(n_blocks):
            back_refs[i][...] = back[i * kept : (i + 1) * kept].astype(BF16)

    outs = call(
        body,
        tuple(jax.ShapeDtypeStruct((kept, columns), BF16) for _ in range(n_blocks))
        + (jax.ShapeDtypeStruct((n_blocks * rows, width3), BF16),),
        2 * 2 * n_blocks * kept * columns * width,
        2 * columns * width * 2 + n_blocks * kept * columns * 2,
    )(*partials, gate_cols, up_cols)
    return outs[:n_blocks], outs[n_blocks]


def weight_grads(packed, slopes, width):
    columns = packed[0].shape[1]
    n_parts = len(packed)
    n_rows = sum(one.shape[0] for one in packed)

    def body(*refs):
        packed_refs = refs[:n_parts]
        slope_refs = refs[n_parts : 2 * n_parts]
        out_refs = refs[2 * n_parts :]
        total = dot(packed_refs[0][...], slope_refs[0][...], 0, 0)
        for left, right in zip(packed_refs[1:], slope_refs[1:]):
            total = total + dot(left[...], right[...], 0, 0)
        for i in range(3):
            out_refs[i][...] = total[:, i * width : (i + 1) * width].astype(BF16)

    return call(
        body,
        tuple(jax.ShapeDtypeStruct((columns, width), BF16) for _ in range(3)),
        2 * 3 * n_rows * columns * width,
        3 * columns * width * 2 + n_rows * columns * 2,
    )(*packed, *slopes)


def combine(routes, merged, n_experts, capacity):
    chosen, n_tokens = routes.shape
    kept, columns = merged[0].shape

    def body(routes_ref, *refs):
        merged_refs, out_ref = refs[:-1], refs[-1]
        relative, slot_rows = slots(routes_ref[...], n_experts)
        row = lax.broadcasted_iota(jnp.int32, (kept, n_tokens), 0)
        total = None
        for which, ref in enumerate(merged_refs):
            pick = jnp.zeros((kept, n_tokens), F32)
            for k in range(chosen):
                target = jnp.where(relative[k : k + 1] == which, slot_rows[k], -1)
                pick = pick + (row == target).astype(F32)
            term = dot(pick.astype(BF16), ref[...], 0, 0)
            total = term if total is None else total + term
        out_ref[...] = total.astype(BF16)

    return call(
        body,
        jax.ShapeDtypeStruct((n_tokens, columns), BF16),
        2 * n_tokens * columns * kept * len(merged),
        kept * columns * 2 * len(merged) + n_tokens * columns * 2,
    )(routes, *merged)


def per_device(token_grads, routing, gate_weights, layer_inputs, w_gate, w_up, w_down):
    n_groups = lax.axis_size("expert")
    n_sections = lax.axis_size("section")
    n_replicas = lax.axis_size("replica")
    n_experts = n_groups // SHARES
    grad_rows, inputs = token_grads[0], layer_inputs[0]
    routes, weights = routing[0].T, gate_weights[0].T
    gate_cols, up_cols, down_cols = w_gate[0], w_up[0], w_down[0]
    chosen, n_tokens = routes.shape
    columns = inputs.shape[1]
    width = gate_cols.shape[1]
    capacity = min(n_tokens, 17 * n_tokens * chosen // (16 * n_experts))
    split = round_up(columns // 2, 128)

    def partner(value, step):
        return lax.ppermute(value, "expert", [(j, j ^ step) for j in range(n_groups)])

    def partner_back(value, step):
        pairs = [
            (s * n_groups + j, s * n_groups + (j ^ step))
            for s in range(1, n_sections)
            for j in range(n_groups)
        ]
        return lax.ppermute(value, ("section", "expert"), pairs)

    def dispatch(which):
        return dispatch_block(
            routes, weights, grad_rows, inputs, which, n_experts, capacity, split
        )

    def crossing(value, which):
        move = SHARES * which
        return lax.ppermute(
            value, "expert", [(j, (j + move) % n_groups) for j in range(n_groups)]
        )

    routes_next = lax.ppermute(
        routes, "section", [(s, s - 1) for s in range(1, n_sections)]
    )

    heads = [None] * n_experts
    for which in list(range(1, n_experts)) + [0]:
        lo, hi = dispatch(which)
        heads[which] = (crossing(lo, which), crossing(hi, which)) if which else (lo, hi)

    packed, slopes, merged = [], [], []
    for which in range(n_experts):
        lo, hi = heads[which]
        lo_y, hi_y = partner(lo, 1), partner(hi, 1)
        lo_z, hi_z = partner(lo, 2), partner(hi, 2)
        if which == 0:
            lo_d, hi_d = partner(lo_z, 1), partner(hi_z, 1)
        else:
            lo_d, hi_d = partner(lo_z, 1), partner(hi_y, 2)
        blocks = ((lo, hi), (lo_y, hi_y), (lo_z, hi_z), (lo_d, hi_d))
        part, rows_packed = partial_products(
            blocks, gate_cols, up_cols, down_cols, capacity, split
        )
        parts = [part]
        for turn in range(1, n_replicas):
            parts.append(
                lax.ppermute(
                    part, "replica", [(r, (r + turn) % n_replicas) for r in range(n_replicas)]
                )
            )
        backs, slope = hidden_backward(parts, gate_cols, up_cols, capacity)
        packed.append(rows_packed)
        slopes.append(slope)
        total = backs[0].astype(F32)
        for step in range(1, SHARES):
            total = total + partner_back(backs[step], step).astype(F32)
        move = SHARES * which
        home = [
            (s * n_groups + j, (s - 1) * n_groups + (j - move) % n_groups)
            for s in range(1, n_sections)
            for j in range(n_groups)
        ]
        merged.append(lax.ppermute(total.astype(BF16), ("section", "expert"), home))

    upstream = combine(routes_next, merged, n_experts, capacity)
    grad_gate, grad_up, grad_down = weight_grads(packed, slopes, width)
    return (upstream[None], grad_gate[None], grad_up[None], grad_down[None])


def solution(mesh):
    placed = (
        P("section", "expert", "replica"),
        P("section", "expert", None),
        P("section", "expert", None),
        P("section", "expert", "replica"),
        P("section", "replica", "expert"),
        P("section", "replica", "expert"),
        P("section", "replica", "expert"),
    )
    return jax.shard_map(
        per_device,
        mesh=mesh,
        in_specs=placed,
        out_specs=(
            P("section", "expert", "replica"),
            P("section", "replica", "expert"),
            P("section", "replica", "expert"),
            P("section", "replica", "expert"),
        ),
        check_vma=False,
    )
```

time: 150 us -> 76.4 us (0.51)
  waiting for transfers between devices: 84.4 us -> 32.5 us
  between operations: 13.9 us -> 0.89 us
  matrix products: 13 us -> 0 us
  Pallas kernels: 0 us -> 9.81 us
  starting transfers between devices: 18.1 us -> 26.9 us
  blocking collectives: 5.85 us -> 0 us
  other arithmetic: 4.82 us -> 0.16 us
  local copies, waits for them, and re-layouts: 9.24 us -> 5.63 us
    all_to_all x3 -> x0, waiting for transfers between devices: 74.8 us -> none  [the longest x1 26.7 us: per_device(): lax.all_to_all(placed, 'expert', split_axis=0, concat_axis=0, tiled=True)]
    ppermute x1 -> x25, waiting for transfers between devices: 2.59 us -> 32.5 us  [the longest x2 21.8 us: per_device(): merged.append(lax.ppermute(total.astype(BF16), ('section', 'expert'), home))]
    ppermute x1 -> x25, starting transfers between devices: 1.29 us -> 26.9 us  [the longest x12 14.7 us: partner(): lax.ppermute(value, 'expert', [(j, j ^ step) for j in range(n_groups)])]
    all_to_all x3 -> x0, starting transfers between devices: 16.7 us -> none  [the longest x1 7.31 us: per_device(): lax.all_to_all(placed, 'expert', split_axis=0, concat_axis=0, tiled=True)]
    dot_general x8 -> x0, matrix products: 13 us -> none  [the longest x3 5.99 us: contract_rows(): lax.dot_general(left, right, (((0,), (0,)), ((), ())), preferred_element_...]
    pallas_call x0 -> x8, Pallas kernels: none -> 9.81 us  [the longest x1 4.28 us: weight_grads(): call(body, tuple((jax.ShapeDtypeStruct((columns, width), BF16) for _ in r...]
    reduce_scatter x3 -> x0, waiting for transfers between devices: 6.94 us -> none  [the longest x1 6.9 us: per_device(): lax.psum_scatter(down_part, 'replica', scatter_dimension=0, tiled=True)]
    all_gather x3 -> x0, blocking collectives: 5.85 us -> none  [the longest x1 2.04 us: per_device(): lax.all_gather(d_gate_share, 'replica', axis=0, tiled=True)]
  transfers between devices with their start and end apart: 7 -> 25, of which waited for: 5 -> 9; matrix products, arithmetic and copies ran while one was open for 11% -> 0% of each run, Pallas kernels for 0% -> 11%
where the time goes in v1:
time: 76.4 us; the launch traced here: 75.9 us
  waiting for transfers between devices  32.5 us (43%)
  starting transfers between devices  26.9 us (35%)
  Pallas kernels  9.81 us (13%)
  local copies, waits for them, and re-layouts  5.63 us (7%)
  between operations  0.89 us (1%)
    ppermute x2, waiting for transfers between devices, per_device(): merged.append(lax.ppermute(total.astype(BF16), ('section', 'expert'), home))  21.8 us
    ppermute x12, starting transfers between devices, partner(): lax.ppermute(value, 'expert', [(j, j ^ step) for j in range(n_groups)])  14.7 us
    unnamed x20, local copies, waits for them, and re-layouts  5.63 us
    ppermute x2, waiting for transfers between devices, crossing(): lax.ppermute(value, 'expert', [(j, (j + move) % n_groups) for j in range(...  5.61 us
    ppermute x12, waiting for transfers between devices, partner(): lax.ppermute(value, 'expert', [(j, j ^ step) for j in range(n_groups)])  4.44 us
    pallas_call x1, Pallas kernels, weight_grads(): call(body, tuple((jax.ShapeDtypeStruct((columns, width), BF16) for _ in r...  4.28 us
    ppermute x2, starting transfers between devices, crossing(): lax.ppermute(value, 'expert', [(j, (j + move) % n_groups) for j in range(...  4.21 us
    ppermute x6, starting transfers between devices, partner_back(): return lax.ppermute(value, ('section', 'expert'), pairs)  4.02 us
  transfers between devices with their start and end apart: 25, of which 9 were waited for; matrix products, arithmetic and copies ran while one was open for 0% of the time, Pallas kernels for 11%

profile of v1, /device:TPU:0, one launch (start us, length us, event | category | flops | bytes accessed | tf_op | source)
XLA Modules:
  0.0 75.9 jit_solution(1909796891911370759)
XLA Ops:
  0.7 1.0 %copy-done.5 = bf16[1,64,1792]{2,1,0:T(8,128)(2,1)S(1)} copy-done((bf16[1,64,1792]{2,1,0:T(8,128)(2,1)S(1)}, bf16[1,64,1792]{2,1,0:T(8,128)(2,1)}, u32[]{:S(2)}) %copy-start.5) | copy-done | bytes 229400
  1.7 0.9 %copy-done.6 = bf16[1,64,1792]{2,1,0:T(8,128)(2,1)S(1)} copy-done((bf16[1,64,1792]{2,1,0:T(8,128)(2,1)S(1)}, bf16[1,64,1792]{2,1,0:T(8,128)(2,1)}, u32[]{:S(2)}) %copy-start.6) | copy-done | bytes 229400
  2.6 0.7 copy-done.7
  3.3 0.7 copy-done.8
  3.9 0.4 shard_map.105
  4.4 4.1 %collective-permute-start.12 = (bf16[72,896]{1,0:T(8,128)(2,1)S(1)}, bf16[72,896]{1,0:T(8,128)(2,1)S(1)}, u32[]{:S(2)}, u32[]{:S(2)}) collective-permute-start(bf16[72,896]{1,0:T(8,128)(2,1)S(1)} %get-tuple-element.32), channel_id=1, source_target_pairs={{0,8},{2,10},{4,12},{6,14},{8,0},{10,2},{12,4},{14,6},{1,9},{3,11}... | collective-permute-start | bytes 387080 | tf_op jit(solution)/shard_map/ppermute | solution.py:258
  8.5 0.1 collective-permute-start.13
  8.6 0.4 shard_map.102
  9.0 1.9 %collective-permute-start.3 = (bf16[72,896]{1,0:T(8,128)(2,1)S(1)}, bf16[72,896]{1,0:T(8,128)(2,1)S(1)}, u32[]{:S(2)}, u32[]{:S(2)}) collective-permute-start(bf16[72,896]{1,0:T(8,128)(2,1)S(1)} %get-tuple-element.25.refs_0_), channel_id=1, source_target_pairs={{0,4},{2,6},{4,0},{6,2},{8,12},{10,14},{12,8},{14,10},{1,5},{3,7},... | collective-permute-start | bytes 387080 | tf_op jit(solution)/shard_map/ppermute | solution.py:241
  10.9 1.5 %collective-permute-start.1 = (bf16[72,896]{1,0:T(8,128)(2,1)S(1)}, bf16[72,896]{1,0:T(8,128)(2,1)S(1)}, u32[]{:S(2)}, u32[]{:S(2)}) collective-permute-start(bf16[72,896]{1,0:T(8,128)(2,1)S(1)} %get-tuple-element.25.refs_0_), channel_id=1, source_target_pairs={{0,2},{2,0},{4,6},{6,4},{8,10},{10,8},{12,14},{14,12},{1,3},{3,1},... | collective-permute-start | bytes 387080 | tf_op jit(solution)/shard_map/ppermute | solution.py:241
  12.4 0.5 collective-permute-start.4
  12.9 5.5 %collective-permute-done.12.refs_0_ = bf16[72,896]{1,0:T(8,128)(2,1)S(1)} collective-permute-done((bf16[72,896]{1,0:T(8,128)(2,1)S(1)}, bf16[72,896]{1,0:T(8,128)(2,1)S(1)}, u32[]{:S(2)}, u32[]{:S(2)}) %collective-permute-start.12) | collective-permute-done | bytes 129056 | tf_op jit(solution)/shard_map/ppermute | solution.py:258
  18.4 1.8 %collective-permute-start.2 = (bf16[72,896]{1,0:T(8,128)(2,1)S(1)}, bf16[72,896]{1,0:T(8,128)(2,1)S(1)}, u32[]{:S(2)}, u32[]{:S(2)}) collective-permute-start(bf16[72,896]{1,0:T(8,128)(2,1)S(1)} %get-tuple-element.26.refs_1_), channel_id=1, source_target_pairs={{0,2},{2,0},{4,6},{6,4},{8,10},{10,8},{12,14},{14,12},{1,3},{3,1},... | collective-permute-start | bytes 387080 | tf_op jit(solution)/shard_map/ppermute | solution.py:241
  20.3 0.1 collective-permute-done.13.refs_1_
  20.3 0.7 collective-permute-start.16
  21.0 0.0 collective-permute-done.3.refs_4_
  21.0 1.5 %collective-permute-start.15 = (bf16[72,896]{1,0:T(8,128)(2,1)S(1)}, bf16[72,896]{1,0:T(8,128)(2,1)S(1)}, u32[]{:S(2)}, u32[]{:S(2)}) collective-permute-start(bf16[72,896]{1,0:T(8,128)(2,1)S(1)} %collective-permute-done.13.refs_1_), channel_id=1, source_target_pairs={{0,2},{2,0},{4,6},{6,4},{8,10},{10,8},{12,14},{14,12},{1,3},{3,1},... | collective-permute-start | bytes 387080 | tf_op jit(solution)/shard_map/ppermute | solution.py:241
  22.5 0.0 collective-permute-done.1.refs_2_
  22.5 0.5 collective-permute-start.5
  23.0 0.0 collective-permute-done.4.refs_5_
  23.0 1.5 %collective-permute-start.6 = (bf16[72,896]{1,0:T(8,128)(2,1)S(1)}, bf16[72,896]{1,0:T(8,128)(2,1)S(1)}, u32[]{:S(2)}, u32[]{:S(2)}) collective-permute-start(bf16[72,896]{1,0:T(8,128)(2,1)S(1)} %collective-permute-done.4.refs_5_), channel_id=1, source_target_pairs={{0,2},{2,0},{4,6},{6,4},{8,10},{10,8},{12,14},{14,12},{1,3},{3,1},... | collective-permute-start | bytes 387080 | tf_op jit(solution)/shard_map/ppermute | solution.py:241
  24.6 0.0 collective-permute-done.2.refs_3_
  24.6 1.0 %collective-permute-start.14 = (bf16[72,896]{1,0:T(8,128)(2,1)S(1)}, bf16[72,896]{1,0:T(8,128)(2,1)S(1)}, u32[]{:S(2)}, u32[]{:S(2)}) collective-permute-start(bf16[72,896]{1,0:T(8,128)(2,1)S(1)} %collective-permute-done.12.refs_0_), channel_id=1, source_target_pairs={{0,2},{2,0},{4,6},{6,4},{8,10},{10,8},{12,14},{14,12},{1,3},{3,1},... | collective-permute-start | bytes 387080 | tf_op jit(solution)/shard_map/ppermute | solution.py:241
  25.5 0.0 collective-permute-done.16.refs_4_
  25.5 0.9 %collective-permute-start.17 = (bf16[72,896]{1,0:T(8,128)(2,1)S(1)}, bf16[72,896]{1,0:T(8,128)(2,1)S(1)}, u32[]{:S(2)}, u32[]{:S(2)}) collective-permute-start(bf16[72,896]{1,0:T(8,128)(2,1)S(1)} %collective-permute-done.13.refs_1_), channel_id=1, source_target_pairs={{0,4},{2,6},{4,0},{6,2},{8,12},{10,14},{12,8},{14,10},{1,5},{3,7},... | collective-permute-start | bytes 387080 | tf_op jit(solution)/shard_map/ppermute | solution.py:241
  26.4 0.9 %collective-permute-done.15.refs_3_ = bf16[72,896]{1,0:T(8,128)(2,1)S(1)} collective-permute-done((bf16[72,896]{1,0:T(8,128)(2,1)S(1)}, bf16[72,896]{1,0:T(8,128)(2,1)S(1)}, u32[]{:S(2)}, u32[]{:S(2)}) %collective-permute-start.15) | collective-permute-done | bytes 129056 | tf_op jit(solution)/shard_map/ppermute | solution.py:241
  27.3 1.5 %collective-permute-start.18 = (bf16[72,896]{1,0:T(8,128)(2,1)S(1)}, bf16[72,896]{1,0:T(8,128)(2,1)S(1)}, u32[]{:S(2)}, u32[]{:S(2)}) collective-permute-start(bf16[72,896]{1,0:T(8,128)(2,1)S(1)} %collective-permute-done.16.refs_4_), channel_id=1, source_target_pairs={{0,2},{2,0},{4,6},{6,4},{8,10},{10,8},{12,14},{14,12},{1,3},{3,1},... | collective-permute-start | bytes 387080 | tf_op jit(solution)/shard_map/ppermute | solution.py:241
  28.9 1.2 %collective-permute-done.5.refs_6_ = bf16[72,896]{1,0:T(8,128)(2,1)S(1)} collective-permute-done((bf16[72,896]{1,0:T(8,128)(2,1)S(1)}, bf16[72,896]{1,0:T(8,128)(2,1)S(1)}, u32[]{:S(2)}, u32[]{:S(2)}) %collective-permute-start.5) | collective-permute-done | bytes 129056 | tf_op jit(solution)/shard_map/ppermute | solution.py:241
  30.1 1.4 %collective-permute-start.19 = (bf16[72,896]{1,0:T(8,128)(2,1)S(1)}, bf16[72,896]{1,0:T(8,128)(2,1)S(1)}, u32[]{:S(2)}, u32[]{:S(2)}) collective-permute-start(bf16[72,896]{1,0:T(8,128)(2,1)S(1)} %collective-permute-done.15.refs_3_), channel_id=1, source_target_pairs={{0,4},{2,6},{4,0},{6,2},{8,12},{10,14},{12,8},{14,10},{1,5},{3,7},... | collective-permute-start | bytes 387080 | tf_op jit(solution)/shard_map/ppermute | solution.py:241
  31.5 1.4 %collective-permute-done.6.refs_7_ = bf16[72,896]{1,0:T(8,128)(2,1)S(1)} collective-permute-done((bf16[72,896]{1,0:T(8,128)(2,1)S(1)}, bf16[72,896]{1,0:T(8,128)(2,1)S(1)}, u32[]{:S(2)}, u32[]{:S(2)}) %collective-permute-start.6) | collective-permute-done | bytes 129056 | tf_op jit(solution)/shard_map/ppermute | solution.py:241
  32.9 1.2 %copy-done.1 = bf16[1,1792,256]{2,1,0:T(8,128)(2,1)S(1)} copy-done((bf16[1,1792,256]{2,1,0:T(8,128)(2,1)S(1)}, bf16[1,1792,256]{2,1,0:T(8,128)(2,1)}, u32[]{:S(2)}) %copy-start.1) | copy-done | bytes 917528
  34.0 1.2 %copy-done.3 = bf16[1,1792,256]{2,1,0:T(8,128)(2,1)S(1)} copy-done((bf16[1,1792,256]{2,1,0:T(8,128)(2,1)S(1)}, bf16[1,1792,256]{2,1,0:T(8,128)(2,1)}, u32[]{:S(2)}) %copy-start.3) | copy-done | bytes 917528
  35.2 1.0 %shard_map.103 = (f32[4,40,768]{2,1,0:T(8,128)S(1)}, bf16[288,1792]{1,0:T(8,128)(2,1)S(1)}) custom-call(bf16[72,896]{1,0:T(8,128)(2,1)S(1)} %get-tuple-element.25.refs_0_, bf16[72,896]{1,0:T(8,128)(2,1)S(1)} %get-tuple-element.26.refs_1_, bf16[72,896]{1,0:T(8,128)(2,1)S(1)} %collective-permute-done.1.refs_2_, ...), custom_call_target="tpu_custom_call" | custom-call | flops 792723456 | bytes 4816896 | tf_op jit(solution)/shard_map/pallas_call | solution.py:118
  36.2 0.1 collective-permute-start.7
  36.3 0.0 collective-permute-done.14.refs_2_
  36.3 0.0 collective-permute-done.17.refs_5_
  36.3 0.9 %collective-permute-done.18.refs_6_ = bf16[72,896]{1,0:T(8,128)(2,1)S(1)} collective-permute-done((bf16[72,896]{1,0:T(8,128)(2,1)S(1)}, bf16[72,896]{1,0:T(8,128)(2,1)S(1)}, u32[]{:S(2)}, u32[]{:S(2)}) %collective-permute-start.18) | collective-permute-done | bytes 129056 | tf_op jit(solution)/shard_map/ppermute | solution.py:241
  37.2 0.0 collective-permute-done.19.refs_7_
  37.2 1.0 %shard_map.106 = (f32[4,40,768]{2,1,0:T(8,128)S(1)}, bf16[288,1792]{1,0:T(8,128)(2,1)S(1)}) custom-call(bf16[72,896]{1,0:T(8,128)(2,1)S(1)} %collective-permute-done.12.refs_0_, bf16[72,896]{1,0:T(8,128)(2,1)S(1)} %collective-permute-done.13.refs_1_, bf16[72,896]{1,0:T(8,128)(2,1)S(1)} %collective-permute-done.14.refs_2_, ...), custom_call_target="tpu_custom_call" | custom-call | flops 792723456 | bytes 4816896 | tf_op jit(solution)/shard_map/pallas_call | solution.py:118
  38.2 0.1 collective-permute-start.20
  38.3 0.0 collective-permute-done.7.refs_1_
  38.3 0.8 %shard_map.104 = (bf16[40,1792]{1,0:T(8,128)(2,1)S(1)}, bf16[40,1792]{1,0:T(8,128)(2,1)S(1)}, bf16[40,1792]{1,0:T(8,128)(2,1)S(1)}, bf16[40,1792]{1,0:T(8,128)(2,1)S(1)}, bf16[288,768]{1,0:T(8,128)(2,1)S(1)}) custom-call(f32[4,40,768]{2,1,0:T(8,128)S(1)} %get-tuple-element.27.refs_0_, f32[4,40,768]{2,1,0:T(8,128)S(1)} %collective-permute-done.7.refs_1_, ...), custom_call_target="tpu_custom_call" | custom-call | flops 293601280 | bytes 2408448 | tf_op jit(solution)/shard_map/pallas_call | solution.py:167
  39.1 0.7 collective-permute-start.8
  39.7 0.0 copy-start.9
  39.7 0.7 collective-permute-start.9
  40.4 0.7 collective-permute-start.10
  41.1 1.3 %collective-permute-start = (s32[1,64]{1,0:T(1,128)S(1)}, s32[1,64]{1,0:T(1,128)S(1)}, u32[]{:S(2)}, u32[]{:S(2)}) collective-permute-start(s32[1,64]{1,0:T(1,128)S(1)} %bitcast.29), channel_id=1, source_target_pairs={{16,0},{17,1},{18,2},{19,3},{20,4},{21,5},{22,6},{23,7},{24,8},{25... | collective-permute-start | bytes 776 | tf_op jit(solution)/shard_map/ppermute | solution.py:262
  42.4 0.0 collective-permute-done.20.refs_1_
  42.4 0.8 %shard_map.107 = (bf16[40,1792]{1,0:T(8,128)(2,1)S(1)}, bf16[40,1792]{1,0:T(8,128)(2,1)S(1)}, bf16[40,1792]{1,0:T(8,128)(2,1)S(1)}, bf16[40,1792]{1,0:T(8,128)(2,1)S(1)}, bf16[288,768]{1,0:T(8,128)(2,1)S(1)}) custom-call(f32[4,40,768]{2,1,0:T(8,128)S(1)} %get-tuple-element.34.refs_0_, f32[4,40,768]{2,1,0:T(8,128)S(1)} %collective-permute-done.20.refs_1_, ...), custom_call_target="tpu_custom_call" | custom-call | flops 293601280 | bytes 2408448 | tf_op jit(solution)/shard_map/pallas_call | solution.py:167
  43.2 0.7 collective-permute-start.21
  43.9 0.0 collective-permute-done.8
  43.9 0.7 collective-permute-start.22
  44.6 0.7 collective-permute-start.23
  45.3 0.1 add_convert_fusion.1
  45.3 1.3 %collective-permute-start.11 = (bf16[40,1792]{1,0:T(8,128)(2,1)S(1)}, bf16[40,1792]{1,0:T(8,128)(2,1)S(1)}, u32[]{:S(2)}, u32[]{:S(2)}) collective-permute-start(bf16[40,1792]{1,0:T(8,128)(2,1)S(1)} %add_convert_fusion.1), channel_id=1, source_target_pairs={{16,0},{18,2},{20,4},{22,6},{24,8},{26,10},{28,12},{30,14},{17,1},... | collective-permute-start | bytes 430088 | tf_op jit(solution)/shard_map/ppermute | solution.py:303
  46.6 0.0 collective-permute-done.21
  46.7 0.0 collective-permute-done.23
  46.7 0.1 add_convert_fusion
  46.8 1.3 %collective-permute-start.24 = (bf16[40,1792]{1,0:T(8,128)(2,1)S(1)}, bf16[40,1792]{1,0:T(8,128)(2,1)S(1)}, u32[]{:S(2)}, u32[]{:S(2)}) collective-permute-start(bf16[40,1792]{1,0:T(8,128)(2,1)S(1)} %add_convert_fusion), channel_id=1, source_target_pairs={{16,8},{18,10},{20,12},{22,14},{24,0},{26,2},{28,4},{30,6},{17,9},... | collective-permute-start | bytes 430088 | tf_op jit(solution)/shard_map/ppermute | solution.py:303
  48.1 4.3 %shard_map.109 = (bf16[1792,256]{1,0:T(8,128)(2,1)}, bf16[1792,256]{1,0:T(8,128)(2,1)}, bf16[1792,256]{1,0:T(8,128)(2,1)}) custom-call(bf16[288,1792]{1,0:T(8,128)(2,1)S(1)} %get-tuple-element.39.refs_0_, bf16[288,1792]{1,0:T(8,128)(2,1)S(1)} %get-tuple-element.40.refs_1_, bf16[288,768]{1,0:T(8,128)(2,1)S(1)} %get-tuple-element.41.refs_2_, ...), custom_call_target="tpu_custom_call" | custom-call | flops 1585446912 | bytes 4816896 | tf_op jit(solution)/shard_map/pallas_call | solution.py:192
  52.3 0.6 collective-permute-done.routes_ref
  52.9 13.0 %collective-permute-done.11.refs_0_ = bf16[40,1792]{1,0:T(8,128)(2,1)S(1)} collective-permute-done((bf16[40,1792]{1,0:T(8,128)(2,1)S(1)}, bf16[40,1792]{1,0:T(8,128)(2,1)S(1)}, u32[]{:S(2)}, u32[]{:S(2)}) %collective-permute-start.11) | collective-permute-done | bytes 143392 | tf_op jit(solution)/shard_map/ppermute | solution.py:303
  65.9 8.9 %collective-permute-done.24.refs_1_ = bf16[40,1792]{1,0:T(8,128)(2,1)S(1)} collective-permute-done((bf16[40,1792]{1,0:T(8,128)(2,1)S(1)}, bf16[40,1792]{1,0:T(8,128)(2,1)S(1)}, u32[]{:S(2)}, u32[]{:S(2)}) %collective-permute-start.24) | collective-permute-done | bytes 143392 | tf_op jit(solution)/shard_map/ppermute | solution.py:303
  74.8 1.1 %shard_map.108 = bf16[64,1792]{1,0:T(8,128)(2,1)} custom-call(s32[1,64]{1,0:T(1,128)S(1)} %collective-permute-done.routes_ref, bf16[40,1792]{1,0:T(8,128)(2,1)S(1)} %collective-permute-done.11.refs_0_, bf16[40,1792]{1,0:T(8,128)(2,1)S(1)} %collective-permute-done.24.refs_1_), custom_call_target="tpu_custom_call" | custom-call | flops 18350080 | bytes 516096 | tf_op jit(solution)/shard_map/pallas_call | solution.py:218
  (16 shorter events, 0.0 us)
Async XLA Ops:
  0.6 32.2 %copy-start = (bf16[1,1792,256]{2,1,0:T(8,128)(2,1)S(1)}, bf16[1,1792,256]{2,1,0:T(8,128)(2,1)}, u32[]{:S(2)}) copy-start(bf16[1,1792,256]{2,1,0:T(8,128)(2,1)} %param.11) | copy-start | bytes 2752516
  0.6 1.0 %copy-start.5 = (bf16[1,64,1792]{2,1,0:T(8,128)(2,1)S(1)}, bf16[1,64,1792]{2,1,0:T(8,128)(2,1)}, u32[]{:S(2)}) copy-start(bf16[1,64,1792]{2,1,0:T(8,128)(2,1)} %param.7) | copy-start | bytes 688132
  1.7 0.9 %copy-start.6 = (bf16[1,64,1792]{2,1,0:T(8,128)(2,1)S(1)}, bf16[1,64,1792]{2,1,0:T(8,128)(2,1)}, u32[]{:S(2)}) copy-start(bf16[1,64,1792]{2,1,0:T(8,128)(2,1)} %param.10) | copy-start | bytes 688132
  2.6 0.7 copy-start.7
  3.3 0.7 copy-start.8
  4.4 14.1 %collective-permute-start.12 = (bf16[72,896]{1,0:T(8,128)(2,1)S(1)}, bf16[72,896]{1,0:T(8,128)(2,1)S(1)}, u32[]{:S(2)}, u32[]{:S(2)}) collective-permute-start(bf16[72,896]{1,0:T(8,128)(2,1)S(1)} %get-tuple-element.32), channel_id=1, source_target_pairs={{0,8},{2,10},{4,12},{6,14},{8,0},{10,2},{12,4},{14,6},{1,9},{3,11}... | collective-permute-start | bytes 387080 | tf_op jit(solution)/shard_map/ppermute | solution.py:258
  8.5 11.8 %collective-permute-start.13 = (bf16[72,896]{1,0:T(8,128)(2,1)S(1)}, bf16[72,896]{1,0:T(8,128)(2,1)S(1)}, u32[]{:S(2)}, u32[]{:S(2)}) collective-permute-start(bf16[72,896]{1,0:T(8,128)(2,1)S(1)} %get-tuple-element.33), channel_id=1, source_target_pairs={{0,8},{2,10},{4,12},{6,14},{8,0},{10,2},{12,4},{14,6},{1,9},{3,11}... | collective-permute-start | bytes 387080 | tf_op jit(solution)/shard_map/ppermute | solution.py:258
  9.0 12.0 %collective-permute-start.3 = (bf16[72,896]{1,0:T(8,128)(2,1)S(1)}, bf16[72,896]{1,0:T(8,128)(2,1)S(1)}, u32[]{:S(2)}, u32[]{:S(2)}) collective-permute-start(bf16[72,896]{1,0:T(8,128)(2,1)S(1)} %get-tuple-element.25.refs_0_), channel_id=1, source_target_pairs={{0,4},{2,6},{4,0},{6,2},{8,12},{10,14},{12,8},{14,10},{1,5},{3,7},... | collective-permute-start | bytes 387080 | tf_op jit(solution)/shard_map/ppermute | solution.py:241
  10.9 11.6 %collective-permute-start.1 = (bf16[72,896]{1,0:T(8,128)(2,1)S(1)}, bf16[72,896]{1,0:T(8,128)(2,1)S(1)}, u32[]{:S(2)}, u32[]{:S(2)}) collective-permute-start(bf16[72,896]{1,0:T(8,128)(2,1)S(1)} %get-tuple-element.25.refs_0_), channel_id=1, source_target_pairs={{0,2},{2,0},{4,6},{6,4},{8,10},{10,8},{12,14},{14,12},{1,3},{3,1},... | collective-permute-start | bytes 387080 | tf_op jit(solution)/shard_map/ppermute | solution.py:241
  12.4 10.6 %collective-permute-start.4 = (bf16[72,896]{1,0:T(8,128)(2,1)S(1)}, bf16[72,896]{1,0:T(8,128)(2,1)S(1)}, u32[]{:S(2)}, u32[]{:S(2)}) collective-permute-start(bf16[72,896]{1,0:T(8,128)(2,1)S(1)} %get-tuple-element.26.refs_1_), channel_id=1, source_target_pairs={{0,4},{2,6},{4,0},{6,2},{8,12},{10,14},{12,8},{14,10},{1,5},{3,7},... | collective-permute-start | bytes 387080 | tf_op jit(solution)/shard_map/ppermute | solution.py:241
  18.4 6.1 %collective-permute-start.2 = (bf16[72,896]{1,0:T(8,128)(2,1)S(1)}, bf16[72,896]{1,0:T(8,128)(2,1)S(1)}, u32[]{:S(2)}, u32[]{:S(2)}) collective-permute-start(bf16[72,896]{1,0:T(8,128)(2,1)S(1)} %get-tuple-element.26.refs_1_), channel_id=1, source_target_pairs={{0,2},{2,0},{4,6},{6,4},{8,10},{10,8},{12,14},{14,12},{1,3},{3,1},... | collective-permute-start | bytes 387080 | tf_op jit(solution)/shard_map/ppermute | solution.py:241
  20.3 5.2 %collective-permute-start.16 = (bf16[72,896]{1,0:T(8,128)(2,1)S(1)}, bf16[72,896]{1,0:T(8,128)(2,1)S(1)}, u32[]{:S(2)}, u32[]{:S(2)}) collective-permute-start(bf16[72,896]{1,0:T(8,128)(2,1)S(1)} %collective-permute-done.12.refs_0_), channel_id=1, source_target_pairs={{0,4},{2,6},{4,0},{6,2},{8,12},{10,14},{12,8},{14,10},{1,5},{3,7},... | collective-permute-start | bytes 387080 | tf_op jit(solution)/shard_map/ppermute | solution.py:241
  21.0 6.3 %collective-permute-start.15 = (bf16[72,896]{1,0:T(8,128)(2,1)S(1)}, bf16[72,896]{1,0:T(8,128)(2,1)S(1)}, u32[]{:S(2)}, u32[]{:S(2)}) collective-permute-start(bf16[72,896]{1,0:T(8,128)(2,1)S(1)} %collective-permute-done.13.refs_1_), channel_id=1, source_target_pairs={{0,2},{2,0},{4,6},{6,4},{8,10},{10,8},{12,14},{14,12},{1,3},{3,1},... | collective-permute-start | bytes 387080 | tf_op jit(solution)/shard_map/ppermute | solution.py:241
  22.5 7.6 %collective-permute-start.5 = (bf16[72,896]{1,0:T(8,128)(2,1)S(1)}, bf16[72,896]{1,0:T(8,128)(2,1)S(1)}, u32[]{:S(2)}, u32[]{:S(2)}) collective-permute-start(bf16[72,896]{1,0:T(8,128)(2,1)S(1)} %collective-permute-done.3.refs_4_), channel_id=1, source_target_pairs={{0,2},{2,0},{4,6},{6,4},{8,10},{10,8},{12,14},{14,12},{1,3},{3,1},... | collective-permute-start | bytes 387080 | tf_op jit(solution)/shard_map/ppermute | solution.py:241
  23.0 9.8 %collective-permute-start.6 = (bf16[72,896]{1,0:T(8,128)(2,1)S(1)}, bf16[72,896]{1,0:T(8,128)(2,1)S(1)}, u32[]{:S(2)}, u32[]{:S(2)}) collective-permute-start(bf16[72,896]{1,0:T(8,128)(2,1)S(1)} %collective-permute-done.4.refs_5_), channel_id=1, source_target_pairs={{0,2},{2,0},{4,6},{6,4},{8,10},{10,8},{12,14},{14,12},{1,3},{3,1},... | collective-permute-start | bytes 387080 | tf_op jit(solution)/shard_map/ppermute | solution.py:241
  24.6 11.7 %collective-permute-start.14 = (bf16[72,896]{1,0:T(8,128)(2,1)S(1)}, bf16[72,896]{1,0:T(8,128)(2,1)S(1)}, u32[]{:S(2)}, u32[]{:S(2)}) collective-permute-start(bf16[72,896]{1,0:T(8,128)(2,1)S(1)} %collective-permute-done.12.refs_0_), channel_id=1, source_target_pairs={{0,2},{2,0},{4,6},{6,4},{8,10},{10,8},{12,14},{14,12},{1,3},{3,1},... | collective-permute-start | bytes 387080 | tf_op jit(solution)/shard_map/ppermute | solution.py:241
  25.5 10.8 %collective-permute-start.17 = (bf16[72,896]{1,0:T(8,128)(2,1)S(1)}, bf16[72,896]{1,0:T(8,128)(2,1)S(1)}, u32[]{:S(2)}, u32[]{:S(2)}) collective-permute-start(bf16[72,896]{1,0:T(8,128)(2,1)S(1)} %collective-permute-done.13.refs_1_), channel_id=1, source_target_pairs={{0,4},{2,6},{4,0},{6,2},{8,12},{10,14},{12,8},{14,10},{1,5},{3,7},... | collective-permute-start | bytes 387080 | tf_op jit(solution)/shard_map/ppermute | solution.py:241
  27.3 9.9 %collective-permute-start.18 = (bf16[72,896]{1,0:T(8,128)(2,1)S(1)}, bf16[72,896]{1,0:T(8,128)(2,1)S(1)}, u32[]{:S(2)}, u32[]{:S(2)}) collective-permute-start(bf16[72,896]{1,0:T(8,128)(2,1)S(1)} %collective-permute-done.16.refs_4_), channel_id=1, source_target_pairs={{0,2},{2,0},{4,6},{6,4},{8,10},{10,8},{12,14},{14,12},{1,3},{3,1},... | collective-permute-start | bytes 387080 | tf_op jit(solution)/shard_map/ppermute | solution.py:241
  30.1 7.1 %collective-permute-start.19 = (bf16[72,896]{1,0:T(8,128)(2,1)S(1)}, bf16[72,896]{1,0:T(8,128)(2,1)S(1)}, u32[]{:S(2)}, u32[]{:S(2)}) collective-permute-start(bf16[72,896]{1,0:T(8,128)(2,1)S(1)} %collective-permute-done.15.refs_3_), channel_id=1, source_target_pairs={{0,4},{2,6},{4,0},{6,2},{8,12},{10,14},{12,8},{14,10},{1,5},{3,7},... | collective-permute-start | bytes 387080 | tf_op jit(solution)/shard_map/ppermute | solution.py:241
  32.9 1.2 %copy-start.1 = (bf16[1,1792,256]{2,1,0:T(8,128)(2,1)S(1)}, bf16[1,1792,256]{2,1,0:T(8,128)(2,1)}, u32[]{:S(2)}) copy-start(bf16[1,1792,256]{2,1,0:T(8,128)(2,1)} %param.12) | copy-start | bytes 2752516
  34.0 1.2 %copy-start.3 = (bf16[1,1792,256]{2,1,0:T(8,128)(2,1)S(1)}, bf16[1,1792,256]{2,1,0:T(8,128)(2,1)}, u32[]{:S(2)}) copy-start(bf16[1,1792,256]{2,1,0:T(8,128)(2,1)} %param.13) | copy-start | bytes 2752516
  35.2 2.0 %copy-start.2 = (bf16[1,1792,256]{2,1,0:T(8,128)(2,1)S(1)}, bf16[1,1792,256]{2,1,0:T(8,128)(2,1)}, u32[]{:S(2)}) copy-start(bf16[1,1792,256]{2,1,0:T(8,128)(2,1)} %param.12) | copy-start | bytes 2752516
  35.2 2.0 %copy-start.4 = (bf16[1,1792,256]{2,1,0:T(8,128)(2,1)S(1)}, bf16[1,1792,256]{2,1,0:T(8,128)(2,1)}, u32[]{:S(2)}) copy-start(bf16[1,1792,256]{2,1,0:T(8,128)(2,1)} %param.13) | copy-start | bytes 2752516
  36.2 2.1 %collective-permute-start.7 = (f32[4,40,768]{2,1,0:T(8,128)S(1)}, f32[4,40,768]{2,1,0:T(8,128)S(1)}, u32[]{:S(2)}, u32[]{:S(2)}) collective-permute-start(f32[4,40,768]{2,1,0:T(8,128)S(1)} %get-tuple-element.27.refs_0_), channel_id=1, source_target_pairs={{0,1},{1,0},{2,3},{3,2},{4,5},{5,4},{6,7},{7,6},{8,9},{9,8},{10,11... | collective-permute-start | bytes 1474568 | tf_op jit(solution)/shard_map/ppermute | solution.py:287
  38.2 4.2 %collective-permute-start.20 = (f32[4,40,768]{2,1,0:T(8,128)S(1)}, f32[4,40,768]{2,1,0:T(8,128)S(1)}, u32[]{:S(2)}, u32[]{:S(2)}) collective-permute-start(f32[4,40,768]{2,1,0:T(8,128)S(1)} %get-tuple-element.34.refs_0_), channel_id=1, source_target_pairs={{0,1},{1,0},{2,3},{3,2},{4,5},{5,4},{6,7},{7,6},{8,9},{9,8},{10,11... | collective-permute-start | bytes 1474568 | tf_op jit(solution)/shard_map/ppermute | solution.py:287
  39.1 4.8 %collective-permute-start.8 = (bf16[40,1792]{1,0:T(8,128)(2,1)S(1)}, bf16[40,1792]{1,0:T(8,128)(2,1)S(1)}, u32[]{:S(2)}, u32[]{:S(2)}) collective-permute-start(bf16[40,1792]{1,0:T(8,128)(2,1)S(1)} %get-tuple-element.29), channel_id=1, source_target_pairs={{16,18},{18,16},{20,22},{22,20},{24,26},{26,24},{28,30},{30,28},{1... | collective-permute-start | bytes 430088 | tf_op jit(solution)/shard_map/ppermute | solution.py:249
  39.7 1.4 %copy-start.9 = (s32[1,64,1]{1,2,0:T(1,128)S(1)}, s32[1,64,1]{1,2,0:T(1,128)}, u32[]{:S(2)}) copy-start(s32[1,64,1]{1,2,0:T(1,128)} %param.8) | copy-start | bytes 772
  39.7 4.8 %collective-permute-start.9 = (bf16[40,1792]{1,0:T(8,128)(2,1)S(1)}, bf16[40,1792]{1,0:T(8,128)(2,1)S(1)}, u32[]{:S(2)}, u32[]{:S(2)}) collective-permute-start(bf16[40,1792]{1,0:T(8,128)(2,1)S(1)} %get-tuple-element.30), channel_id=1, source_target_pairs={{16,20},{18,22},{20,16},{22,18},{24,28},{26,30},{28,24},{30,26},{1... | collective-permute-start | bytes 430088 | tf_op jit(solution)/shard_map/ppermute | solution.py:249
  40.4 4.8 %collective-permute-start.10 = (bf16[40,1792]{1,0:T(8,128)(2,1)S(1)}, bf16[40,1792]{1,0:T(8,128)(2,1)S(1)}, u32[]{:S(2)}, u32[]{:S(2)}) collective-permute-start(bf16[40,1792]{1,0:T(8,128)(2,1)S(1)} %get-tuple-element.31), channel_id=1, source_target_pairs={{16,22},{18,20},{20,18},{22,16},{24,30},{26,28},{28,26},{30,24},{1... | collective-permute-start | bytes 430088 | tf_op jit(solution)/shard_map/ppermute | solution.py:249
  41.1 11.8 %collective-permute-start = (s32[1,64]{1,0:T(1,128)S(1)}, s32[1,64]{1,0:T(1,128)S(1)}, u32[]{:S(2)}, u32[]{:S(2)}) collective-permute-start(s32[1,64]{1,0:T(1,128)S(1)} %bitcast.29), channel_id=1, source_target_pairs={{16,0},{17,1},{18,2},{19,3},{20,4},{21,5},{22,6},{23,7},{24,8},{25... | collective-permute-start | bytes 776 | tf_op jit(solution)/shard_map/ppermute | solution.py:262
  43.2 3.5 %collective-permute-start.21 = (bf16[40,1792]{1,0:T(8,128)(2,1)S(1)}, bf16[40,1792]{1,0:T(8,128)(2,1)S(1)}, u32[]{:S(2)}, u32[]{:S(2)}) collective-permute-start(bf16[40,1792]{1,0:T(8,128)(2,1)S(1)} %get-tuple-element.36), channel_id=1, source_target_pairs={{16,18},{18,16},{20,22},{22,20},{24,26},{26,24},{28,30},{30,28},{1... | collective-permute-start | bytes 430088 | tf_op jit(solution)/shard_map/ppermute | solution.py:249
  43.9 2.8 %collective-permute-start.22 = (bf16[40,1792]{1,0:T(8,128)(2,1)S(1)}, bf16[40,1792]{1,0:T(8,128)(2,1)S(1)}, u32[]{:S(2)}, u32[]{:S(2)}) collective-permute-start(bf16[40,1792]{1,0:T(8,128)(2,1)S(1)} %get-tuple-element.37), channel_id=1, source_target_pairs={{16,20},{18,22},{20,16},{22,18},{24,28},{26,30},{28,24},{30,26},{1... | collective-permute-start | bytes 430088 | tf_op jit(solution)/shard_map/ppermute | solution.py:249
  44.6 2.1 %collective-permute-start.23 = (bf16[40,1792]{1,0:T(8,128)(2,1)S(1)}, bf16[40,1792]{1,0:T(8,128)(2,1)S(1)}, u32[]{:S(2)}, u32[]{:S(2)}) collective-permute-start(bf16[40,1792]{1,0:T(8,128)(2,1)S(1)} %get-tuple-element.38), channel_id=1, source_target_pairs={{16,22},{18,20},{20,18},{22,16},{24,30},{26,28},{28,26},{30,24},{1... | collective-permute-start | bytes 430088 | tf_op jit(solution)/shard_map/ppermute | solution.py:249
  45.3 20.6 %collective-permute-start.11 = (bf16[40,1792]{1,0:T(8,128)(2,1)S(1)}, bf16[40,1792]{1,0:T(8,128)(2,1)S(1)}, u32[]{:S(2)}, u32[]{:S(2)}) collective-permute-start(bf16[40,1792]{1,0:T(8,128)(2,1)S(1)} %add_convert_fusion.1), channel_id=1, source_target_pairs={{16,0},{18,2},{20,4},{22,6},{24,8},{26,10},{28,12},{30,14},{17,1},... | collective-permute-start | bytes 430088 | tf_op jit(solution)/shard_map/ppermute | solution.py:303
  46.8 28.0 %collective-permute-start.24 = (bf16[40,1792]{1,0:T(8,128)(2,1)S(1)}, bf16[40,1792]{1,0:T(8,128)(2,1)S(1)}, u32[]{:S(2)}, u32[]{:S(2)}) collective-permute-start(bf16[40,1792]{1,0:T(8,128)(2,1)S(1)} %add_convert_fusion), channel_id=1, source_target_pairs={{16,8},{18,10},{20,12},{22,14},{24,0},{26,2},{28,4},{30,6},{17,9},... | collective-permute-start | bytes 430088 | tf_op jit(solution)/shard_map/ppermute | solution.py:303

commit v2 on v1

v2 whole, which is shorter than its diff:
```python
import functools

import jax
import jax.numpy as jnp
from jax import lax
from jax.experimental import pallas as pl
from jax.experimental.pallas import tpu as pltpu
from jax.sharding import PartitionSpec as P

SHARES = 4
F32 = jnp.float32
BF16 = jnp.bfloat16
VMEM_BYTES = 16 * 1024 * 1024


def round_up(value, multiple):
    return -(-value // multiple) * multiple


def call(body, out_shape, flops, n_bytes, scratch=(), in_specs=None):
    placed = {} if in_specs is None else {"in_specs": in_specs}
    return functools.partial(
        pl.pallas_call,
        out_shape=out_shape,
        scratch_shapes=list(scratch),
        **placed,
        compiler_params=pltpu.CompilerParams(vmem_limit_bytes=VMEM_BYTES),
        cost_estimate=pl.CostEstimate(flops=flops, bytes_accessed=n_bytes, transcendentals=0),
    )(body)


def dot(left, right, left_dim=1, right_dim=0):
    return lax.dot_general(
        left, right, (((left_dim,), (right_dim,)), ((), ())), preferred_element_type=F32
    )


def slots(routes, n_experts):
    chosen, n_tokens = routes.shape
    shift = lax.axis_index("expert") // SHARES
    relative = routes - shift
    relative = jnp.where(relative < 0, relative + n_experts, relative)
    experts = lax.broadcasted_iota(jnp.int32, (round_up(n_experts, 8), n_tokens), 0)
    named = [relative[k : k + 1] == experts for k in range(chosen)]
    count = sum(one.astype(F32) for one in named)
    earlier = (
        lax.broadcasted_iota(jnp.int32, (n_tokens, n_tokens), 0)
        < lax.broadcasted_iota(jnp.int32, (n_tokens, n_tokens), 1)
    ).astype(BF16)
    before = dot(count.astype(BF16), earlier)
    slot_rows = []
    for k in range(chosen):
        rank = jnp.sum(jnp.where(named[k], before, 0.0), axis=0, keepdims=True).astype(jnp.int32)
        for other in range(k):
            rank = rank + (relative[other : other + 1] == relative[k : k + 1]).astype(jnp.int32)
        slot_rows.append(rank)
    return relative, slot_rows


def dispatch_blocks(routes, weights, grad_rows, inputs, n_experts, capacity, split):
    chosen, n_tokens = routes.shape
    columns = inputs.shape[1]
    rows = round_up(2 * capacity, 8)
    order = list(range(1, n_experts)) + [0]

    def body(routes_ref, weights_ref, grads_hbm, inputs_hbm, *refs):
        out_refs = refs[: 2 * n_experts]
        grads_ref, inputs_ref, sems = refs[2 * n_experts :]
        copies = [
            pltpu.make_async_copy(inputs_hbm, inputs_ref, sems.at[0]),
            pltpu.make_async_copy(grads_hbm, grads_ref, sems.at[1]),
        ]
        for copy in copies:
            copy.start()
        relative, slot_rows = slots(routes_ref[...], n_experts)
        row = lax.broadcasted_iota(jnp.int32, (rows, n_tokens), 0)
        for copy in copies:
            copy.wait()
        for which in order:
            pick_input = jnp.zeros((rows, n_tokens), F32)
            pick_grad = jnp.zeros((rows, n_tokens), F32)
            scale = jnp.zeros((rows, n_tokens), F32)
            for k in range(chosen):
                target = jnp.where(relative[k : k + 1] == which, slot_rows[k], -2 * rows)
                pick_input = pick_input + (row == target).astype(F32)
                hit = (row == target + capacity).astype(F32)
                pick_grad = pick_grad + hit
                scale = scale + hit * weights_ref[k : k + 1, :]
            scale = jnp.sum(scale, axis=1, keepdims=True)
            pick_input = pick_input.astype(BF16)
            pick_grad = pick_grad.astype(BF16)
            for part, (begin, end) in enumerate(((0, split), (split, columns))):
                block = dot(pick_input, inputs_ref[:, begin:end])
                block = block + dot(pick_grad, grads_ref[:, begin:end]) * scale
                out_refs[2 * which + part][...] = block.astype(BF16)

    shapes = (
        jax.ShapeDtypeStruct((rows, split), BF16),
        jax.ShapeDtypeStruct((rows, columns - split), BF16),
    )
    in_vmem, in_hbm = pl.BlockSpec(memory_space=pltpu.VMEM), pl.BlockSpec(memory_space=pltpu.HBM)
    outs = call(
        body,
        shapes * n_experts,
        2 * 2 * n_experts * rows * n_tokens * columns,
        2 * n_tokens * columns * 2 + n_experts * rows * columns * 2,
        [
            pltpu.VMEM((n_tokens, columns), BF16),
            pltpu.VMEM((n_tokens, columns), BF16),
            pltpu.SemaphoreType.DMA((2,)),
        ],
        [in_vmem, in_vmem, in_hbm, in_hbm],
    )(routes, weights, grad_rows, inputs)
    return [(outs[2 * which], outs[2 * which + 1]) for which in range(n_experts)]


def stage_weights(gate_cols, up_cols, down_cols):
    columns, width = gate_cols.shape

    def body(gate_hbm, up_hbm, down_hbm, out_ref, sems):
        copies = [
            pltpu.make_async_copy(ref, out_ref.at[:, i * width : (i + 1) * width], sems.at[i])
            for i, ref in enumerate((gate_hbm, up_hbm, down_hbm))
        ]
        for copy in copies:
            copy.start()
        for copy in copies:
            copy.wait()

    return call(
        body,
        jax.ShapeDtypeStruct((columns, 3 * width), BF16),
        2 * columns * width * 256,
        6 * columns * width * 2,
        [pltpu.SemaphoreType.DMA((3,))],
        [pl.BlockSpec(memory_space=pltpu.HBM)] * 3,
    )(gate_cols, up_cols, down_cols)


def partial_products(blocks, staged, capacity, split):
    rows = round_up(2 * capacity, 8)
    kept = round_up(capacity, 8)
    n_blocks = len(blocks)
    columns, width = staged.shape[0], staged.shape[1] // 3

    def body(*refs):
        block_refs = refs[: 2 * n_blocks]
        staged_ref, out_ref, packed_ref = refs[2 * n_blocks :]
        for i in range(n_blocks):
            packed_ref[i * rows : (i + 1) * rows, :split] = block_refs[2 * i][...]
            packed_ref[i * rows : (i + 1) * rows, split:] = block_refs[2 * i + 1][...]
        packed = packed_ref[...]
        gate_up = dot(packed, staged_ref[:, : 2 * width])
        down = dot(packed, staged_ref[:, 2 * width :])
        for i in range(n_blocks):
            at = i * rows
            out_ref[i, :, : 2 * width] = gate_up[at : at + kept]
            out_ref[i, :capacity, 2 * width :] = down[at + capacity : at + 2 * capacity]
            if kept > capacity:
                out_ref[i, capacity:, 2 * width :] = jnp.zeros((kept - capacity, width), F32)

    return call(
        body,
        (
            jax.ShapeDtypeStruct((n_blocks, kept, 3 * width), F32),
            jax.ShapeDtypeStruct((n_blocks * rows, columns), BF16),
        ),
        2 * 3 * n_blocks * rows * columns * width,
        3 * columns * width * 2 + n_blocks * rows * columns * 4,
    )(*[half for block in blocks for half in block], staged)


def hidden_backward(partials, staged, capacity, split):
    n_blocks, kept, width3 = partials[0].shape
    columns, width = staged.shape[0], staged.shape[1] // 3
    rows = round_up(2 * capacity, 8)
    n_parts = len(partials)

    def body(*refs):
        part_refs = refs[:n_parts]
        staged_ref = refs[n_parts]
        back_refs = refs[n_parts + 1 : n_parts + 1 + n_blocks]
        slope_ref = refs[n_parts + 1 + n_blocks]
        valid = lax.broadcasted_iota(jnp.int32, (kept, width), 0) < capacity
        d_gates, d_ups = [], []
        slope_ref[...] = jnp.zeros(slope_ref.shape, BF16)
        for i in range(n_blocks):
            total = part_refs[0][i]
            for ref in part_refs[1:]:
                total = total + ref[i]
            gate = jnp.where(valid, total[:, :width], 0.0)
            up = jnp.where(valid, total[:, width : 2 * width], 0.0)
            grad_hidden = total[:, 2 * width :]
            sigmoid_gate = jax.nn.sigmoid(gate)
            activated = gate * sigmoid_gate
            hidden = (activated * up).astype(BF16)
            slope_term = sigmoid_gate * (1.0 + gate * (1.0 - sigmoid_gate))
            d_gate = (grad_hidden * up * slope_term).astype(BF16)
            d_up = (grad_hidden * activated).astype(BF16)
            at = i * rows
            slope_ref[at : at + capacity, :width] = d_gate[:capacity]
            slope_ref[at : at + capacity, width : 2 * width] = d_up[:capacity]
            slope_ref[at + capacity : at + 2 * capacity, 2 * width :] = hidden[:capacity]
            d_gates.append(d_gate)
            d_ups.append(d_up)
        slope = jnp.concatenate(
            [jnp.concatenate(d_gates, axis=0), jnp.concatenate(d_ups, axis=0)], axis=1
        )
        back = dot(slope, staged_ref[:, : 2 * width], 1, 1)
        for i in range(n_blocks):
            part = back[i * kept : i * kept + capacity].astype(BF16)
            back_refs[i][:capacity, :] = part[:, :split]
            back_refs[i][capacity : 2 * capacity, : columns - split] = part[:, split:]
            if columns < 2 * split:
                back_refs[i][capacity : 2 * capacity, columns - split :] = jnp.zeros(
                    (capacity, 2 * split - columns), BF16
                )
            if rows > 2 * capacity:
                back_refs[i][2 * capacity :, :] = jnp.zeros((rows - 2 * capacity, split), BF16)

    outs = call(
        body,
        tuple(jax.ShapeDtypeStruct((rows, split), BF16) for _ in range(n_blocks))
        + (jax.ShapeDtypeStruct((n_blocks * rows, width3), BF16),),
        2 * 2 * n_blocks * kept * columns * width,
        2 * columns * width * 2 + n_blocks * kept * columns * 2,
    )(*partials, staged)
    return outs[:n_blocks], outs[n_blocks]


def weight_grads(packed, slopes, width):
    columns = packed[0].shape[1]
    n_parts = len(packed)
    n_rows = sum(one.shape[0] for one in packed)

    def body(*refs):
        packed_refs = refs[:n_parts]
        slope_refs = refs[n_parts : 2 * n_parts]
        out_refs = refs[2 * n_parts :]
        total = dot(packed_refs[0][...], slope_refs[0][...], 0, 0)
        for left, right in zip(packed_refs[1:], slope_refs[1:]):
            total = total + dot(left[...], right[...], 0, 0)
        for i in range(3):
            out_refs[i][...] = total[:, i * width : (i + 1) * width].astype(BF16)

    return call(
        body,
        tuple(jax.ShapeDtypeStruct((columns, width), BF16) for _ in range(3)),
        2 * 3 * n_rows * columns * width,
        3 * columns * width * 2 + n_rows * columns * 2,
    )(*packed, *slopes)


def combine(routes, merged, n_experts, capacity, columns):
    chosen, n_tokens = routes.shape
    rows, split = merged[0].shape

    def body(routes_ref, *refs):
        merged_refs, out_ref = refs[:-1], refs[-1]
        relative, slot_rows = slots(routes_ref[...], n_experts)
        row = lax.broadcasted_iota(jnp.int32, (rows, n_tokens), 0)
        last = lax.axis_index("section") == lax.axis_size("section") - 1
        for offset, begin, end in ((0, 0, split), (capacity, split, columns)):
            total = jnp.zeros((n_tokens, end - begin), F32)
            for which, ref in enumerate(merged_refs):
                pick = jnp.zeros((rows, n_tokens), F32)
                for k in range(chosen):
                    target = jnp.where(relative[k : k + 1] == which, slot_rows[k], -2 * rows)
                    pick = pick + (row == target + offset).astype(F32)
                total = total + dot(pick.astype(BF16), ref[:, : end - begin], 0, 0)
            out_ref[:, begin:end] = jnp.where(last, 0.0, total).astype(BF16)

    return call(
        body,
        jax.ShapeDtypeStruct((n_tokens, columns), BF16),
        2 * 2 * n_tokens * columns * rows * len(merged),
        rows * columns * 2 * len(merged) + n_tokens * columns * 2,
    )(routes, *merged)


def per_device(token_grads, routing, gate_weights, layer_inputs, w_gate, w_up, w_down):
    n_groups = lax.axis_size("expert")
    n_sections = lax.axis_size("section")
    n_replicas = lax.axis_size("replica")
    n_experts = n_groups // SHARES
    grad_rows, inputs = token_grads[0], layer_inputs[0]
    routes, weights = routing[0].T, gate_weights[0].T
    gate_cols, up_cols, down_cols = w_gate[0], w_up[0], w_down[0]
    chosen, n_tokens = routes.shape
    columns = inputs.shape[1]
    width = gate_cols.shape[1]
    capacity = min(n_tokens, 17 * n_tokens * chosen // (16 * n_experts))
    split = round_up(columns // 2, 128)

    def partner(value, step):
        return lax.ppermute(value, "expert", [(j, j ^ step) for j in range(n_groups)])

    def crossing(value, which):
        move = SHARES * which
        return lax.ppermute(
            value, "expert", [(j, (j + move) % n_groups) for j in range(n_groups)]
        )

    def homeward(value, which):
        move = SHARES * which
        pairs = [
            (s * n_groups + j, (s - 1) % n_sections * n_groups + (j - move) % n_groups)
            for s in range(n_sections)
            for j in range(n_groups)
        ]
        return lax.ppermute(value, ("section", "expert"), pairs)

    routes_next = lax.ppermute(
        routes, "section", [(s, (s - 1) % n_sections) for s in range(n_sections)]
    )
    own = dispatch_blocks(routes, weights, grad_rows, inputs, n_experts, capacity, split)
    staged = stage_weights(gate_cols, up_cols, down_cols)
    heads = [own[0]] + [
        tuple(crossing(part, which) for part in own[which]) for which in range(1, n_experts)
    ]

    packed, slopes, merged = [], [], []
    for which in range(n_experts):
        lo, hi = heads[which]
        lo_y, hi_y = partner(lo, 1), partner(hi, 1)
        lo_z, hi_z = partner(lo, 2), partner(hi, 2)
        if which == 0:
            lo_d, hi_d = partner(lo_z, 1), partner(hi_z, 1)
        else:
            lo_d, hi_d = partner(lo_z, 1), partner(hi_y, 2)
        blocks = ((lo, hi), (lo_y, hi_y), (lo_z, hi_z), (lo_d, hi_d))
        part, rows_packed = partial_products(blocks, staged, capacity, split)
        parts = [part]
        for turn in range(1, n_replicas):
            parts.append(
                lax.ppermute(
                    part, "replica", [(r, (r + turn) % n_replicas) for r in range(n_replicas)]
                )
            )
        backs, slope = hidden_backward(parts, staged, capacity, split)
        packed.append(rows_packed)
        slopes.append(slope)
        total = backs[0].astype(F32)
        for step in range(1, SHARES):
            total = total + partner(backs[step], step).astype(F32)
        merged.append(homeward(total.astype(BF16), which))

    upstream = combine(routes_next, merged, n_experts, capacity, columns)
    grad_gate, grad_up, grad_down = weight_grads(packed, slopes, width)
    return (upstream[None], grad_gate[None], grad_up[None], grad_down[None])


def solution(mesh):
    placed = (
        P("section", "expert", "replica"),
        P("section", "expert", None),
        P("section", "expert", None),
        P("section", "expert", "replica"),
        P("section", "replica", "expert"),
        P("section", "replica", "expert"),
        P("section", "replica", "expert"),
    )
    return jax.shard_map(
        per_device,
        mesh=mesh,
        in_specs=placed,
        out_specs=(
            P("section", "expert", "replica"),
            P("section", "replica", "expert"),
            P("section", "replica", "expert"),
            P("section", "replica", "expert"),
        ),
        check_vma=False,
    )
```

time: 76.4 us -> 66.6 us (0.87)
  waiting for transfers between devices: 32.5 us -> 15.5 us
  starting transfers between devices: 26.9 us -> 32.8 us
  local copies, waits for them, and re-layouts: 5.63 us -> 6.72 us
    ppermute x9 -> x3, waiting for transfers between devices: 22.4 us -> 1.25 us  [the longest x2 1.25 us: homeward(): return lax.ppermute(value, ('section', 'expert'), pairs)]
    ppermute x12 -> x18, starting transfers between devices: 14.7 us -> 20.6 us  [partner(): lax.ppermute(value, 'expert', [(j, j ^ step) for j in range(n_groups)])]
    ppermute x12 -> x18, waiting for transfers between devices: 4.44 us -> 8.11 us  [partner(): lax.ppermute(value, 'expert', [(j, j ^ step) for j in range(n_groups)])]
    unnamed x20 -> x16, local copies, waits for them, and re-layouts: 5.63 us -> 6.72 us
    ppermute x9 -> x3, starting transfers between devices: 7.9 us -> 7.93 us  [the longest x2 6.13 us: homeward(): return lax.ppermute(value, ('section', 'expert'), pairs)]
  transfers between devices with their start and end apart: 25 -> 25, of which waited for: 9 -> 11; matrix products, arithmetic and copies ran while one was open for 0% -> 0% of each run, Pallas kernels for 11% -> 12%
where the time goes in v2:
time: 66.6 us; the launch traced here: 66.3 us
  starting transfers between devices  32.8 us (49%)
  waiting for transfers between devices  15.5 us (23%)
  Pallas kernels  10.3 us (15%)
  local copies, waits for them, and re-layouts  6.72 us (10%)
  between operations  0.75 us (1%)
    ppermute x18, starting transfers between devices, partner(): lax.ppermute(value, 'expert', [(j, j ^ step) for j in range(n_groups)])  20.6 us
    ppermute x18, waiting for transfers between devices, partner(): lax.ppermute(value, 'expert', [(j, j ^ step) for j in range(n_groups)])  8.11 us
    unnamed x16, local copies, waits for them, and re-layouts  6.72 us
    ppermute x2, starting transfers between devices, homeward(): return lax.ppermute(value, ('section', 'expert'), pairs)  6.13 us
    ppermute x2, waiting for transfers between devices, crossing(): lax.ppermute(value, 'expert', [(j, (j + move) % n_groups) for j in range(...  6.12 us
    pallas_call x1, Pallas kernels, weight_grads(): call(body, tuple((jax.ShapeDtypeStruct((columns, width), BF16) for _ in r...  4.28 us
    ppermute x2, starting transfers between devices, crossing(): lax.ppermute(value, 'expert', [(j, (j + move) % n_groups) for j in range(...  4.21 us
    pallas_call x2, Pallas kernels, partial_products(): call(body, (jax.ShapeDtypeStruct((n_blocks, kept, 3 * width), F32), jax.S...  1.97 us
  transfers between devices with their start and end apart: 25, of which 11 were waited for; matrix products, arithmetic and copies ran while one was open for 0% of the time, Pallas kernels for 12%

profile of v2, /device:TPU:0, one launch (start us, length us, event | category | flops | bytes accessed | tf_op | source)
XLA Modules:
  0.0 66.3 jit_solution(8159246764104581878)
XLA Ops:
  0.6 0.9 %copy-done.3 = bf16[1,64,1792]{2,1,0:T(8,128)(2,1)S(1)} copy-done((bf16[1,64,1792]{2,1,0:T(8,128)(2,1)S(1)}, bf16[1,64,1792]{2,1,0:T(8,128)(2,1)}, u32[]{:S(2)}) %copy-start.3) | copy-done | bytes 229400
  1.6 0.9 %copy-done.4 = bf16[1,64,1792]{2,1,0:T(8,128)(2,1)S(1)} copy-done((bf16[1,64,1792]{2,1,0:T(8,128)(2,1)S(1)}, bf16[1,64,1792]{2,1,0:T(8,128)(2,1)}, u32[]{:S(2)}) %copy-start.4) | copy-done | bytes 229400
  2.5 0.7 copy-done.5
  3.2 0.7 copy-done.6
  3.8 1.2 %shard_map.102 = (bf16[72,896]{1,0:T(8,128)(2,1)S(1)}, bf16[72,896]{1,0:T(8,128)(2,1)S(1)}, bf16[72,896]{1,0:T(8,128)(2,1)S(1)}, bf16[72,896]{1,0:T(8,128)(2,1)S(1)}) custom-call(s32[1,64]{1,0:T(1,128)S(1)} %bitcast.17, f32[1,64]{1,0:T(1,128)S(1)} %bitcast.16, bf16[64,1792]{1,0:T(8,128)(2,1)S(1)} %bitcast.14, bf16[64,1792]{1,0:T(8,128)(2,1)S(1)} %bitcast.15), custom_call_target="tpu_custom_call" | custom-call | flops 66060288 | bytes 974848 | tf_op jit(solution)/shard_map/pallas_call | solution.py:102
  5.0 4.1 %collective-permute-start.12 = (bf16[72,896]{1,0:T(8,128)(2,1)S(1)}, bf16[72,896]{1,0:T(8,128)(2,1)S(1)}, u32[]{:S(2)}, u32[]{:S(2)}) collective-permute-start(bf16[72,896]{1,0:T(8,128)(2,1)S(1)} %get-tuple-element.32), channel_id=1, source_target_pairs={{0,8},{2,10},{4,12},{6,14},{8,0},{10,2},{12,4},{14,6},{1,9},{3,11}... | collective-permute-start | bytes 387080 | tf_op jit(solution)/shard_map/ppermute | solution.py:300
  9.2 0.1 collective-permute-start.13
  9.2 1.8 %collective-permute-start.3 = (bf16[72,896]{1,0:T(8,128)(2,1)S(1)}, bf16[72,896]{1,0:T(8,128)(2,1)S(1)}, u32[]{:S(2)}, u32[]{:S(2)}) collective-permute-start(bf16[72,896]{1,0:T(8,128)(2,1)S(1)} %get-tuple-element.25.refs_0_), channel_id=1, source_target_pairs={{0,4},{2,6},{4,0},{6,2},{8,12},{10,14},{12,8},{14,10},{1,5},{3,7},... | collective-permute-start | bytes 387080 | tf_op jit(solution)/shard_map/ppermute | solution.py:296
  11.1 1.5 %collective-permute-start.1 = (bf16[72,896]{1,0:T(8,128)(2,1)S(1)}, bf16[72,896]{1,0:T(8,128)(2,1)S(1)}, u32[]{:S(2)}, u32[]{:S(2)}) collective-permute-start(bf16[72,896]{1,0:T(8,128)(2,1)S(1)} %get-tuple-element.25.refs_0_), channel_id=1, source_target_pairs={{0,2},{2,0},{4,6},{6,4},{8,10},{10,8},{12,14},{14,12},{1,3},{3,1},... | collective-permute-start | bytes 387080 | tf_op jit(solution)/shard_map/ppermute | solution.py:296
  12.6 0.4 collective-permute-start.4
  13.0 6.1 %collective-permute-done.12.refs_0_ = bf16[72,896]{1,0:T(8,128)(2,1)S(1)} collective-permute-done((bf16[72,896]{1,0:T(8,128)(2,1)S(1)}, bf16[72,896]{1,0:T(8,128)(2,1)S(1)}, u32[]{:S(2)}, u32[]{:S(2)}) %collective-permute-start.12) | collective-permute-done | bytes 129056 | tf_op jit(solution)/shard_map/ppermute | solution.py:300
  19.1 1.8 %collective-permute-start.2 = (bf16[72,896]{1,0:T(8,128)(2,1)S(1)}, bf16[72,896]{1,0:T(8,128)(2,1)S(1)}, u32[]{:S(2)}, u32[]{:S(2)}) collective-permute-start(bf16[72,896]{1,0:T(8,128)(2,1)S(1)} %get-tuple-element.26.refs_1_), channel_id=1, source_target_pairs={{0,2},{2,0},{4,6},{6,4},{8,10},{10,8},{12,14},{14,12},{1,3},{3,1},... | collective-permute-start | bytes 387080 | tf_op jit(solution)/shard_map/ppermute | solution.py:296
  20.9 0.1 collective-permute-done.13.refs_1_
  21.0 0.7 %collective-permute-start.16 = (bf16[72,896]{1,0:T(8,128)(2,1)S(1)}, bf16[72,896]{1,0:T(8,128)(2,1)S(1)}, u32[]{:S(2)}, u32[]{:S(2)}) collective-permute-start(bf16[72,896]{1,0:T(8,128)(2,1)S(1)} %collective-permute-done.12.refs_0_), channel_id=1, source_target_pairs={{0,4},{2,6},{4,0},{6,2},{8,12},{10,14},{12,8},{14,10},{1,5},{3,7},... | collective-permute-start | bytes 387080 | tf_op jit(solution)/shard_map/ppermute | solution.py:296
  21.7 0.0 collective-permute-done.3.refs_4_
  21.7 1.5 %collective-permute-start.15 = (bf16[72,896]{1,0:T(8,128)(2,1)S(1)}, bf16[72,896]{1,0:T(8,128)(2,1)S(1)}, u32[]{:S(2)}, u32[]{:S(2)}) collective-permute-start(bf16[72,896]{1,0:T(8,128)(2,1)S(1)} %collective-permute-done.13.refs_1_), channel_id=1, source_target_pairs={{0,2},{2,0},{4,6},{6,4},{8,10},{10,8},{12,14},{14,12},{1,3},{3,1},... | collective-permute-start | bytes 387080 | tf_op jit(solution)/shard_map/ppermute | solution.py:296
  23.2 0.0 collective-permute-done.1.refs_2_
  23.2 0.5 collective-permute-start.5
  23.7 0.0 collective-permute-done.4.refs_5_
  23.7 1.5 %collective-permute-start.6 = (bf16[72,896]{1,0:T(8,128)(2,1)S(1)}, bf16[72,896]{1,0:T(8,128)(2,1)S(1)}, u32[]{:S(2)}, u32[]{:S(2)}) collective-permute-start(bf16[72,896]{1,0:T(8,128)(2,1)S(1)} %collective-permute-done.4.refs_5_), channel_id=1, source_target_pairs={{0,2},{2,0},{4,6},{6,4},{8,10},{10,8},{12,14},{14,12},{1,3},{3,1},... | collective-permute-start | bytes 387080 | tf_op jit(solution)/shard_map/ppermute | solution.py:296
  25.2 1.2 %copy-done = bf16[1,1792,256]{2,1,0:T(8,128)(2,1)S(1)} copy-done((bf16[1,1792,256]{2,1,0:T(8,128)(2,1)S(1)}, bf16[1,1792,256]{2,1,0:T(8,128)(2,1)}, u32[]{:S(2)}) %copy-start) | copy-done | bytes 917528
  26.4 1.2 %copy-done.1 = bf16[1,1792,256]{2,1,0:T(8,128)(2,1)S(1)} copy-done((bf16[1,1792,256]{2,1,0:T(8,128)(2,1)S(1)}, bf16[1,1792,256]{2,1,0:T(8,128)(2,1)}, u32[]{:S(2)}) %copy-start.1) | copy-done | bytes 917528
  27.6 1.2 %copy-done.2 = bf16[1,1792,256]{2,1,0:T(8,128)(2,1)S(1)} copy-done((bf16[1,1792,256]{2,1,0:T(8,128)(2,1)S(1)}, bf16[1,1792,256]{2,1,0:T(8,128)(2,1)}, u32[]{:S(2)}) %copy-start.2) | copy-done | bytes 917528
  28.8 0.2 shard_map.103.refs_8_.refs_2_
  29.0 0.0 collective-permute-done.2.refs_3_
  29.0 0.6 collective-permute-start.14
  29.6 0.0 collective-permute-done.16.refs_4_
  29.6 1.4 %collective-permute-start.17 = (bf16[72,896]{1,0:T(8,128)(2,1)S(1)}, bf16[72,896]{1,0:T(8,128)(2,1)S(1)}, u32[]{:S(2)}, u32[]{:S(2)}) collective-permute-start(bf16[72,896]{1,0:T(8,128)(2,1)S(1)} %collective-permute-done.13.refs_1_), channel_id=1, source_target_pairs={{0,4},{2,6},{4,0},{6,2},{8,12},{10,14},{12,8},{14,10},{1,5},{3,7},... | collective-permute-start | bytes 387080 | tf_op jit(solution)/shard_map/ppermute | solution.py:296
  30.9 0.0 collective-permute-done.15.refs_3_
  30.9 1.6 %collective-permute-start.18 = (bf16[72,896]{1,0:T(8,128)(2,1)S(1)}, bf16[72,896]{1,0:T(8,128)(2,1)S(1)}, u32[]{:S(2)}, u32[]{:S(2)}) collective-permute-start(bf16[72,896]{1,0:T(8,128)(2,1)S(1)} %collective-permute-done.16.refs_4_), channel_id=1, source_target_pairs={{0,2},{2,0},{4,6},{6,4},{8,10},{10,8},{12,14},{14,12},{1,3},{3,1},... | collective-permute-start | bytes 387080 | tf_op jit(solution)/shard_map/ppermute | solution.py:296
  32.5 0.0 collective-permute-done.5.refs_6_
  32.5 0.6 collective-permute-start.19
  33.1 0.4 collective-permute-done.6.refs_7_
  33.5 1.0 %shard_map.104 = (f32[4,40,768]{2,1,0:T(8,128)S(1)}, bf16[288,1792]{1,0:T(8,128)(2,1)S(1)}) custom-call(bf16[72,896]{1,0:T(8,128)(2,1)S(1)} %get-tuple-element.25.refs_0_, bf16[72,896]{1,0:T(8,128)(2,1)S(1)} %get-tuple-element.26.refs_1_, bf16[72,896]{1,0:T(8,128)(2,1)S(1)} %collective-permute-done.1.refs_2_, ...), custom_call_target="tpu_custom_call" | custom-call | flops 792723456 | bytes 4816896 | tf_op jit(solution)/shard_map/pallas_call | solution.py:162
  34.5 0.1 collective-permute-start.7
  34.6 1.7 %collective-permute-done.14.refs_2_ = bf16[72,896]{1,0:T(8,128)(2,1)S(1)} collective-permute-done((bf16[72,896]{1,0:T(8,128)(2,1)S(1)}, bf16[72,896]{1,0:T(8,128)(2,1)S(1)}, u32[]{:S(2)}, u32[]{:S(2)}) %collective-permute-start.14) | collective-permute-done | bytes 129056 | tf_op jit(solution)/shard_map/ppermute | solution.py:296
  36.3 0.0 collective-permute-done.17.refs_5_
  36.3 1.6 %collective-permute-done.18.refs_6_ = bf16[72,896]{1,0:T(8,128)(2,1)S(1)} collective-permute-done((bf16[72,896]{1,0:T(8,128)(2,1)S(1)}, bf16[72,896]{1,0:T(8,128)(2,1)S(1)}, u32[]{:S(2)}, u32[]{:S(2)}) %collective-permute-start.18) | collective-permute-done | bytes 129056 | tf_op jit(solution)/shard_map/ppermute | solution.py:296
  37.9 1.0 %shard_map.106 = (f32[4,40,768]{2,1,0:T(8,128)S(1)}, bf16[288,1792]{1,0:T(8,128)(2,1)S(1)}) custom-call(bf16[72,896]{1,0:T(8,128)(2,1)S(1)} %collective-permute-done.12.refs_0_, bf16[72,896]{1,0:T(8,128)(2,1)S(1)} %collective-permute-done.13.refs_1_, bf16[72,896]{1,0:T(8,128)(2,1)S(1)} %collective-permute-done.14.refs_2_, ...), custom_call_target="tpu_custom_call" | custom-call | flops 792723456 | bytes 4816896 | tf_op jit(solution)/shard_map/pallas_call | solution.py:162
  38.9 0.0 copy-start.7
  38.9 0.1 collective-permute-start.20
  39.0 0.8 %shard_map.105 = (bf16[72,896]{1,0:T(8,128)(2,1)S(1)}, bf16[72,896]{1,0:T(8,128)(2,1)S(1)}, bf16[72,896]{1,0:T(8,128)(2,1)S(1)}, bf16[72,896]{1,0:T(8,128)(2,1)S(1)}, bf16[288,768]{1,0:T(8,128)(2,1)S(1)}) custom-call(f32[4,40,768]{2,1,0:T(8,128)S(1)} %get-tuple-element.27.refs_0_, f32[4,40,768]{2,1,0:T(8,128)S(1)} %collective-permute-done.7.refs_1_, ...), custom_call_target="tpu_custom_call" | custom-call | flops 293601280 | bytes 2408448 | tf_op jit(solution)/shard_map/pallas_call | solution.py:221
  39.7 1.9 %collective-permute-start.8 = (bf16[72,896]{1,0:T(8,128)(2,1)S(1)}, bf16[72,896]{1,0:T(8,128)(2,1)S(1)}, u32[]{:S(2)}, u32[]{:S(2)}) collective-permute-start(bf16[72,896]{1,0:T(8,128)(2,1)S(1)} %get-tuple-element.29), channel_id=1, source_target_pairs={{0,2},{2,0},{4,6},{6,4},{8,10},{10,8},{12,14},{14,12},{1,3},{3,1},... | collective-permute-start | bytes 387080 | tf_op jit(solution)/shard_map/ppermute | solution.py:296
  41.6 1.6 %collective-permute-start.10 = (bf16[72,896]{1,0:T(8,128)(2,1)S(1)}, bf16[72,896]{1,0:T(8,128)(2,1)S(1)}, u32[]{:S(2)}, u32[]{:S(2)}) collective-permute-start(bf16[72,896]{1,0:T(8,128)(2,1)S(1)} %get-tuple-element.31), channel_id=1, source_target_pairs={{0,6},{2,4},{4,2},{6,0},{8,14},{10,12},{12,10},{14,8},{1,7},{3,5},... | collective-permute-start | bytes 387080 | tf_op jit(solution)/shard_map/ppermute | solution.py:296
  43.3 1.8 %collective-permute-start = (s32[1,64]{1,0:T(1,128)S(1)}, s32[1,64]{1,0:T(1,128)S(1)}, u32[]{:S(2)}, u32[]{:S(2)}) collective-permute-start(s32[1,64]{1,0:T(1,128)S(1)} %bitcast.18), channel_id=1, source_target_pairs={{0,16},{16,0},{1,17},{17,1},{2,18},{18,2},{3,19},{19,3},{4,20},{20... | collective-permute-start | bytes 776 | tf_op jit(solution)/shard_map/ppermute | solution.py:313
  45.1 0.0 collective-permute-done.20.refs_1_
  45.1 0.8 %shard_map.107 = (bf16[72,896]{1,0:T(8,128)(2,1)S(1)}, bf16[72,896]{1,0:T(8,128)(2,1)S(1)}, bf16[72,896]{1,0:T(8,128)(2,1)S(1)}, bf16[72,896]{1,0:T(8,128)(2,1)S(1)}, bf16[288,768]{1,0:T(8,128)(2,1)S(1)}) custom-call(f32[4,40,768]{2,1,0:T(8,128)S(1)} %get-tuple-element.34.refs_0_, f32[4,40,768]{2,1,0:T(8,128)S(1)} %collective-permute-done.20.refs_1_, ...), custom_call_target="tpu_custom_call" | custom-call | flops 293601280 | bytes 2408448 | tf_op jit(solution)/shard_map/pallas_call | solution.py:221
  45.8 1.6 %collective-permute-start.21 = (bf16[72,896]{1,0:T(8,128)(2,1)S(1)}, bf16[72,896]{1,0:T(8,128)(2,1)S(1)}, u32[]{:S(2)}, u32[]{:S(2)}) collective-permute-start(bf16[72,896]{1,0:T(8,128)(2,1)S(1)} %get-tuple-element.36), channel_id=1, source_target_pairs={{0,2},{2,0},{4,6},{6,4},{8,10},{10,8},{12,14},{14,12},{1,3},{3,1},... | collective-permute-start | bytes 387080 | tf_op jit(solution)/shard_map/ppermute | solution.py:296
  47.4 0.0 collective-permute-start.22
  47.4 0.5 collective-permute-done.9
  48.0 1.5 %collective-permute-start.23 = (bf16[72,896]{1,0:T(8,128)(2,1)S(1)}, bf16[72,896]{1,0:T(8,128)(2,1)S(1)}, u32[]{:S(2)}, u32[]{:S(2)}) collective-permute-start(bf16[72,896]{1,0:T(8,128)(2,1)S(1)} %get-tuple-element.38), channel_id=1, source_target_pairs={{0,6},{2,4},{4,2},{6,0},{8,14},{10,12},{12,10},{14,8},{1,7},{3,5},... | collective-permute-start | bytes 387080 | tf_op jit(solution)/shard_map/ppermute | solution.py:296
  49.4 0.9 %collective-permute-done.10 = bf16[72,896]{1,0:T(8,128)(2,1)S(1)} collective-permute-done((bf16[72,896]{1,0:T(8,128)(2,1)S(1)}, bf16[72,896]{1,0:T(8,128)(2,1)S(1)}, u32[]{:S(2)}, u32[]{:S(2)}) %collective-permute-start.10) | collective-permute-done | bytes 129056 | tf_op jit(solution)/shard_map/ppermute | solution.py:296
  50.3 0.1 add_convert_fusion.1
  50.4 1.9 %collective-permute-start.11 = (bf16[72,896]{1,0:T(8,128)(2,1)S(1)}, bf16[72,896]{1,0:T(8,128)(2,1)S(1)}, u32[]{:S(2)}, u32[]{:S(2)}) collective-permute-start(bf16[72,896]{1,0:T(8,128)(2,1)S(1)} %add_convert_fusion.1), channel_id=1, source_target_pairs={{0,16},{2,18},{4,20},{6,22},{8,24},{10,26},{12,28},{14,30},{16,0},... | collective-permute-start | bytes 387080 | tf_op jit(solution)/shard_map/ppermute | solution.py:311
  52.3 1.4 %collective-permute-done.21 = bf16[72,896]{1,0:T(8,128)(2,1)S(1)} collective-permute-done((bf16[72,896]{1,0:T(8,128)(2,1)S(1)}, bf16[72,896]{1,0:T(8,128)(2,1)S(1)}, u32[]{:S(2)}, u32[]{:S(2)}) %collective-permute-start.21) | collective-permute-done | bytes 129056 | tf_op jit(solution)/shard_map/ppermute | solution.py:296
  53.7 0.1 collective-permute-done.22
  53.8 1.5 %collective-permute-done.23 = bf16[72,896]{1,0:T(8,128)(2,1)S(1)} collective-permute-done((bf16[72,896]{1,0:T(8,128)(2,1)S(1)}, bf16[72,896]{1,0:T(8,128)(2,1)S(1)}, u32[]{:S(2)}, u32[]{:S(2)}) %collective-permute-start.23) | collective-permute-done | bytes 129056 | tf_op jit(solution)/shard_map/ppermute | solution.py:296
  55.3 0.1 add_convert_fusion
  55.4 4.2 %collective-permute-start.24 = (bf16[72,896]{1,0:T(8,128)(2,1)S(1)}, bf16[72,896]{1,0:T(8,128)(2,1)S(1)}, u32[]{:S(2)}, u32[]{:S(2)}) collective-permute-start(bf16[72,896]{1,0:T(8,128)(2,1)S(1)} %add_convert_fusion), channel_id=1, source_target_pairs={{0,24},{2,26},{4,28},{6,30},{8,16},{10,18},{12,20},{14,22},{16,8},... | collective-permute-start | bytes 387080 | tf_op jit(solution)/shard_map/ppermute | solution.py:311
  59.6 4.3 %shard_map.109 = (bf16[1792,256]{1,0:T(8,128)(2,1)}, bf16[1792,256]{1,0:T(8,128)(2,1)}, bf16[1792,256]{1,0:T(8,128)(2,1)}) custom-call(bf16[288,1792]{1,0:T(8,128)(2,1)S(1)} %get-tuple-element.39.refs_0_, bf16[288,1792]{1,0:T(8,128)(2,1)S(1)} %get-tuple-element.40.refs_1_, bf16[288,768]{1,0:T(8,128)(2,1)S(1)} %get-tuple-element.41.refs_2_, ...), custom_call_target="tpu_custom_call" | custom-call | flops 1585446912 | bytes 4816896 | tf_op jit(solution)/shard_map/pallas_call | solution.py:246
  63.9 0.0 collective-permute-done.routes_ref
  63.9 0.0 collective-permute-done.11.refs_0_
  63.9 1.2 %collective-permute-done.24.refs_1_ = bf16[72,896]{1,0:T(8,128)(2,1)S(1)} collective-permute-done((bf16[72,896]{1,0:T(8,128)(2,1)S(1)}, bf16[72,896]{1,0:T(8,128)(2,1)S(1)}, u32[]{:S(2)}, u32[]{:S(2)}) %collective-permute-start.24) | collective-permute-done | bytes 129056 | tf_op jit(solution)/shard_map/ppermute | solution.py:311
  65.1 1.1 %shard_map.108 = bf16[64,1792]{1,0:T(8,128)(2,1)} custom-call(s32[1,64]{1,0:T(1,128)S(1)} %collective-permute-done.routes_ref, bf16[72,896]{1,0:T(8,128)(2,1)S(1)} %collective-permute-done.11.refs_0_, bf16[72,896]{1,0:T(8,128)(2,1)S(1)} %collective-permute-done.24.refs_1_), custom_call_target="tpu_custom_call" | custom-call | flops 66060288 | bytes 745472 | tf_op jit(solution)/shard_map/pallas_call | solution.py:273
  (12 shorter events, 0.0 us)
Async XLA Ops:
  0.6 0.9 %copy-start.3 = (bf16[1,64,1792]{2,1,0:T(8,128)(2,1)S(1)}, bf16[1,64,1792]{2,1,0:T(8,128)(2,1)}, u32[]{:S(2)}) copy-start(bf16[1,64,1792]{2,1,0:T(8,128)(2,1)} %param.7) | copy-start | bytes 688132
  1.6 0.9 %copy-start.4 = (bf16[1,64,1792]{2,1,0:T(8,128)(2,1)S(1)}, bf16[1,64,1792]{2,1,0:T(8,128)(2,1)}, u32[]{:S(2)}) copy-start(bf16[1,64,1792]{2,1,0:T(8,128)(2,1)} %param.10) | copy-start | bytes 688132
  2.5 0.7 copy-start.5
  3.2 0.7 copy-start.6
  5.0 14.1 %collective-permute-start.12 = (bf16[72,896]{1,0:T(8,128)(2,1)S(1)}, bf16[72,896]{1,0:T(8,128)(2,1)S(1)}, u32[]{:S(2)}, u32[]{:S(2)}) collective-permute-start(bf16[72,896]{1,0:T(8,128)(2,1)S(1)} %get-tuple-element.32), channel_id=1, source_target_pairs={{0,8},{2,10},{4,12},{6,14},{8,0},{10,2},{12,4},{14,6},{1,9},{3,11}... | collective-permute-start | bytes 387080 | tf_op jit(solution)/shard_map/ppermute | solution.py:300
  9.2 11.8 %collective-permute-start.13 = (bf16[72,896]{1,0:T(8,128)(2,1)S(1)}, bf16[72,896]{1,0:T(8,128)(2,1)S(1)}, u32[]{:S(2)}, u32[]{:S(2)}) collective-permute-start(bf16[72,896]{1,0:T(8,128)(2,1)S(1)} %get-tuple-element.33), channel_id=1, source_target_pairs={{0,8},{2,10},{4,12},{6,14},{8,0},{10,2},{12,4},{14,6},{1,9},{3,11}... | collective-permute-start | bytes 387080 | tf_op jit(solution)/shard_map/ppermute | solution.py:300
  9.2 12.4 %collective-permute-start.3 = (bf16[72,896]{1,0:T(8,128)(2,1)S(1)}, bf16[72,896]{1,0:T(8,128)(2,1)S(1)}, u32[]{:S(2)}, u32[]{:S(2)}) collective-permute-start(bf16[72,896]{1,0:T(8,128)(2,1)S(1)} %get-tuple-element.25.refs_0_), channel_id=1, source_target_pairs={{0,4},{2,6},{4,0},{6,2},{8,12},{10,14},{12,8},{14,10},{1,5},{3,7},... | collective-permute-start | bytes 387080 | tf_op jit(solution)/shard_map/ppermute | solution.py:296
  11.1 12.1 %collective-permute-start.1 = (bf16[72,896]{1,0:T(8,128)(2,1)S(1)}, bf16[72,896]{1,0:T(8,128)(2,1)S(1)}, u32[]{:S(2)}, u32[]{:S(2)}) collective-permute-start(bf16[72,896]{1,0:T(8,128)(2,1)S(1)} %get-tuple-element.25.refs_0_), channel_id=1, source_target_pairs={{0,2},{2,0},{4,6},{6,4},{8,10},{10,8},{12,14},{14,12},{1,3},{3,1},... | collective-permute-start | bytes 387080 | tf_op jit(solution)/shard_map/ppermute | solution.py:296
  12.6 11.1 %collective-permute-start.4 = (bf16[72,896]{1,0:T(8,128)(2,1)S(1)}, bf16[72,896]{1,0:T(8,128)(2,1)S(1)}, u32[]{:S(2)}, u32[]{:S(2)}) collective-permute-start(bf16[72,896]{1,0:T(8,128)(2,1)S(1)} %get-tuple-element.26.refs_1_), channel_id=1, source_target_pairs={{0,4},{2,6},{4,0},{6,2},{8,12},{10,14},{12,8},{14,10},{1,5},{3,7},... | collective-permute-start | bytes 387080 | tf_op jit(solution)/shard_map/ppermute | solution.py:296
  19.1 9.9 %collective-permute-start.2 = (bf16[72,896]{1,0:T(8,128)(2,1)S(1)}, bf16[72,896]{1,0:T(8,128)(2,1)S(1)}, u32[]{:S(2)}, u32[]{:S(2)}) collective-permute-start(bf16[72,896]{1,0:T(8,128)(2,1)S(1)} %get-tuple-element.26.refs_1_), channel_id=1, source_target_pairs={{0,2},{2,0},{4,6},{6,4},{8,10},{10,8},{12,14},{14,12},{1,3},{3,1},... | collective-permute-start | bytes 387080 | tf_op jit(solution)/shard_map/ppermute | solution.py:296
  21.0 8.6 %collective-permute-start.16 = (bf16[72,896]{1,0:T(8,128)(2,1)S(1)}, bf16[72,896]{1,0:T(8,128)(2,1)S(1)}, u32[]{:S(2)}, u32[]{:S(2)}) collective-permute-start(bf16[72,896]{1,0:T(8,128)(2,1)S(1)} %collective-permute-done.12.refs_0_), channel_id=1, source_target_pairs={{0,4},{2,6},{4,0},{6,2},{8,12},{10,14},{12,8},{14,10},{1,5},{3,7},... | collective-permute-start | bytes 387080 | tf_op jit(solution)/shard_map/ppermute | solution.py:296
  21.7 9.3 %collective-permute-start.15 = (bf16[72,896]{1,0:T(8,128)(2,1)S(1)}, bf16[72,896]{1,0:T(8,128)(2,1)S(1)}, u32[]{:S(2)}, u32[]{:S(2)}) collective-permute-start(bf16[72,896]{1,0:T(8,128)(2,1)S(1)} %collective-permute-done.13.refs_1_), channel_id=1, source_target_pairs={{0,2},{2,0},{4,6},{6,4},{8,10},{10,8},{12,14},{14,12},{1,3},{3,1},... | collective-permute-start | bytes 387080 | tf_op jit(solution)/shard_map/ppermute | solution.py:296
  23.2 9.3 %collective-permute-start.5 = (bf16[72,896]{1,0:T(8,128)(2,1)S(1)}, bf16[72,896]{1,0:T(8,128)(2,1)S(1)}, u32[]{:S(2)}, u32[]{:S(2)}) collective-permute-start(bf16[72,896]{1,0:T(8,128)(2,1)S(1)} %collective-permute-done.3.refs_4_), channel_id=1, source_target_pairs={{0,2},{2,0},{4,6},{6,4},{8,10},{10,8},{12,14},{14,12},{1,3},{3,1},... | collective-permute-start | bytes 387080 | tf_op jit(solution)/shard_map/ppermute | solution.py:296
  23.7 9.8 %collective-permute-start.6 = (bf16[72,896]{1,0:T(8,128)(2,1)S(1)}, bf16[72,896]{1,0:T(8,128)(2,1)S(1)}, u32[]{:S(2)}, u32[]{:S(2)}) collective-permute-start(bf16[72,896]{1,0:T(8,128)(2,1)S(1)} %collective-permute-done.4.refs_5_), channel_id=1, source_target_pairs={{0,2},{2,0},{4,6},{6,4},{8,10},{10,8},{12,14},{14,12},{1,3},{3,1},... | collective-permute-start | bytes 387080 | tf_op jit(solution)/shard_map/ppermute | solution.py:296
  25.2 1.2 %copy-start = (bf16[1,1792,256]{2,1,0:T(8,128)(2,1)S(1)}, bf16[1,1792,256]{2,1,0:T(8,128)(2,1)}, u32[]{:S(2)}) copy-start(bf16[1,1792,256]{2,1,0:T(8,128)(2,1)} %param.11) | copy-start | bytes 2752516
  26.4 1.2 %copy-start.1 = (bf16[1,1792,256]{2,1,0:T(8,128)(2,1)S(1)}, bf16[1,1792,256]{2,1,0:T(8,128)(2,1)}, u32[]{:S(2)}) copy-start(bf16[1,1792,256]{2,1,0:T(8,128)(2,1)} %param.12) | copy-start | bytes 2752516
  27.6 1.2 %copy-start.2 = (bf16[1,1792,256]{2,1,0:T(8,128)(2,1)S(1)}, bf16[1,1792,256]{2,1,0:T(8,128)(2,1)}, u32[]{:S(2)}) copy-start(bf16[1,1792,256]{2,1,0:T(8,128)(2,1)} %param.13) | copy-start | bytes 2752516
  29.0 7.3 %collective-permute-start.14 = (bf16[72,896]{1,0:T(8,128)(2,1)S(1)}, bf16[72,896]{1,0:T(8,128)(2,1)S(1)}, u32[]{:S(2)}, u32[]{:S(2)}) collective-permute-start(bf16[72,896]{1,0:T(8,128)(2,1)S(1)} %collective-permute-done.12.refs_0_), channel_id=1, source_target_pairs={{0,2},{2,0},{4,6},{6,4},{8,10},{10,8},{12,14},{14,12},{1,3},{3,1},... | collective-permute-start | bytes 387080 | tf_op jit(solution)/shard_map/ppermute | solution.py:296
  29.6 6.7 %collective-permute-start.17 = (bf16[72,896]{1,0:T(8,128)(2,1)S(1)}, bf16[72,896]{1,0:T(8,128)(2,1)S(1)}, u32[]{:S(2)}, u32[]{:S(2)}) collective-permute-start(bf16[72,896]{1,0:T(8,128)(2,1)S(1)} %collective-permute-done.13.refs_1_), channel_id=1, source_target_pairs={{0,4},{2,6},{4,0},{6,2},{8,12},{10,14},{12,8},{14,10},{1,5},{3,7},... | collective-permute-start | bytes 387080 | tf_op jit(solution)/shard_map/ppermute | solution.py:296
  30.9 6.9 %collective-permute-start.18 = (bf16[72,896]{1,0:T(8,128)(2,1)S(1)}, bf16[72,896]{1,0:T(8,128)(2,1)S(1)}, u32[]{:S(2)}, u32[]{:S(2)}) collective-permute-start(bf16[72,896]{1,0:T(8,128)(2,1)S(1)} %collective-permute-done.16.refs_4_), channel_id=1, source_target_pairs={{0,2},{2,0},{4,6},{6,4},{8,10},{10,8},{12,14},{14,12},{1,3},{3,1},... | collective-permute-start | bytes 387080 | tf_op jit(solution)/shard_map/ppermute | solution.py:296
  32.5 5.4 %collective-permute-start.19 = (bf16[72,896]{1,0:T(8,128)(2,1)S(1)}, bf16[72,896]{1,0:T(8,128)(2,1)S(1)}, u32[]{:S(2)}, u32[]{:S(2)}) collective-permute-start(bf16[72,896]{1,0:T(8,128)(2,1)S(1)} %collective-permute-done.15.refs_3_), channel_id=1, source_target_pairs={{0,4},{2,6},{4,0},{6,2},{8,12},{10,14},{12,8},{14,10},{1,5},{3,7},... | collective-permute-start | bytes 387080 | tf_op jit(solution)/shard_map/ppermute | solution.py:296
  34.5 4.4 %collective-permute-start.7 = (f32[4,40,768]{2,1,0:T(8,128)S(1)}, f32[4,40,768]{2,1,0:T(8,128)S(1)}, u32[]{:S(2)}, u32[]{:S(2)}) collective-permute-start(f32[4,40,768]{2,1,0:T(8,128)S(1)} %get-tuple-element.27.refs_0_), channel_id=1, source_target_pairs={{0,1},{1,0},{2,3},{3,2},{4,5},{5,4},{6,7},{7,6},{8,9},{9,8},{10,11... | collective-permute-start | bytes 1474568 | tf_op jit(solution)/shard_map/ppermute | solution.py:336
  38.9 4.4 %copy-start.7 = (s32[1,64,1]{1,2,0:T(1,128)S(1)}, s32[1,64,1]{1,2,0:T(1,128)}, u32[]{:S(2)}) copy-start(s32[1,64,1]{1,2,0:T(1,128)} %param.8) | copy-start | bytes 772
  38.9 6.2 %collective-permute-start.20 = (f32[4,40,768]{2,1,0:T(8,128)S(1)}, f32[4,40,768]{2,1,0:T(8,128)S(1)}, u32[]{:S(2)}, u32[]{:S(2)}) collective-permute-start(f32[4,40,768]{2,1,0:T(8,128)S(1)} %get-tuple-element.34.refs_0_), channel_id=1, source_target_pairs={{0,1},{1,0},{2,3},{3,2},{4,5},{5,4},{6,7},{7,6},{8,9},{9,8},{10,11... | collective-permute-start | bytes 1474568 | tf_op jit(solution)/shard_map/ppermute | solution.py:336
  39.7 7.7 %collective-permute-start.8 = (bf16[72,896]{1,0:T(8,128)(2,1)S(1)}, bf16[72,896]{1,0:T(8,128)(2,1)S(1)}, u32[]{:S(2)}, u32[]{:S(2)}) collective-permute-start(bf16[72,896]{1,0:T(8,128)(2,1)S(1)} %get-tuple-element.29), channel_id=1, source_target_pairs={{0,2},{2,0},{4,6},{6,4},{8,10},{10,8},{12,14},{14,12},{1,3},{3,1},... | collective-permute-start | bytes 387080 | tf_op jit(solution)/shard_map/ppermute | solution.py:296
  41.6 6.3 %collective-permute-start.9 = (bf16[72,896]{1,0:T(8,128)(2,1)S(1)}, bf16[72,896]{1,0:T(8,128)(2,1)S(1)}, u32[]{:S(2)}, u32[]{:S(2)}) collective-permute-start(bf16[72,896]{1,0:T(8,128)(2,1)S(1)} %get-tuple-element.30), channel_id=1, source_target_pairs={{0,4},{2,6},{4,0},{6,2},{8,12},{10,14},{12,8},{14,10},{1,5},{3,7},... | collective-permute-start | bytes 387080 | tf_op jit(solution)/shard_map/ppermute | solution.py:296
  41.6 8.7 %collective-permute-start.10 = (bf16[72,896]{1,0:T(8,128)(2,1)S(1)}, bf16[72,896]{1,0:T(8,128)(2,1)S(1)}, u32[]{:S(2)}, u32[]{:S(2)}) collective-permute-start(bf16[72,896]{1,0:T(8,128)(2,1)S(1)} %get-tuple-element.31), channel_id=1, source_target_pairs={{0,6},{2,4},{4,2},{6,0},{8,14},{10,12},{12,10},{14,8},{1,7},{3,5},... | collective-permute-start | bytes 387080 | tf_op jit(solution)/shard_map/ppermute | solution.py:296
  43.3 20.6 %collective-permute-start = (s32[1,64]{1,0:T(1,128)S(1)}, s32[1,64]{1,0:T(1,128)S(1)}, u32[]{:S(2)}, u32[]{:S(2)}) collective-permute-start(s32[1,64]{1,0:T(1,128)S(1)} %bitcast.18), channel_id=1, source_target_pairs={{0,16},{16,0},{1,17},{17,1},{2,18},{18,2},{3,19},{19,3},{4,20},{20... | collective-permute-start | bytes 776 | tf_op jit(solution)/shard_map/ppermute | solution.py:313
  45.8 7.9 %collective-permute-start.21 = (bf16[72,896]{1,0:T(8,128)(2,1)S(1)}, bf16[72,896]{1,0:T(8,128)(2,1)S(1)}, u32[]{:S(2)}, u32[]{:S(2)}) collective-permute-start(bf16[72,896]{1,0:T(8,128)(2,1)S(1)} %get-tuple-element.36), channel_id=1, source_target_pairs={{0,2},{2,0},{4,6},{6,4},{8,10},{10,8},{12,14},{14,12},{1,3},{3,1},... | collective-permute-start | bytes 387080 | tf_op jit(solution)/shard_map/ppermute | solution.py:296
  47.4 6.3 %collective-permute-start.22 = (bf16[72,896]{1,0:T(8,128)(2,1)S(1)}, bf16[72,896]{1,0:T(8,128)(2,1)S(1)}, u32[]{:S(2)}, u32[]{:S(2)}) collective-permute-start(bf16[72,896]{1,0:T(8,128)(2,1)S(1)} %get-tuple-element.37), channel_id=1, source_target_pairs={{0,4},{2,6},{4,0},{6,2},{8,12},{10,14},{12,8},{14,10},{1,5},{3,7},... | collective-permute-start | bytes 387080 | tf_op jit(solution)/shard_map/ppermute | solution.py:296
  48.0 7.3 %collective-permute-start.23 = (bf16[72,896]{1,0:T(8,128)(2,1)S(1)}, bf16[72,896]{1,0:T(8,128)(2,1)S(1)}, u32[]{:S(2)}, u32[]{:S(2)}) collective-permute-start(bf16[72,896]{1,0:T(8,128)(2,1)S(1)} %get-tuple-element.38), channel_id=1, source_target_pairs={{0,6},{2,4},{4,2},{6,0},{8,14},{10,12},{12,10},{14,8},{1,7},{3,5},... | collective-permute-start | bytes 387080 | tf_op jit(solution)/shard_map/ppermute | solution.py:296
  50.4 13.5 %collective-permute-start.11 = (bf16[72,896]{1,0:T(8,128)(2,1)S(1)}, bf16[72,896]{1,0:T(8,128)(2,1)S(1)}, u32[]{:S(2)}, u32[]{:S(2)}) collective-permute-start(bf16[72,896]{1,0:T(8,128)(2,1)S(1)} %add_convert_fusion.1), channel_id=1, source_target_pairs={{0,16},{2,18},{4,20},{6,22},{8,24},{10,26},{12,28},{14,30},{16,0},... | collective-permute-start | bytes 387080 | tf_op jit(solution)/shard_map/ppermute | solution.py:311
  55.4 9.8 %collective-permute-start.24 = (bf16[72,896]{1,0:T(8,128)(2,1)S(1)}, bf16[72,896]{1,0:T(8,128)(2,1)S(1)}, u32[]{:S(2)}, u32[]{:S(2)}) collective-permute-start(bf16[72,896]{1,0:T(8,128)(2,1)S(1)} %add_convert_fusion), channel_id=1, source_target_pairs={{0,24},{2,26},{4,28},{6,30},{8,16},{10,18},{12,20},{14,22},{16,8},... | collective-permute-start | bytes 387080 | tf_op jit(solution)/shard_map/ppermute | solution.py:311

commit v3 on v2

--- a/solution.py
+++ b/solution.py
@@ -6,6 +6,7 @@
 from jax.experimental import pallas as pl
 from jax.experimental.pallas import tpu as pltpu
 from jax.sharding import PartitionSpec as P
+
 
 SHARES = 4
 F32 = jnp.float32
@@ -27,6 +28,10 @@
         compiler_params=pltpu.CompilerParams(vmem_limit_bytes=VMEM_BYTES),
         cost_estimate=pl.CostEstimate(flops=flops, bytes_accessed=n_bytes, transcendentals=0),
     )(body)
+
+
+def in_hbm(value):
+    return pltpu.with_memory_space_constraint(value, pltpu.HBM)
 
 
 def dot(left, right, left_dim=1, right_dim=0):
@@ -57,24 +62,31 @@
     return relative, slot_rows
 
 
-def dispatch_blocks(routes, weights, grad_rows, inputs, n_experts, capacity, split):
+def dispatch_blocks(routes, weights, grad_rows, inputs, cuts, capacity):
+    n_experts = len(cuts)
     chosen, n_tokens = routes.shape
     columns = inputs.shape[1]
     rows = round_up(2 * capacity, 8)
     order = list(range(1, n_experts)) + [0]
 
-    def body(routes_ref, weights_ref, grads_hbm, inputs_hbm, *refs):
-        out_refs = refs[: 2 * n_experts]
-        grads_ref, inputs_ref, sems = refs[2 * n_experts :]
+    operands = (routes, weights, inputs, grad_rows)
+    first = [sum(len(one) for one in cuts[:which]) for which in range(n_experts)]
+    n_outs = first[-1] + len(cuts[-1])
+
+    def body(*refs):
+        out_refs = list(refs[len(operands) : len(operands) + n_outs])
+        *held, sems = refs[len(operands) + n_outs :]
+        routes_ref, weights_ref, inputs_ref, grads_ref = held
         copies = [
-            pltpu.make_async_copy(inputs_hbm, inputs_ref, sems.at[0]),
-            pltpu.make_async_copy(grads_hbm, grads_ref, sems.at[1]),
+            pltpu.make_async_copy(source, target, sems.at[i])
+            for i, (source, target) in enumerate(zip(refs, held))
         ]
         for copy in copies:
             copy.start()
+        copies[0].wait()
         relative, slot_rows = slots(routes_ref[...], n_experts)
         row = lax.broadcasted_iota(jnp.int32, (rows, n_tokens), 0)
-        for copy in copies:
+        for copy in copies[1:]:
             copy.wait()
         for which in order:
             pick_input = jnp.zeros((rows, n_tokens), F32)
@@ -89,29 +101,25 @@
             scale = jnp.sum(scale, axis=1, keepdims=True)
             pick_input = pick_input.astype(BF16)
             pick_grad = pick_grad.astype(BF16)
-            for part, (begin, end) in enumerate(((0, split), (split, columns))):
+            for part, (begin, end) in enumerate(cuts[which]):
                 block = dot(pick_input, inputs_ref[:, begin:end])
                 block = block + dot(pick_grad, grads_ref[:, begin:end]) * scale
-                out_refs[2 * which + part][...] = block.astype(BF16)
-
-    shapes = (
-        jax.ShapeDtypeStruct((rows, split), BF16),
-        jax.ShapeDtypeStruct((rows, columns - split), BF16),
-    )
-    in_vmem, in_hbm = pl.BlockSpec(memory_space=pltpu.VMEM), pl.BlockSpec(memory_space=pltpu.HBM)
+                out_refs[first[which] + part][...] = block.astype(BF16)
+
     outs = call(
         body,
-        shapes * n_experts,
+        tuple(
+            jax.ShapeDtypeStruct((rows, end - begin), BF16) for one in cuts for begin, end in one
+        ),
         2 * 2 * n_experts * rows * n_tokens * columns,
         2 * n_tokens * columns * 2 + n_experts * rows * columns * 2,
-        [
-            pltpu.VMEM((n_tokens, columns), BF16),
-            pltpu.VMEM((n_tokens, columns), BF16),
-            pltpu.SemaphoreType.DMA((2,)),
-        ],
-        [in_vmem, in_vmem, in_hbm, in_hbm],
-    )(routes, weights, grad_rows, inputs)
-    return [(outs[2 * which], outs[2 * which + 1]) for which in range(n_experts)]
+        [pltpu.VMEM(value.shape, value.dtype) for value in operands]
+        + [pltpu.SemaphoreType.DMA((len(operands),))],
+        [pl.BlockSpec(memory_space=pltpu.HBM)] * len(operands),
+    )(*(in_hbm(value) for value in operands))
+    return [
+        list(outs[first[which] : first[which] + len(cuts[which])]) for which in range(n_experts)
+    ]
 
 
 def stage_weights(gate_cols, up_cols, down_cols):
@@ -134,21 +142,22 @@
         6 * columns * width * 2,
         [pltpu.SemaphoreType.DMA((3,))],
         [pl.BlockSpec(memory_space=pltpu.HBM)] * 3,
-    )(gate_cols, up_cols, down_cols)
-
-
-def partial_products(blocks, staged, capacity, split):
+    )(*(in_hbm(value) for value in (gate_cols, up_cols, down_cols)))
+
+
+def partial_products(blocks, staged, cuts, capacity):
     rows = round_up(2 * capacity, 8)
     kept = round_up(capacity, 8)
     n_blocks = len(blocks)
     columns, width = staged.shape[0], staged.shape[1] // 3
 
     def body(*refs):
-        block_refs = refs[: 2 * n_blocks]
-        staged_ref, out_ref, packed_ref = refs[2 * n_blocks :]
+        block_refs = refs[: n_blocks * len(cuts)]
+        staged_ref, out_ref, packed_ref = refs[n_blocks * len(cuts) :]
         for i in range(n_blocks):
-            packed_ref[i * rows : (i + 1) * rows, :split] = block_refs[2 * i][...]
-            packed_ref[i * rows : (i + 1) * rows, split:] = block_refs[2 * i + 1][...]
+            for part, (begin, end) in enumerate(cuts):
+                ref = block_refs[i * len(cuts) + part]
+                packed_ref[i * rows : (i + 1) * rows, begin:end] = ref[...]
         packed = packed_ref[...]
         gate_up = dot(packed, staged_ref[:, : 2 * width])
         down = dot(packed, staged_ref[:, 2 * width :])
@@ -167,7 +176,7 @@
         ),
         2 * 3 * n_blocks * rows * columns * width,
         3 * columns * width * 2 + n_blocks * rows * columns * 4,
-    )(*[half for block in blocks for half in block], staged)
+    )(*[part for block in blocks for part in block], staged)
 
 
 def hidden_backward(partials, staged, capacity, split):
@@ -295,16 +304,18 @@
     def partner(value, step):
         return lax.ppermute(value, "expert", [(j, j ^ step) for j in range(n_groups)])
 
+    def across(j, which):
+        expert, share = j // SHARES, j % SHARES
+        return (expert + which) % n_experts * SHARES + (share ^ (2 if which else 0))
+
     def crossing(value, which):
-        move = SHARES * which
         return lax.ppermute(
-            value, "expert", [(j, (j + move) % n_groups) for j in range(n_groups)]
+            value, "expert", [(j, across(j, which)) for j in range(n_groups)]
         )
 
     def homeward(value, which):
-        move = SHARES * which
         pairs = [
-            (s * n_groups + j, (s - 1) % n_sections * n_groups + (j - move) % n_groups)
+            (s * n_groups + j, (s - 1) % n_sections * n_groups + across(j, -which))
             for s in range(n_sections)
             for j in range(n_groups)
         ]
@@ -313,30 +324,30 @@
     routes_next = lax.ppermute(
         routes, "section", [(s, (s - 1) % n_sections) for s in range(n_sections)]
     )
-    own = dispatch_blocks(routes, weights, grad_rows, inputs, n_experts, capacity, split)
+    halves = ((0, split), (split, columns))
+    cuts = [((0, columns),)] + [halves] * (n_experts - 1)
+    own = dispatch_blocks(routes, weights, grad_rows, inputs, cuts, capacity)
     staged = stage_weights(gate_cols, up_cols, down_cols)
     heads = [own[0]] + [
-        tuple(crossing(part, which) for part in own[which]) for which in range(1, n_experts)
+        [crossing(part, which) for part in own[which]]
+        for which in range(1, n_experts)
     ]
 
     packed, slopes, merged = [], [], []
     for which in range(n_experts):
-        lo, hi = heads[which]
-        lo_y, hi_y = partner(lo, 1), partner(hi, 1)
-        lo_z, hi_z = partner(lo, 2), partner(hi, 2)
-        if which == 0:
-            lo_d, hi_d = partner(lo_z, 1), partner(hi_z, 1)
-        else:
-            lo_d, hi_d = partner(lo_z, 1), partner(hi_y, 2)
-        blocks = ((lo, hi), (lo_y, hi_y), (lo_z, hi_z), (lo_d, hi_d))
-        part, rows_packed = partial_products(blocks, staged, capacity, split)
+        head = heads[which]
+        by_y = [partner(part, 1) for part in head]
+        by_z = [partner(part, 2) for part in head]
+        by_d = [partner(by_z[0], 1)]
+        if which:
+            by_d.append(partner(by_y[1], 2))
+        part, rows_packed = partial_products(
+            (head, by_y, by_z, by_d), staged, cuts[which], capacity
+        )
         parts = [part]
         for turn in range(1, n_replicas):
-            parts.append(
-                lax.ppermute(
-                    part, "replica", [(r, (r + turn) % n_replicas) for r in range(n_replicas)]
-                )
-            )
+            pairs = [(r, (r + turn) % n_replicas) for r in range(n_replicas)]
+            parts.append(lax.ppermute(part, "replica", pairs))
         backs, slope = hidden_backward(parts, staged, capacity, split)
         packed.append(rows_packed)
         slopes.append(slope)
@@ -360,6 +371,7 @@
         P("section", "replica", "expert"),
         P("section", "replica", "expert"),
     )
+
     return jax.shard_map(
         per_device,
         mesh=mesh,

time: 66.6 us -> 63.8 us (0.958)
  local copies, waits for them, and re-layouts: 6.72 us -> 0.01 us
  waiting for transfers between devices: 15.5 us -> 21 us
  starting transfers between devices: 32.8 us -> 29.4 us
  Pallas kernels: 10.3 us -> 12.3 us
    unnamed x16 -> x2, local copies, waits for them, and re-layouts: 6.72 us -> 0.01 us
    ppermute x18 -> x15, starting transfers between devices: 20.6 us -> 16.3 us  [partner(): lax.ppermute(value, 'expert', [(j, j ^ step) for j in range(n_groups)])]
    ppermute x18 -> x15, waiting for transfers between devices: 8.11 us -> 11.4 us  [partner(): lax.ppermute(value, 'expert', [(j, j ^ step) for j in range(n_groups)])]
    ppermute x4, starting transfers between devices: 4.35 us -> 6.18 us  [the longest x2 6.04 us: crossing(): lax.ppermute(value, 'expert', [(j, across(j, which)) for j in range(n_gro...]
    ppermute x4, waiting for transfers between devices: 6.12 us -> 7.71 us  [the longest x2 7.71 us: crossing(): lax.ppermute(value, 'expert', [(j, across(j, which)) for j in range(n_gro...]
    pallas_call x1, Pallas kernels: 0.21 us -> 1.76 us  [stage_weights(): call(body, jax.ShapeDtypeStruct((columns, 3 * width), BF16), 2 * columns...]
  transfers between devices with their start and end apart: 25 -> 22, of which waited for: 11 -> 9; matrix products, arithmetic and copies ran while one was open for 0% -> 0% of each run, Pallas kernels for 12% -> 15%
where the time goes in v3:
time: 63.8 us; the launch traced here: 63.6 us
  starting transfers between devices  29.4 us (46%)
  waiting for transfers between devices  21 us (33%)
  Pallas kernels  12.3 us (19%)
  between operations  0.74 us (1%)
    ppermute x15, starting transfers between devices, partner(): lax.ppermute(value, 'expert', [(j, j ^ step) for j in range(n_groups)])  16.3 us
    ppermute x15, waiting for transfers between devices, partner(): lax.ppermute(value, 'expert', [(j, j ^ step) for j in range(n_groups)])  11.4 us
    ppermute x2, waiting for transfers between devices, crossing(): lax.ppermute(value, 'expert', [(j, across(j, which)) for j in range(n_gro...  7.71 us
    ppermute x2, starting transfers between devices, crossing(): lax.ppermute(value, 'expert', [(j, across(j, which)) for j in range(n_gro...  6.04 us
    ppermute x2, starting transfers between devices, homeward(): return lax.ppermute(value, ('section', 'expert'), pairs)  5.64 us
    pallas_call x1, Pallas kernels, weight_grads(): call(body, tuple((jax.ShapeDtypeStruct((columns, width), BF16) for _ in r...  4.28 us
    pallas_call x2, Pallas kernels, partial_products(): call(body, (jax.ShapeDtypeStruct((n_blocks, kept, 3 * width), F32), jax.S...  1.98 us
    ppermute x2, waiting for transfers between devices, homeward(): return lax.ppermute(value, ('section', 'expert'), pairs)  1.84 us
  transfers between devices with their start and end apart: 22, of which 9 were waited for; matrix products, arithmetic and copies ran while one was open for 0% of the time, Pallas kernels for 15%

profile of v3, /device:TPU:0, one launch (start us, length us, event | category | flops | bytes accessed | tf_op | source)
XLA Modules:
  0.0 63.6 jit_solution(10226768413863232759)
XLA Ops:
  0.6 1.6 %shard_map.102 = (bf16[72,1792]{1,0:T(8,128)(2,1)S(1)}, bf16[72,896]{1,0:T(8,128)(2,1)S(1)}, bf16[72,896]{1,0:T(8,128)(2,1)S(1)}) custom-call(s32[1,64]{1,0:T(1,128)} %bitcast.18, f32[1,64]{1,0:T(1,128)} %bitcast.17, bf16[64,1792]{1,0:T(8,128)(2,1)} %bitcast.14, bf16[64,1792]{1,0:T(8,128)(2,1)} %bitcast.15), custom_call_target="tpu_custom_call" | custom-call | flops 66060288 | bytes 974848 | tf_op jit(solution)/shard_map/pallas_call | solution.py:109
  2.2 5.2 %collective-permute-start.9 = (bf16[72,896]{1,0:T(8,128)(2,1)S(1)}, bf16[72,896]{1,0:T(8,128)(2,1)S(1)}, u32[]{:S(2)}, u32[]{:S(2)}) collective-permute-start(bf16[72,896]{1,0:T(8,128)(2,1)S(1)} %get-tuple-element.30), channel_id=1, source_target_pairs={{0,12},{2,14},{4,8},{6,10},{8,4},{10,6},{12,0},{14,2},{1,13},{3,15... | collective-permute-start | bytes 387080 | tf_op jit(solution)/shard_map/ppermute | solution.py:312
  7.4 0.0 collective-permute-start.2
  7.4 0.9 %collective-permute-start.10 = (bf16[72,896]{1,0:T(8,128)(2,1)S(1)}, bf16[72,896]{1,0:T(8,128)(2,1)S(1)}, u32[]{:S(2)}, u32[]{:S(2)}) collective-permute-start(bf16[72,896]{1,0:T(8,128)(2,1)S(1)} %get-tuple-element.31), channel_id=1, source_target_pairs={{0,12},{2,14},{4,8},{6,10},{8,4},{10,6},{12,0},{14,2},{1,13},{3,15... | collective-permute-start | bytes 387080 | tf_op jit(solution)/shard_map/ppermute | solution.py:312
  8.3 3.5 %collective-permute-done.9.refs_0_ = bf16[72,896]{1,0:T(8,128)(2,1)S(1)} collective-permute-done((bf16[72,896]{1,0:T(8,128)(2,1)S(1)}, bf16[72,896]{1,0:T(8,128)(2,1)S(1)}, u32[]{:S(2)}, u32[]{:S(2)}) %collective-permute-start.9) | collective-permute-done | bytes 129056 | tf_op jit(solution)/shard_map/ppermute | solution.py:312
  11.7 2.5 %collective-permute-start.13 = (bf16[72,896]{1,0:T(8,128)(2,1)S(1)}, bf16[72,896]{1,0:T(8,128)(2,1)S(1)}, u32[]{:S(2)}, u32[]{:S(2)}) collective-permute-start(bf16[72,896]{1,0:T(8,128)(2,1)S(1)} %collective-permute-done.9.refs_0_), channel_id=1, source_target_pairs={{0,4},{2,6},{4,0},{6,2},{8,12},{10,14},{12,8},{14,10},{1,5},{3,7},... | collective-permute-start | bytes 387080 | tf_op jit(solution)/shard_map/ppermute | solution.py:305
  14.2 1.5 %collective-permute-start.11 = (bf16[72,896]{1,0:T(8,128)(2,1)S(1)}, bf16[72,896]{1,0:T(8,128)(2,1)S(1)}, u32[]{:S(2)}, u32[]{:S(2)}) collective-permute-start(bf16[72,896]{1,0:T(8,128)(2,1)S(1)} %collective-permute-done.9.refs_0_), channel_id=1, source_target_pairs={{0,2},{2,0},{4,6},{6,4},{8,10},{10,8},{12,14},{14,12},{1,3},{3,1},... | collective-permute-start | bytes 387080 | tf_op jit(solution)/shard_map/ppermute | solution.py:305
  15.8 4.2 %collective-permute-done.10.refs_1_ = bf16[72,896]{1,0:T(8,128)(2,1)S(1)} collective-permute-done((bf16[72,896]{1,0:T(8,128)(2,1)S(1)}, bf16[72,896]{1,0:T(8,128)(2,1)S(1)}, u32[]{:S(2)}, u32[]{:S(2)}) %collective-permute-start.10) | collective-permute-done | bytes 129056 | tf_op jit(solution)/shard_map/ppermute | solution.py:312
  20.0 1.7 %collective-permute-start.12 = (bf16[72,896]{1,0:T(8,128)(2,1)S(1)}, bf16[72,896]{1,0:T(8,128)(2,1)S(1)}, u32[]{:S(2)}, u32[]{:S(2)}) collective-permute-start(bf16[72,896]{1,0:T(8,128)(2,1)S(1)} %collective-permute-done.10.refs_1_), channel_id=1, source_target_pairs={{0,2},{2,0},{4,6},{6,4},{8,10},{10,8},{12,14},{14,12},{1,3},{3,1},... | collective-permute-start | bytes 387080 | tf_op jit(solution)/shard_map/ppermute | solution.py:305
  21.7 0.3 collective-permute-start.1
  22.0 0.0 collective-permute-done.13.refs_4_
  22.0 1.6 %collective-permute-start.14 = (bf16[72,896]{1,0:T(8,128)(2,1)S(1)}, bf16[72,896]{1,0:T(8,128)(2,1)S(1)}, u32[]{:S(2)}, u32[]{:S(2)}) collective-permute-start(bf16[72,896]{1,0:T(8,128)(2,1)S(1)} %collective-permute-done.10.refs_1_), channel_id=1, source_target_pairs={{0,4},{2,6},{4,0},{6,2},{8,12},{10,14},{12,8},{14,10},{1,5},{3,7},... | collective-permute-start | bytes 387080 | tf_op jit(solution)/shard_map/ppermute | solution.py:305
  23.7 0.0 collective-permute-done.11.refs_2_
  23.7 1.5 %collective-permute-start.15 = (bf16[72,896]{1,0:T(8,128)(2,1)S(1)}, bf16[72,896]{1,0:T(8,128)(2,1)S(1)}, u32[]{:S(2)}, u32[]{:S(2)}) collective-permute-start(bf16[72,896]{1,0:T(8,128)(2,1)S(1)} %collective-permute-done.13.refs_4_), channel_id=1, source_target_pairs={{0,2},{2,0},{4,6},{6,4},{8,10},{10,8},{12,14},{14,12},{1,3},{3,1},... | collective-permute-start | bytes 387080 | tf_op jit(solution)/shard_map/ppermute | solution.py:305
  25.2 0.0 collective-permute-done.2.refs_2_
  25.2 0.5 collective-permute-start.3
  25.7 0.6 collective-permute-done.12.refs_3_
  26.3 0.0 collective-permute-start.16
  26.3 1.8 %shard_map.103.refs_4_.refs_2_.refs_8_ = bf16[1792,768]{1,0:T(8,128)(2,1)S(1)} custom-call(bf16[1792,256]{1,0:T(8,128)(2,1)} %bitcast.11, bf16[1792,256]{1,0:T(8,128)(2,1)} %bitcast.12, bf16[1792,256]{1,0:T(8,128)(2,1)} %bitcast.13), custom_call_target="tpu_custom_call" | custom-call | flops 234881024 | bytes 5505024 | tf_op jit(solution)/shard_map/pallas_call | solution.py:138
  28.1 0.0 collective-permute-done.14.refs_5_
  28.1 6.5 %collective-permute-done.15.refs_6_ = bf16[72,896]{1,0:T(8,128)(2,1)S(1)} collective-permute-done((bf16[72,896]{1,0:T(8,128)(2,1)S(1)}, bf16[72,896]{1,0:T(8,128)(2,1)S(1)}, u32[]{:S(2)}, u32[]{:S(2)}) %collective-permute-start.15) | collective-permute-done | bytes 129056 | tf_op jit(solution)/shard_map/ppermute | solution.py:305
  34.6 0.0 collective-permute-done.16.refs_7_
  34.6 1.0 %shard_map.106 = (f32[4,40,768]{2,1,0:T(8,128)S(1)}, bf16[288,1792]{1,0:T(8,128)(2,1)S(1)}) custom-call(bf16[72,896]{1,0:T(8,128)(2,1)S(1)} %collective-permute-done.9.refs_0_, bf16[72,896]{1,0:T(8,128)(2,1)S(1)} %collective-permute-done.10.refs_1_, bf16[72,896]{1,0:T(8,128)(2,1)S(1)} %collective-permute-done.11.refs_2_, ...), custom_call_target="tpu_custom_call" | custom-call | flops 792723456 | bytes 4816896 | tf_op jit(solution)/shard_map/pallas_call | solution.py:171
  35.6 0.1 collective-permute-start.17
  35.7 0.0 collective-permute-done.1.refs_1_
  35.7 1.9 %collective-permute-done.3.refs_3_ = bf16[72,1792]{1,0:T(8,128)(2,1)S(1)} collective-permute-done((bf16[72,1792]{1,0:T(8,128)(2,1)S(1)}, bf16[72,1792]{1,0:T(8,128)(2,1)S(1)}, u32[]{:S(2)}, u32[]{:S(2)}) %collective-permute-start.3) | collective-permute-done | bytes 258080 | tf_op jit(solution)/shard_map/ppermute | solution.py:305
  37.6 1.0 %shard_map.104 = (f32[4,40,768]{2,1,0:T(8,128)S(1)}, bf16[288,1792]{1,0:T(8,128)(2,1)S(1)}) custom-call(bf16[72,1792]{1,0:T(8,128)(2,1)S(1)} %get-tuple-element.24.refs_0_, bf16[72,1792]{1,0:T(8,128)(2,1)S(1)} %collective-permute-done.1.refs_1_, bf16[72,1792]{1,0:T(8,128)(2,1)S(1)} %collective-permute-done.2.refs_2_, ...), custom_call_target="tpu_custom_call" | custom-call | flops 792723456 | bytes 4816896 | tf_op jit(solution)/shard_map/pallas_call | solution.py:171
  38.6 0.0 copy-start
  38.6 0.1 collective-permute-start.4
  38.7 0.0 collective-permute-done.17.refs_1_
  38.7 0.8 %shard_map.107 = (bf16[72,896]{1,0:T(8,128)(2,1)S(1)}, bf16[72,896]{1,0:T(8,128)(2,1)S(1)}, bf16[72,896]{1,0:T(8,128)(2,1)S(1)}, bf16[72,896]{1,0:T(8,128)(2,1)S(1)}, bf16[288,768]{1,0:T(8,128)(2,1)S(1)}) custom-call(f32[4,40,768]{2,1,0:T(8,128)S(1)} %get-tuple-element.32.refs_0_, f32[4,40,768]{2,1,0:T(8,128)S(1)} %collective-permute-done.17.refs_1_, ...), custom_call_target="tpu_custom_call" | custom-call | flops 293601280 | bytes 2408448 | tf_op jit(solution)/shard_map/pallas_call | solution.py:230
  39.5 1.4 %collective-permute-start.18 = (bf16[72,896]{1,0:T(8,128)(2,1)S(1)}, bf16[72,896]{1,0:T(8,128)(2,1)S(1)}, u32[]{:S(2)}, u32[]{:S(2)}) collective-permute-start(bf16[72,896]{1,0:T(8,128)(2,1)S(1)} %get-tuple-element.34), channel_id=1, source_target_pairs={{0,2},{2,0},{4,6},{6,4},{8,10},{10,8},{12,14},{14,12},{1,3},{3,1},... | collective-permute-start | bytes 387080 | tf_op jit(solution)/shard_map/ppermute | solution.py:305
  40.9 0.0 collective-permute-start.19
  40.9 2.1 %collective-permute-start.20 = (bf16[72,896]{1,0:T(8,128)(2,1)S(1)}, bf16[72,896]{1,0:T(8,128)(2,1)S(1)}, u32[]{:S(2)}, u32[]{:S(2)}) collective-permute-start(bf16[72,896]{1,0:T(8,128)(2,1)S(1)} %get-tuple-element.36), channel_id=1, source_target_pairs={{0,6},{2,4},{4,2},{6,0},{8,14},{10,12},{12,10},{14,8},{1,7},{3,5},... | collective-permute-start | bytes 387080 | tf_op jit(solution)/shard_map/ppermute | solution.py:305
  43.0 0.0 copy-done
  43.0 1.3 %collective-permute-start = (s32[1,64]{1,0:T(1,128)S(1)}, s32[1,64]{1,0:T(1,128)S(1)}, u32[]{:S(2)}, u32[]{:S(2)}) collective-permute-start(s32[1,64]{1,0:T(1,128)S(1)} %bitcast.19), channel_id=1, source_target_pairs={{0,16},{16,0},{1,17},{17,1},{2,18},{18,2},{3,19},{19,3},{4,20},{20... | collective-permute-start | bytes 776 | tf_op jit(solution)/shard_map/ppermute | solution.py:324
  44.3 0.0 collective-permute-done.4.refs_1_
  44.3 0.8 %shard_map.105 = (bf16[72,896]{1,0:T(8,128)(2,1)S(1)}, bf16[72,896]{1,0:T(8,128)(2,1)S(1)}, bf16[72,896]{1,0:T(8,128)(2,1)S(1)}, bf16[72,896]{1,0:T(8,128)(2,1)S(1)}, bf16[288,768]{1,0:T(8,128)(2,1)S(1)}) custom-call(f32[4,40,768]{2,1,0:T(8,128)S(1)} %get-tuple-element.25.refs_0_, f32[4,40,768]{2,1,0:T(8,128)S(1)} %collective-permute-done.4.refs_1_, ...), custom_call_target="tpu_custom_call" | custom-call | flops 293601280 | bytes 2408448 | tf_op jit(solution)/shard_map/pallas_call | solution.py:230
  45.1 1.6 %collective-permute-start.5 = (bf16[72,896]{1,0:T(8,128)(2,1)S(1)}, bf16[72,896]{1,0:T(8,128)(2,1)S(1)}, u32[]{:S(2)}, u32[]{:S(2)}) collective-permute-start(bf16[72,896]{1,0:T(8,128)(2,1)S(1)} %get-tuple-element.27), channel_id=1, source_target_pairs={{0,2},{2,0},{4,6},{6,4},{8,10},{10,8},{12,14},{14,12},{1,3},{3,1},... | collective-permute-start | bytes 387080 | tf_op jit(solution)/shard_map/ppermute | solution.py:305
  46.7 0.0 collective-permute-done.18
  46.7 0.0 collective-permute-start.6
  46.7 0.5 collective-permute-done.19
  47.2 1.5 %collective-permute-start.7 = (bf16[72,896]{1,0:T(8,128)(2,1)S(1)}, bf16[72,896]{1,0:T(8,128)(2,1)S(1)}, u32[]{:S(2)}, u32[]{:S(2)}) collective-permute-start(bf16[72,896]{1,0:T(8,128)(2,1)S(1)} %get-tuple-element.29), channel_id=1, source_target_pairs={{0,6},{2,4},{4,2},{6,0},{8,14},{10,12},{12,10},{14,8},{1,7},{3,5},... | collective-permute-start | bytes 387080 | tf_op jit(solution)/shard_map/ppermute | solution.py:305
  48.7 1.5 %collective-permute-done.20 = bf16[72,896]{1,0:T(8,128)(2,1)S(1)} collective-permute-done((bf16[72,896]{1,0:T(8,128)(2,1)S(1)}, bf16[72,896]{1,0:T(8,128)(2,1)S(1)}, u32[]{:S(2)}, u32[]{:S(2)}) %collective-permute-start.20) | collective-permute-done | bytes 129056 | tf_op jit(solution)/shard_map/ppermute | solution.py:305
  50.1 0.1 add_convert_fusion
  50.2 4.3 %collective-permute-start.21 = (bf16[72,896]{1,0:T(8,128)(2,1)S(1)}, bf16[72,896]{1,0:T(8,128)(2,1)S(1)}, u32[]{:S(2)}, u32[]{:S(2)}) collective-permute-start(bf16[72,896]{1,0:T(8,128)(2,1)S(1)} %add_convert_fusion), channel_id=1, source_target_pairs={{0,28},{2,30},{4,24},{6,26},{8,20},{10,22},{12,16},{14,18},{16,12}... | collective-permute-start | bytes 387080 | tf_op jit(solution)/shard_map/ppermute | solution.py:322
  54.5 0.0 collective-permute-done.5
  54.5 0.0 collective-permute-done.6
  54.5 0.4 collective-permute-done.7
  54.9 0.1 add_convert_fusion.1
  55.0 1.4 %collective-permute-start.8 = (bf16[72,896]{1,0:T(8,128)(2,1)S(1)}, bf16[72,896]{1,0:T(8,128)(2,1)S(1)}, u32[]{:S(2)}, u32[]{:S(2)}) collective-permute-start(bf16[72,896]{1,0:T(8,128)(2,1)S(1)} %add_convert_fusion.1), channel_id=1, source_target_pairs={{0,16},{2,18},{4,20},{6,22},{8,24},{10,26},{12,28},{14,30},{16,0},... | collective-permute-start | bytes 387080 | tf_op jit(solution)/shard_map/ppermute | solution.py:322
  56.3 4.3 %shard_map.109 = (bf16[1792,256]{1,0:T(8,128)(2,1)}, bf16[1792,256]{1,0:T(8,128)(2,1)}, bf16[1792,256]{1,0:T(8,128)(2,1)}) custom-call(bf16[288,1792]{1,0:T(8,128)(2,1)S(1)} %get-tuple-element.37.refs_0_, bf16[288,1792]{1,0:T(8,128)(2,1)S(1)} %get-tuple-element.38.refs_1_, bf16[288,768]{1,0:T(8,128)(2,1)S(1)} %get-tuple-element.39.refs_2_, ...), custom_call_target="tpu_custom_call" | custom-call | flops 1585446912 | bytes 4816896 | tf_op jit(solution)/shard_map/pallas_call | solution.py:255
  60.6 0.0 collective-permute-done.routes_ref
  60.6 0.0 collective-permute-done.21.refs_1_
  60.6 1.8 %collective-permute-done.8.refs_0_ = bf16[72,896]{1,0:T(8,128)(2,1)S(1)} collective-permute-done((bf16[72,896]{1,0:T(8,128)(2,1)S(1)}, bf16[72,896]{1,0:T(8,128)(2,1)S(1)}, u32[]{:S(2)}, u32[]{:S(2)}) %collective-permute-start.8) | collective-permute-done | bytes 129056 | tf_op jit(solution)/shard_map/ppermute | solution.py:322
  62.5 1.1 %shard_map.108 = bf16[64,1792]{1,0:T(8,128)(2,1)} custom-call(s32[1,64]{1,0:T(1,128)S(1)} %collective-permute-done.routes_ref, bf16[72,896]{1,0:T(8,128)(2,1)S(1)} %collective-permute-done.8.refs_0_, bf16[72,896]{1,0:T(8,128)(2,1)S(1)} %collective-permute-done.21.refs_1_), custom_call_target="tpu_custom_call" | custom-call | flops 66060288 | bytes 745472 | tf_op jit(solution)/shard_map/pallas_call | solution.py:282
Async XLA Ops:
  2.2 9.5 %collective-permute-start.9 = (bf16[72,896]{1,0:T(8,128)(2,1)S(1)}, bf16[72,896]{1,0:T(8,128)(2,1)S(1)}, u32[]{:S(2)}, u32[]{:S(2)}) collective-permute-start(bf16[72,896]{1,0:T(8,128)(2,1)S(1)} %get-tuple-element.30), channel_id=1, source_target_pairs={{0,12},{2,14},{4,8},{6,10},{8,4},{10,6},{12,0},{14,2},{1,13},{3,15... | collective-permute-start | bytes 387080 | tf_op jit(solution)/shard_map/ppermute | solution.py:312
  7.4 17.8 %collective-permute-start.2 = (bf16[72,1792]{1,0:T(8,128)(2,1)S(1)}, bf16[72,1792]{1,0:T(8,128)(2,1)S(1)}, u32[]{:S(2)}, u32[]{:S(2)}) collective-permute-start(bf16[72,1792]{1,0:T(8,128)(2,1)S(1)} %get-tuple-element.24.refs_0_), channel_id=1, source_target_pairs={{0,4},{2,6},{4,0},{6,2},{8,12},{10,14},{12,8},{14,10},{1,5},{3,7},... | collective-permute-start | bytes 774152 | tf_op jit(solution)/shard_map/ppermute | solution.py:305
  7.4 12.6 %collective-permute-start.10 = (bf16[72,896]{1,0:T(8,128)(2,1)S(1)}, bf16[72,896]{1,0:T(8,128)(2,1)S(1)}, u32[]{:S(2)}, u32[]{:S(2)}) collective-permute-start(bf16[72,896]{1,0:T(8,128)(2,1)S(1)} %get-tuple-element.31), channel_id=1, source_target_pairs={{0,12},{2,14},{4,8},{6,10},{8,4},{10,6},{12,0},{14,2},{1,13},{3,15... | collective-permute-start | bytes 387080 | tf_op jit(solution)/shard_map/ppermute | solution.py:312
  11.7 10.3 %collective-permute-start.13 = (bf16[72,896]{1,0:T(8,128)(2,1)S(1)}, bf16[72,896]{1,0:T(8,128)(2,1)S(1)}, u32[]{:S(2)}, u32[]{:S(2)}) collective-permute-start(bf16[72,896]{1,0:T(8,128)(2,1)S(1)} %collective-permute-done.9.refs_0_), channel_id=1, source_target_pairs={{0,4},{2,6},{4,0},{6,2},{8,12},{10,14},{12,8},{14,10},{1,5},{3,7},... | collective-permute-start | bytes 387080 | tf_op jit(solution)/shard_map/ppermute | solution.py:305
  14.2 9.4 %collective-permute-start.11 = (bf16[72,896]{1,0:T(8,128)(2,1)S(1)}, bf16[72,896]{1,0:T(8,128)(2,1)S(1)}, u32[]{:S(2)}, u32[]{:S(2)}) collective-permute-start(bf16[72,896]{1,0:T(8,128)(2,1)S(1)} %collective-permute-done.9.refs_0_), channel_id=1, source_target_pairs={{0,2},{2,0},{4,6},{6,4},{8,10},{10,8},{12,14},{14,12},{1,3},{3,1},... | collective-permute-start | bytes 387080 | tf_op jit(solution)/shard_map/ppermute | solution.py:305
  20.0 6.3 %collective-permute-start.12 = (bf16[72,896]{1,0:T(8,128)(2,1)S(1)}, bf16[72,896]{1,0:T(8,128)(2,1)S(1)}, u32[]{:S(2)}, u32[]{:S(2)}) collective-permute-start(bf16[72,896]{1,0:T(8,128)(2,1)S(1)} %collective-permute-done.10.refs_1_), channel_id=1, source_target_pairs={{0,2},{2,0},{4,6},{6,4},{8,10},{10,8},{12,14},{14,12},{1,3},{3,1},... | collective-permute-start | bytes 387080 | tf_op jit(solution)/shard_map/ppermute | solution.py:305
  21.7 14.0 %collective-permute-start.1 = (bf16[72,1792]{1,0:T(8,128)(2,1)S(1)}, bf16[72,1792]{1,0:T(8,128)(2,1)S(1)}, u32[]{:S(2)}, u32[]{:S(2)}) collective-permute-start(bf16[72,1792]{1,0:T(8,128)(2,1)S(1)} %get-tuple-element.24.refs_0_), channel_id=1, source_target_pairs={{0,2},{2,0},{4,6},{6,4},{8,10},{10,8},{12,14},{14,12},{1,3},{3,1},... | collective-permute-start | bytes 774152 | tf_op jit(solution)/shard_map/ppermute | solution.py:305
  22.0 6.1 %collective-permute-start.14 = (bf16[72,896]{1,0:T(8,128)(2,1)S(1)}, bf16[72,896]{1,0:T(8,128)(2,1)S(1)}, u32[]{:S(2)}, u32[]{:S(2)}) collective-permute-start(bf16[72,896]{1,0:T(8,128)(2,1)S(1)} %collective-permute-done.10.refs_1_), channel_id=1, source_target_pairs={{0,4},{2,6},{4,0},{6,2},{8,12},{10,14},{12,8},{14,10},{1,5},{3,7},... | collective-permute-start | bytes 387080 | tf_op jit(solution)/shard_map/ppermute | solution.py:305
  23.7 11.0 %collective-permute-start.15 = (bf16[72,896]{1,0:T(8,128)(2,1)S(1)}, bf16[72,896]{1,0:T(8,128)(2,1)S(1)}, u32[]{:S(2)}, u32[]{:S(2)}) collective-permute-start(bf16[72,896]{1,0:T(8,128)(2,1)S(1)} %collective-permute-done.13.refs_4_), channel_id=1, source_target_pairs={{0,2},{2,0},{4,6},{6,4},{8,10},{10,8},{12,14},{14,12},{1,3},{3,1},... | collective-permute-start | bytes 387080 | tf_op jit(solution)/shard_map/ppermute | solution.py:305
  25.2 12.4 %collective-permute-start.3 = (bf16[72,1792]{1,0:T(8,128)(2,1)S(1)}, bf16[72,1792]{1,0:T(8,128)(2,1)S(1)}, u32[]{:S(2)}, u32[]{:S(2)}) collective-permute-start(bf16[72,1792]{1,0:T(8,128)(2,1)S(1)} %collective-permute-done.2.refs_2_), channel_id=1, source_target_pairs={{0,2},{2,0},{4,6},{6,4},{8,10},{10,8},{12,14},{14,12},{1,3},{3,1},... | collective-permute-start | bytes 774152 | tf_op jit(solution)/shard_map/ppermute | solution.py:305
  26.3 8.3 %collective-permute-start.16 = (bf16[72,896]{1,0:T(8,128)(2,1)S(1)}, bf16[72,896]{1,0:T(8,128)(2,1)S(1)}, u32[]{:S(2)}, u32[]{:S(2)}) collective-permute-start(bf16[72,896]{1,0:T(8,128)(2,1)S(1)} %collective-permute-done.12.refs_3_), channel_id=1, source_target_pairs={{0,4},{2,6},{4,0},{6,2},{8,12},{10,14},{12,8},{14,10},{1,5},{3,7},... | collective-permute-start | bytes 387080 | tf_op jit(solution)/shard_map/ppermute | solution.py:305
  35.6 3.1 %collective-permute-start.17 = (f32[4,40,768]{2,1,0:T(8,128)S(1)}, f32[4,40,768]{2,1,0:T(8,128)S(1)}, u32[]{:S(2)}, u32[]{:S(2)}) collective-permute-start(f32[4,40,768]{2,1,0:T(8,128)S(1)} %get-tuple-element.32.refs_0_), channel_id=1, source_target_pairs={{0,1},{1,0},{2,3},{3,2},{4,5},{5,4},{6,7},{7,6},{8,9},{9,8},{10,11... | collective-permute-start | bytes 1474568 | tf_op jit(solution)/shard_map/ppermute | solution.py:350
  38.6 4.4 %copy-start = (s32[1,64,1]{1,2,0:T(1,128)S(1)}, s32[1,64,1]{1,2,0:T(1,128)}, u32[]{:S(2)}) copy-start(s32[1,64,1]{1,2,0:T(1,128)} %param.8) | copy-start | bytes 772
  38.6 5.7 %collective-permute-start.4 = (f32[4,40,768]{2,1,0:T(8,128)S(1)}, f32[4,40,768]{2,1,0:T(8,128)S(1)}, u32[]{:S(2)}, u32[]{:S(2)}) collective-permute-start(f32[4,40,768]{2,1,0:T(8,128)S(1)} %get-tuple-element.25.refs_0_), channel_id=1, source_target_pairs={{0,1},{1,0},{2,3},{3,2},{4,5},{5,4},{6,7},{7,6},{8,9},{9,8},{10,11... | collective-permute-start | bytes 1474568 | tf_op jit(solution)/shard_map/ppermute | solution.py:350
  39.5 7.2 %collective-permute-start.18 = (bf16[72,896]{1,0:T(8,128)(2,1)S(1)}, bf16[72,896]{1,0:T(8,128)(2,1)S(1)}, u32[]{:S(2)}, u32[]{:S(2)}) collective-permute-start(bf16[72,896]{1,0:T(8,128)(2,1)S(1)} %get-tuple-element.34), channel_id=1, source_target_pairs={{0,2},{2,0},{4,6},{6,4},{8,10},{10,8},{12,14},{14,12},{1,3},{3,1},... | collective-permute-start | bytes 387080 | tf_op jit(solution)/shard_map/ppermute | solution.py:305
  40.9 6.3 %collective-permute-start.19 = (bf16[72,896]{1,0:T(8,128)(2,1)S(1)}, bf16[72,896]{1,0:T(8,128)(2,1)S(1)}, u32[]{:S(2)}, u32[]{:S(2)}) collective-permute-start(bf16[72,896]{1,0:T(8,128)(2,1)S(1)} %get-tuple-element.35), channel_id=1, source_target_pairs={{0,4},{2,6},{4,0},{6,2},{8,12},{10,14},{12,8},{14,10},{1,5},{3,7},... | collective-permute-start | bytes 387080 | tf_op jit(solution)/shard_map/ppermute | solution.py:305
  40.9 9.2 %collective-permute-start.20 = (bf16[72,896]{1,0:T(8,128)(2,1)S(1)}, bf16[72,896]{1,0:T(8,128)(2,1)S(1)}, u32[]{:S(2)}, u32[]{:S(2)}) collective-permute-start(bf16[72,896]{1,0:T(8,128)(2,1)S(1)} %get-tuple-element.36), channel_id=1, source_target_pairs={{0,6},{2,4},{4,2},{6,0},{8,14},{10,12},{12,10},{14,8},{1,7},{3,5},... | collective-permute-start | bytes 387080 | tf_op jit(solution)/shard_map/ppermute | solution.py:305
  43.0 17.6 %collective-permute-start = (s32[1,64]{1,0:T(1,128)S(1)}, s32[1,64]{1,0:T(1,128)S(1)}, u32[]{:S(2)}, u32[]{:S(2)}) collective-permute-start(s32[1,64]{1,0:T(1,128)S(1)} %bitcast.19), channel_id=1, source_target_pairs={{0,16},{16,0},{1,17},{17,1},{2,18},{18,2},{3,19},{19,3},{4,20},{20... | collective-permute-start | bytes 776 | tf_op jit(solution)/shard_map/ppermute | solution.py:324
  45.1 9.4 %collective-permute-start.5 = (bf16[72,896]{1,0:T(8,128)(2,1)S(1)}, bf16[72,896]{1,0:T(8,128)(2,1)S(1)}, u32[]{:S(2)}, u32[]{:S(2)}) collective-permute-start(bf16[72,896]{1,0:T(8,128)(2,1)S(1)} %get-tuple-element.27), channel_id=1, source_target_pairs={{0,2},{2,0},{4,6},{6,4},{8,10},{10,8},{12,14},{14,12},{1,3},{3,1},... | collective-permute-start | bytes 387080 | tf_op jit(solution)/shard_map/ppermute | solution.py:305
  46.7 7.8 %collective-permute-start.6 = (bf16[72,896]{1,0:T(8,128)(2,1)S(1)}, bf16[72,896]{1,0:T(8,128)(2,1)S(1)}, u32[]{:S(2)}, u32[]{:S(2)}) collective-permute-start(bf16[72,896]{1,0:T(8,128)(2,1)S(1)} %get-tuple-element.28), channel_id=1, source_target_pairs={{0,4},{2,6},{4,0},{6,2},{8,12},{10,14},{12,8},{14,10},{1,5},{3,7},... | collective-permute-start | bytes 387080 | tf_op jit(solution)/shard_map/ppermute | solution.py:305
  47.2 7.7 %collective-permute-start.7 = (bf16[72,896]{1,0:T(8,128)(2,1)S(1)}, bf16[72,896]{1,0:T(8,128)(2,1)S(1)}, u32[]{:S(2)}, u32[]{:S(2)}) collective-permute-start(bf16[72,896]{1,0:T(8,128)(2,1)S(1)} %get-tuple-element.29), channel_id=1, source_target_pairs={{0,6},{2,4},{4,2},{6,0},{8,14},{10,12},{12,10},{14,8},{1,7},{3,5},... | collective-permute-start | bytes 387080 | tf_op jit(solution)/shard_map/ppermute | solution.py:305
  50.2 10.4 %collective-permute-start.21 = (bf16[72,896]{1,0:T(8,128)(2,1)S(1)}, bf16[72,896]{1,0:T(8,128)(2,1)S(1)}, u32[]{:S(2)}, u32[]{:S(2)}) collective-permute-start(bf16[72,896]{1,0:T(8,128)(2,1)S(1)} %add_convert_fusion), channel_id=1, source_target_pairs={{0,28},{2,30},{4,24},{6,26},{8,20},{10,22},{12,16},{14,18},{16,12}... | collective-permute-start | bytes 387080 | tf_op jit(solution)/shard_map/ppermute | solution.py:322
  55.0 7.5 %collective-permute-start.8 = (bf16[72,896]{1,0:T(8,128)(2,1)S(1)}, bf16[72,896]{1,0:T(8,128)(2,1)S(1)}, u32[]{:S(2)}, u32[]{:S(2)}) collective-permute-start(bf16[72,896]{1,0:T(8,128)(2,1)S(1)} %add_convert_fusion.1), channel_id=1, source_target_pairs={{0,16},{2,18},{4,20},{6,22},{8,24},{10,26},{12,28},{14,30},{16,0},... | collective-permute-start | bytes 387080 | tf_op jit(solution)/shard_map/ppermute | solution.py:322

commit v4 on v3

--- a/solution.py
+++ b/solution.py
@@ -145,19 +145,22 @@
     )(*(in_hbm(value) for value in (gate_cols, up_cols, down_cols)))
 
 
-def partial_products(blocks, staged, cuts, capacity):
+def partial_products(blocks, staged, capacity):
     rows = round_up(2 * capacity, 8)
     kept = round_up(capacity, 8)
     n_blocks = len(blocks)
     columns, width = staged.shape[0], staged.shape[1] // 3
 
     def body(*refs):
-        block_refs = refs[: n_blocks * len(cuts)]
-        staged_ref, out_ref, packed_ref = refs[n_blocks * len(cuts) :]
+        block_refs = list(refs[: sum(len(block) for block in blocks)])
+        staged_ref, out_ref, packed_ref = refs[len(block_refs) :]
         for i in range(n_blocks):
-            for part, (begin, end) in enumerate(cuts):
-                ref = block_refs[i * len(cuts) + part]
+            begin = 0
+            for _ in blocks[i]:
+                ref = block_refs.pop(0)
+                end = begin + ref.shape[1]
                 packed_ref[i * rows : (i + 1) * rows, begin:end] = ref[...]
+                begin = end
         packed = packed_ref[...]
         gate_up = dot(packed, staged_ref[:, : 2 * width])
         down = dot(packed, staged_ref[:, 2 * width :])
@@ -262,21 +265,29 @@
 
 def combine(routes, merged, n_experts, capacity, columns):
     chosen, n_tokens = routes.shape
-    rows, split = merged[0].shape
+    rows, split = merged[0][0].shape
 
     def body(routes_ref, *refs):
-        merged_refs, out_ref = refs[:-1], refs[-1]
+        refs, out_ref = list(refs[:-1]), refs[-1]
         relative, slot_rows = slots(routes_ref[...], n_experts)
         row = lax.broadcasted_iota(jnp.int32, (rows, n_tokens), 0)
         last = lax.axis_index("section") == lax.axis_size("section") - 1
+        blocks = []
+        for parts in merged:
+            block = refs.pop(0)[...]
+            if len(parts) > 1:
+                block = block.astype(F32)
+                for _ in parts[1:]:
+                    block = block + refs.pop(0)[...].astype(F32)
+            blocks.append(block.astype(BF16))
         for offset, begin, end in ((0, 0, split), (capacity, split, columns)):
             total = jnp.zeros((n_tokens, end - begin), F32)
-            for which, ref in enumerate(merged_refs):
+            for which, block in enumerate(blocks):
                 pick = jnp.zeros((rows, n_tokens), F32)
                 for k in range(chosen):
                     target = jnp.where(relative[k : k + 1] == which, slot_rows[k], -2 * rows)
                     pick = pick + (row == target + offset).astype(F32)
-                total = total + dot(pick.astype(BF16), ref[:, : end - begin], 0, 0)
+                total = total + dot(pick.astype(BF16), block[:, : end - begin], 0, 0)
             out_ref[:, begin:end] = jnp.where(last, 0.0, total).astype(BF16)
 
     return call(
@@ -284,7 +295,7 @@
         jax.ShapeDtypeStruct((n_tokens, columns), BF16),
         2 * 2 * n_tokens * columns * rows * len(merged),
         rows * columns * 2 * len(merged) + n_tokens * columns * 2,
-    )(routes, *merged)
+    )(routes, *[part for parts in merged for part in parts])
 
 
 def per_device(token_grads, routing, gate_weights, layer_inputs, w_gate, w_up, w_down):
@@ -313,9 +324,9 @@
             value, "expert", [(j, across(j, which)) for j in range(n_groups)]
         )
 
-    def homeward(value, which):
+    def homeward(value, target):
         pairs = [
-            (s * n_groups + j, (s - 1) % n_sections * n_groups + across(j, -which))
+            (s * n_groups + j, (s - 1) % n_sections * n_groups + target(j))
             for s in range(n_sections)
             for j in range(n_groups)
         ]
@@ -333,17 +344,19 @@
         for which in range(1, n_experts)
     ]
 
-    packed, slopes, merged = [], [], []
-    for which in range(n_experts):
-        head = heads[which]
+    shared = []
+    for which, head in enumerate(heads):
         by_y = [partner(part, 1) for part in head]
         by_z = [partner(part, 2) for part in head]
         by_d = [partner(by_z[0], 1)]
         if which:
             by_d.append(partner(by_y[1], 2))
-        part, rows_packed = partial_products(
-            (head, by_y, by_z, by_d), staged, cuts[which], capacity
-        )
+        shared.append((head, by_y, by_z, by_d))
+
+    packed, slopes = [], []
+
+    def returned(blocks):
+        part, rows_packed = partial_products(blocks, staged, capacity)
         parts = [part]
         for turn in range(1, n_replicas):
             pairs = [(r, (r + turn) % n_replicas) for r in range(n_replicas)]
@@ -351,10 +364,32 @@
         backs, slope = hidden_backward(parts, staged, capacity, split)
         packed.append(rows_packed)
         slopes.append(slope)
+        return list(backs)
+
+    backs = returned(shared[0][:3])
+    backs_by_expert = [backs]
+    for which in range(1, n_experts):
+        if which == 1:
+            backs = returned(shared[0][3:] + shared[1])
+            backs_by_expert[0].append(backs.pop(0))
+        else:
+            backs = returned(shared[which])
+        backs_by_expert.append(backs)
+    if n_experts == 1:
+        backs_by_expert[0] += returned(shared[0][3:])
+
+    merged = [
+        [
+            homeward(back, lambda j, step=step: j ^ step)
+            for step, back in enumerate(backs_by_expert[0])
+        ]
+    ]
+    for which in range(1, n_experts):
+        backs = backs_by_expert[which]
         total = backs[0].astype(F32)
         for step in range(1, SHARES):
             total = total + partner(backs[step], step).astype(F32)
-        merged.append(homeward(total.astype(BF16), which))
+        merged.append([homeward(total.astype(BF16), lambda j, which=which: across(j, -which))])
 
     upstream = combine(routes_next, merged, n_experts, capacity, columns)
     grad_gate, grad_up, grad_down = weight_grads(packed, slopes, width)

time: 63.8 us -> 70.3 us (1.10)
  waiting for transfers between devices: 21 us -> 33 us
  starting transfers between devices: 29.4 us -> 24.6 us
    ppermute x15 -> x12, waiting for transfers between devices: 11.4 us -> 16.5 us  [partner(): lax.ppermute(value, 'expert', [(j, j ^ step) for j in range(n_groups)])]
    ppermute x15 -> x12, starting transfers between devices: 16.3 us -> 12.3 us  [partner(): lax.ppermute(value, 'expert', [(j, j ^ step) for j in range(n_groups)])]
    ppermute x2, waiting for transfers between devices: 7.71 us -> 11.3 us  [crossing(): lax.ppermute(value, 'expert', [(j, across(j, which)) for j in range(n_gro...]
    ppermute x2 -> x5, waiting for transfers between devices: 1.84 us -> 5.2 us  [homeward(): return lax.ppermute(value, ('section', 'expert'), pairs)]
    ppermute x2, starting transfers between devices: 6.04 us -> 3.82 us  [crossing(): lax.ppermute(value, 'expert', [(j, across(j, which)) for j in range(n_gro...]
    ppermute x2 -> x5, starting transfers between devices: 5.64 us -> 6.9 us  [homeward(): return lax.ppermute(value, ('section', 'expert'), pairs)]
  transfers between devices with their start and end apart: 22 -> 22, of which waited for: 9 -> 8; matrix products, arithmetic and copies ran while one was open for 0% -> 0% of each run, Pallas kernels for 15% -> 11%
where the time goes in v4:
time: 70.3 us; the launch traced here: 70.1 us
  waiting for transfers between devices  33 us (47%)
  starting transfers between devices  24.6 us (35%)
  Pallas kernels  11.6 us (17%)
  between operations  0.75 us (1%)
    ppermute x12, waiting for transfers between devices, partner(): lax.ppermute(value, 'expert', [(j, j ^ step) for j in range(n_groups)])  16.5 us
    ppermute x12, starting transfers between devices, partner(): lax.ppermute(value, 'expert', [(j, j ^ step) for j in range(n_groups)])  12.3 us
    ppermute x2, waiting for transfers between devices, crossing(): lax.ppermute(value, 'expert', [(j, across(j, which)) for j in range(n_gro...  11.3 us
    ppermute x5, starting transfers between devices, homeward(): return lax.ppermute(value, ('section', 'expert'), pairs)  6.9 us
    ppermute x5, waiting for transfers between devices, homeward(): return lax.ppermute(value, ('section', 'expert'), pairs)  5.2 us
    ppermute x2, starting transfers between devices, crossing(): lax.ppermute(value, 'expert', [(j, across(j, which)) for j in range(n_gro...  3.82 us
    pallas_call x1, Pallas kernels, weight_grads(): call(body, tuple((jax.ShapeDtypeStruct((columns, width), BF16) for _ in r...  3.58 us
    pallas_call x2, Pallas kernels, partial_products(): call(body, (jax.ShapeDtypeStruct((n_blocks, kept, 3 * width), F32), jax.S...  2.03 us
  transfers between devices with their start and end apart: 22, of which 8 were waited for; matrix products, arithmetic and copies ran while one was open for 0% of the time, Pallas kernels for 11%

profile of v4, /device:TPU:0, one launch (start us, length us, event | category | flops | bytes accessed | tf_op | source)
XLA Modules:
  0.0 70.1 jit_solution(2402029107968883338)
XLA Ops:
  0.6 1.6 %shard_map.102 = (bf16[72,1792]{1,0:T(8,128)(2,1)S(1)}, bf16[72,896]{1,0:T(8,128)(2,1)S(1)}, bf16[72,896]{1,0:T(8,128)(2,1)S(1)}) custom-call(s32[1,64]{1,0:T(1,128)} %bitcast.18, f32[1,64]{1,0:T(1,128)} %bitcast.17, bf16[64,1792]{1,0:T(8,128)(2,1)} %bitcast.14, bf16[64,1792]{1,0:T(8,128)(2,1)} %bitcast.15), custom_call_target="tpu_custom_call" | custom-call | flops 66060288 | bytes 974848 | tf_op jit(solution)/shard_map/pallas_call | solution.py:109
  2.2 3.1 %collective-permute-start.2 = (bf16[72,1792]{1,0:T(8,128)(2,1)S(1)}, bf16[72,1792]{1,0:T(8,128)(2,1)S(1)}, u32[]{:S(2)}, u32[]{:S(2)}) collective-permute-start(bf16[72,1792]{1,0:T(8,128)(2,1)S(1)} %get-tuple-element.24.refs_0_), channel_id=1, source_target_pairs={{0,4},{2,6},{4,0},{6,2},{8,12},{10,14},{12,8},{14,10},{1,5},{3,7},... | collective-permute-start | bytes 774152 | tf_op jit(solution)/shard_map/ppermute | solution.py:316
  5.3 2.5 %collective-permute-start.8 = (bf16[72,896]{1,0:T(8,128)(2,1)S(1)}, bf16[72,896]{1,0:T(8,128)(2,1)S(1)}, u32[]{:S(2)}, u32[]{:S(2)}) collective-permute-start(bf16[72,896]{1,0:T(8,128)(2,1)S(1)} %get-tuple-element.29), channel_id=1, source_target_pairs={{0,12},{2,14},{4,8},{6,10},{8,4},{10,6},{12,0},{14,2},{1,13},{3,15... | collective-permute-start | bytes 387080 | tf_op jit(solution)/shard_map/ppermute | solution.py:323
  7.8 1.3 %collective-permute-start.9 = (bf16[72,896]{1,0:T(8,128)(2,1)S(1)}, bf16[72,896]{1,0:T(8,128)(2,1)S(1)}, u32[]{:S(2)}, u32[]{:S(2)}) collective-permute-start(bf16[72,896]{1,0:T(8,128)(2,1)S(1)} %get-tuple-element.30), channel_id=1, source_target_pairs={{0,12},{2,14},{4,8},{6,10},{8,4},{10,6},{12,0},{14,2},{1,13},{3,15... | collective-permute-start | bytes 387080 | tf_op jit(solution)/shard_map/ppermute | solution.py:323
  9.2 8.6 %collective-permute-done.8.refs_1_ = bf16[72,896]{1,0:T(8,128)(2,1)S(1)} collective-permute-done((bf16[72,896]{1,0:T(8,128)(2,1)S(1)}, bf16[72,896]{1,0:T(8,128)(2,1)S(1)}, u32[]{:S(2)}, u32[]{:S(2)}) %collective-permute-start.8) | collective-permute-done | bytes 129056 | tf_op jit(solution)/shard_map/ppermute | solution.py:323
  17.7 0.0 collective-permute-start.12
  17.7 2.7 %collective-permute-done.9.refs_2_ = bf16[72,896]{1,0:T(8,128)(2,1)S(1)} collective-permute-done((bf16[72,896]{1,0:T(8,128)(2,1)S(1)}, bf16[72,896]{1,0:T(8,128)(2,1)S(1)}, u32[]{:S(2)}, u32[]{:S(2)}) %collective-permute-start.9) | collective-permute-done | bytes 129056 | tf_op jit(solution)/shard_map/ppermute | solution.py:323
  20.4 1.5 %collective-permute-start.11 = (bf16[72,896]{1,0:T(8,128)(2,1)S(1)}, bf16[72,896]{1,0:T(8,128)(2,1)S(1)}, u32[]{:S(2)}, u32[]{:S(2)}) collective-permute-start(bf16[72,896]{1,0:T(8,128)(2,1)S(1)} %collective-permute-done.9.refs_2_), channel_id=1, source_target_pairs={{0,2},{2,0},{4,6},{6,4},{8,10},{10,8},{12,14},{14,12},{1,3},{3,1},... | collective-permute-start | bytes 387080 | tf_op jit(solution)/shard_map/ppermute | solution.py:316
  22.0 0.0 collective-permute-done.2.refs_2_
  22.0 0.5 collective-permute-start.7
  22.5 1.5 %collective-permute-start.10 = (bf16[72,896]{1,0:T(8,128)(2,1)S(1)}, bf16[72,896]{1,0:T(8,128)(2,1)S(1)}, u32[]{:S(2)}, u32[]{:S(2)}) collective-permute-start(bf16[72,896]{1,0:T(8,128)(2,1)S(1)} %collective-permute-done.8.refs_1_), channel_id=1, source_target_pairs={{0,2},{2,0},{4,6},{6,4},{8,10},{10,8},{12,14},{14,12},{1,3},{3,1},... | collective-permute-start | bytes 387080 | tf_op jit(solution)/shard_map/ppermute | solution.py:316
  24.0 0.0 collective-permute-start.13
  24.0 0.0 collective-permute-done.12.refs_5_
  24.0 0.5 collective-permute-start.14
  24.5 2.3 %collective-permute-done.11.refs_4_ = bf16[72,896]{1,0:T(8,128)(2,1)S(1)} collective-permute-done((bf16[72,896]{1,0:T(8,128)(2,1)S(1)}, bf16[72,896]{1,0:T(8,128)(2,1)S(1)}, u32[]{:S(2)}, u32[]{:S(2)}) %collective-permute-start.11) | collective-permute-done | bytes 129056 | tf_op jit(solution)/shard_map/ppermute | solution.py:316
  26.8 0.0 collective-permute-start.15
  26.8 1.8 %shard_map.103.refs_3_.refs_2_.refs_9_ = bf16[1792,768]{1,0:T(8,128)(2,1)S(1)} custom-call(bf16[1792,256]{1,0:T(8,128)(2,1)} %bitcast.11, bf16[1792,256]{1,0:T(8,128)(2,1)} %bitcast.12, bf16[1792,256]{1,0:T(8,128)(2,1)} %bitcast.13), custom_call_target="tpu_custom_call" | custom-call | flops 234881024 | bytes 5505024 | tf_op jit(solution)/shard_map/pallas_call | solution.py:138
  28.5 4.8 %collective-permute-done.10.refs_3_ = bf16[72,896]{1,0:T(8,128)(2,1)S(1)} collective-permute-done((bf16[72,896]{1,0:T(8,128)(2,1)S(1)}, bf16[72,896]{1,0:T(8,128)(2,1)S(1)}, u32[]{:S(2)}, u32[]{:S(2)}) %collective-permute-start.10) | collective-permute-done | bytes 129056 | tf_op jit(solution)/shard_map/ppermute | solution.py:316
  33.3 0.0 collective-permute-done.13.refs_6_
  33.4 1.4 %collective-permute-done.14.refs_7_ = bf16[72,896]{1,0:T(8,128)(2,1)S(1)} collective-permute-done((bf16[72,896]{1,0:T(8,128)(2,1)S(1)}, bf16[72,896]{1,0:T(8,128)(2,1)S(1)}, u32[]{:S(2)}, u32[]{:S(2)}) %collective-permute-start.14) | collective-permute-done | bytes 129056 | tf_op jit(solution)/shard_map/ppermute | solution.py:316
  34.7 0.0 collective-permute-done.15.refs_8_
  34.7 0.0 collective-permute-done.7.refs_0_
  34.7 1.2 %shard_map.106 = (f32[5,40,768]{2,1,0:T(8,128)S(1)}, bf16[360,1792]{1,0:T(8,128)(2,1)S(1)}) custom-call(bf16[72,1792]{1,0:T(8,128)(2,1)S(1)} %collective-permute-done.7.refs_0_, bf16[72,896]{1,0:T(8,128)(2,1)S(1)} %collective-permute-done.8.refs_1_, bf16[72,896]{1,0:T(8,128)(2,1)S(1)} %collective-permute-done.9.refs_2_, ...), custom_call_target="tpu_custom_call" | custom-call | flops 990904320 | bytes 5332992 | tf_op jit(solution)/shard_map/pallas_call | solution.py:174
  36.0 0.1 collective-permute-start.16
  36.1 1.6 %collective-permute-start.1 = (bf16[72,1792]{1,0:T(8,128)(2,1)S(1)}, bf16[72,1792]{1,0:T(8,128)(2,1)S(1)}, u32[]{:S(2)}, u32[]{:S(2)}) collective-permute-start(bf16[72,1792]{1,0:T(8,128)(2,1)S(1)} %get-tuple-element.24.refs_0_), channel_id=1, source_target_pairs={{0,2},{2,0},{4,6},{6,4},{8,10},{10,8},{12,14},{14,12},{1,3},{3,1},... | collective-permute-start | bytes 774152 | tf_op jit(solution)/shard_map/ppermute | solution.py:316
  37.6 7.0 %collective-permute-done.1.refs_1_ = bf16[72,1792]{1,0:T(8,128)(2,1)S(1)} collective-permute-done((bf16[72,1792]{1,0:T(8,128)(2,1)S(1)}, bf16[72,1792]{1,0:T(8,128)(2,1)S(1)}, u32[]{:S(2)}, u32[]{:S(2)}) %collective-permute-start.1) | collective-permute-done | bytes 258080 | tf_op jit(solution)/shard_map/ppermute | solution.py:316
  44.7 0.8 %shard_map.104 = (f32[3,40,768]{2,1,0:T(8,128)S(1)}, bf16[216,1792]{1,0:T(8,128)(2,1)S(1)}) custom-call(bf16[72,1792]{1,0:T(8,128)(2,1)S(1)} %get-tuple-element.24.refs_0_, bf16[72,1792]{1,0:T(8,128)(2,1)S(1)} %collective-permute-done.1.refs_1_, bf16[72,1792]{1,0:T(8,128)(2,1)S(1)} %collective-permute-done.2.refs_2_, ...), custom_call_target="tpu_custom_call" | custom-call | flops 594542592 | bytes 4300800 | tf_op jit(solution)/shard_map/pallas_call | solution.py:174
  45.5 0.0 copy-start
  45.5 0.1 collective-permute-start.3
  45.6 0.0 collective-permute-done.16.refs_1_
  45.6 0.8 %shard_map.107 = (bf16[72,896]{1,0:T(8,128)(2,1)S(1)}, bf16[72,896]{1,0:T(8,128)(2,1)S(1)}, bf16[72,896]{1,0:T(8,128)(2,1)S(1)}, bf16[72,896]{1,0:T(8,128)(2,1)S...) custom-call(f32[5,40,768]{2,1,0:T(8,128)S(1)} %get-tuple-element.31.refs_0_, ...), custom_call_target="tpu_custom_call" | custom-call | flops 367001600 | bytes 2551808 | tf_op jit(solution)/shard_map/pallas_call | solution.py:233
  46.4 1.6 %collective-permute-start.18 = (bf16[72,896]{1,0:T(8,128)(2,1)S(1)}, bf16[72,896]{1,0:T(8,128)(2,1)S(1)}, u32[]{:S(2)}, u32[]{:S(2)}) collective-permute-start(bf16[72,896]{1,0:T(8,128)(2,1)S(1)} %get-tuple-element.34), channel_id=1, source_target_pairs={{0,2},{2,0},{4,6},{6,4},{8,10},{10,8},{12,14},{14,12},{1,3},{3,1},... | collective-permute-start | bytes 387080 | tf_op jit(solution)/shard_map/ppermute | solution.py:316
  48.0 0.0 collective-permute-start.19
  48.0 2.0 %collective-permute-start.20 = (bf16[72,896]{1,0:T(8,128)(2,1)S(1)}, bf16[72,896]{1,0:T(8,128)(2,1)S(1)}, u32[]{:S(2)}, u32[]{:S(2)}) collective-permute-start(bf16[72,896]{1,0:T(8,128)(2,1)S(1)} %get-tuple-element.36), channel_id=1, source_target_pairs={{0,6},{2,4},{4,2},{6,0},{8,14},{10,12},{12,10},{14,8},{1,7},{3,5},... | collective-permute-start | bytes 387080 | tf_op jit(solution)/shard_map/ppermute | solution.py:316
  49.9 0.0 copy-done
  49.9 1.5 %collective-permute-start = (s32[1,64]{1,0:T(1,128)S(1)}, s32[1,64]{1,0:T(1,128)S(1)}, u32[]{:S(2)}, u32[]{:S(2)}) collective-permute-start(s32[1,64]{1,0:T(1,128)S(1)} %bitcast.19), channel_id=1, source_target_pairs={{0,16},{16,0},{1,17},{17,1},{2,18},{18,2},{3,19},{19,3},{4,20},{20... | collective-permute-start | bytes 776 | tf_op jit(solution)/shard_map/ppermute | solution.py:335
  51.4 0.0 collective-permute-done.3.refs_1_
  51.4 0.7 %shard_map.105 = (bf16[72,896]{1,0:T(8,128)(2,1)S(1)}, bf16[72,896]{1,0:T(8,128)(2,1)S(1)}, bf16[72,896]{1,0:T(8,128)(2,1)S(1)}, bf16[216,768]{1,0:T(8,128)(2,1)S(1)}) custom-call(f32[3,40,768]{2,1,0:T(8,128)S(1)} %get-tuple-element.25.refs_0_, f32[3,40,768]{2,1,0:T(8,128)S(1)} %collective-permute-done.3.refs_1_, ...), custom_call_target="tpu_custom_call" | custom-call | flops 220200960 | bytes 2265088 | tf_op jit(solution)/shard_map/pallas_call | solution.py:233
  52.2 0.6 collective-permute-start.4
  52.8 0.0 collective-permute-done.18
  52.8 2.4 %collective-permute-start.5 = (bf16[72,896]{1,0:T(8,128)(2,1)S(1)}, bf16[72,896]{1,0:T(8,128)(2,1)S(1)}, u32[]{:S(2)}, u32[]{:S(2)}) collective-permute-start(bf16[72,896]{1,0:T(8,128)(2,1)S(1)} %get-tuple-element.27), channel_id=1, source_target_pairs={{0,18},{2,16},{4,22},{6,20},{8,26},{10,24},{12,30},{14,28},{16,2},... | collective-permute-start | bytes 387080 | tf_op jit(solution)/shard_map/ppermute | solution.py:333
  55.2 0.0 collective-permute-done.19
  55.2 0.0 collective-permute-start.6
  55.2 1.0 %collective-permute-done.20 = bf16[72,896]{1,0:T(8,128)(2,1)S(1)} collective-permute-done((bf16[72,896]{1,0:T(8,128)(2,1)S(1)}, bf16[72,896]{1,0:T(8,128)(2,1)S(1)}, u32[]{:S(2)}, u32[]{:S(2)}) %collective-permute-start.20) | collective-permute-done | bytes 129056 | tf_op jit(solution)/shard_map/ppermute | solution.py:316
  56.2 2.6 %collective-permute-start.17 = (bf16[72,896]{1,0:T(8,128)(2,1)S(1)}, bf16[72,896]{1,0:T(8,128)(2,1)S(1)}, u32[]{:S(2)}, u32[]{:S(2)}) collective-permute-start(bf16[72,896]{1,0:T(8,128)(2,1)S(1)} %get-tuple-element.32), channel_id=1, source_target_pairs={{0,22},{2,20},{4,18},{6,16},{8,30},{10,28},{12,26},{14,24},{16,6},... | collective-permute-start | bytes 387080 | tf_op jit(solution)/shard_map/ppermute | solution.py:333
  58.8 0.1 add_convert_fusion
  58.9 0.0 collective-permute-done.routes_ref
  58.9 1.3 %collective-permute-start.21 = (bf16[72,896]{1,0:T(8,128)(2,1)S(1)}, bf16[72,896]{1,0:T(8,128)(2,1)S(1)}, u32[]{:S(2)}, u32[]{:S(2)}) collective-permute-start(bf16[72,896]{1,0:T(8,128)(2,1)S(1)} %add_convert_fusion), channel_id=1, source_target_pairs={{0,28},{2,30},{4,24},{6,26},{8,20},{10,22},{12,16},{14,18},{16,12}... | collective-permute-start | bytes 387080 | tf_op jit(solution)/shard_map/ppermute | solution.py:333
  60.2 3.6 %shard_map.109 = (bf16[1792,256]{1,0:T(8,128)(2,1)}, bf16[1792,256]{1,0:T(8,128)(2,1)}, bf16[1792,256]{1,0:T(8,128)(2,1)}) custom-call(bf16[216,1792]{1,0:T(8,128)(2,1)S(1)} %get-tuple-element.37.refs_0_, bf16[360,1792]{1,0:T(8,128)(2,1)S(1)} %get-tuple-element.38.refs_1_, bf16[216,768]{1,0:T(8,128)(2,1)S(1)} %get-tuple-element.39.refs_2_, ...), custom_call_target="tpu_custom_call" | custom-call | flops 1585446912 | bytes 4816896 | tf_op jit(solution)/shard_map/pallas_call | solution.py:258
  63.8 0.0 collective-permute-done.4.refs_0_
  63.8 5.2 %collective-permute-done.5.refs_1_ = bf16[72,896]{1,0:T(8,128)(2,1)S(1)} collective-permute-done((bf16[72,896]{1,0:T(8,128)(2,1)S(1)}, bf16[72,896]{1,0:T(8,128)(2,1)S(1)}, u32[]{:S(2)}, u32[]{:S(2)}) %collective-permute-start.5) | collective-permute-done | bytes 129056 | tf_op jit(solution)/shard_map/ppermute | solution.py:333
  69.0 0.0 collective-permute-done.6.refs_2_
  69.0 0.0 collective-permute-done.17.refs_3_
  69.0 0.0 collective-permute-done.21.refs_4_
  69.0 1.2 %shard_map.108 = bf16[64,1792]{1,0:T(8,128)(2,1)} custom-call(s32[1,64]{1,0:T(1,128)S(1)} %collective-permute-done.routes_ref, bf16[72,896]{1,0:T(8,128)(2,1)S(1)} %collective-permute-done.4.refs_0_, bf16[72,896]{1,0:T(8,128)(2,1)S(1)} %collective-permute-done.5.refs_1_, bf16[72,896]{1,0:T(8,128)(2,1)S(1)} %collective-permute-done.6.refs_2_, ...), custom_call_target="tpu_custom_call" | custom-call | flops 66060288 | bytes 745472 | tf_op jit(solution)/shard_map/pallas_call | solution.py:293
Async XLA Ops:
  2.2 19.8 %collective-permute-start.2 = (bf16[72,1792]{1,0:T(8,128)(2,1)S(1)}, bf16[72,1792]{1,0:T(8,128)(2,1)S(1)}, u32[]{:S(2)}, u32[]{:S(2)}) collective-permute-start(bf16[72,1792]{1,0:T(8,128)(2,1)S(1)} %get-tuple-element.24.refs_0_), channel_id=1, source_target_pairs={{0,4},{2,6},{4,0},{6,2},{8,12},{10,14},{12,8},{14,10},{1,5},{3,7},... | collective-permute-start | bytes 774152 | tf_op jit(solution)/shard_map/ppermute | solution.py:316
  5.3 12.4 %collective-permute-start.8 = (bf16[72,896]{1,0:T(8,128)(2,1)S(1)}, bf16[72,896]{1,0:T(8,128)(2,1)S(1)}, u32[]{:S(2)}, u32[]{:S(2)}) collective-permute-start(bf16[72,896]{1,0:T(8,128)(2,1)S(1)} %get-tuple-element.29), channel_id=1, source_target_pairs={{0,12},{2,14},{4,8},{6,10},{8,4},{10,6},{12,0},{14,2},{1,13},{3,15... | collective-permute-start | bytes 387080 | tf_op jit(solution)/shard_map/ppermute | solution.py:323
  7.8 12.6 %collective-permute-start.9 = (bf16[72,896]{1,0:T(8,128)(2,1)S(1)}, bf16[72,896]{1,0:T(8,128)(2,1)S(1)}, u32[]{:S(2)}, u32[]{:S(2)}) collective-permute-start(bf16[72,896]{1,0:T(8,128)(2,1)S(1)} %get-tuple-element.30), channel_id=1, source_target_pairs={{0,12},{2,14},{4,8},{6,10},{8,4},{10,6},{12,0},{14,2},{1,13},{3,15... | collective-permute-start | bytes 387080 | tf_op jit(solution)/shard_map/ppermute | solution.py:323
  17.7 6.3 %collective-permute-start.12 = (bf16[72,896]{1,0:T(8,128)(2,1)S(1)}, bf16[72,896]{1,0:T(8,128)(2,1)S(1)}, u32[]{:S(2)}, u32[]{:S(2)}) collective-permute-start(bf16[72,896]{1,0:T(8,128)(2,1)S(1)} %collective-permute-done.8.refs_1_), channel_id=1, source_target_pairs={{0,4},{2,6},{4,0},{6,2},{8,12},{10,14},{12,8},{14,10},{1,5},{3,7},... | collective-permute-start | bytes 387080 | tf_op jit(solution)/shard_map/ppermute | solution.py:316
  20.4 6.3 %collective-permute-start.11 = (bf16[72,896]{1,0:T(8,128)(2,1)S(1)}, bf16[72,896]{1,0:T(8,128)(2,1)S(1)}, u32[]{:S(2)}, u32[]{:S(2)}) collective-permute-start(bf16[72,896]{1,0:T(8,128)(2,1)S(1)} %collective-permute-done.9.refs_2_), channel_id=1, source_target_pairs={{0,2},{2,0},{4,6},{6,4},{8,10},{10,8},{12,14},{14,12},{1,3},{3,1},... | collective-permute-start | bytes 387080 | tf_op jit(solution)/shard_map/ppermute | solution.py:316
  22.0 12.8 %collective-permute-start.7 = (bf16[72,1792]{1,0:T(8,128)(2,1)S(1)}, bf16[72,1792]{1,0:T(8,128)(2,1)S(1)}, u32[]{:S(2)}, u32[]{:S(2)}) collective-permute-start(bf16[72,1792]{1,0:T(8,128)(2,1)S(1)} %collective-permute-done.2.refs_2_), channel_id=1, source_target_pairs={{0,2},{2,0},{4,6},{6,4},{8,10},{10,8},{12,14},{14,12},{1,3},{3,1},... | collective-permute-start | bytes 774152 | tf_op jit(solution)/shard_map/ppermute | solution.py:316
  22.5 10.9 %collective-permute-start.10 = (bf16[72,896]{1,0:T(8,128)(2,1)S(1)}, bf16[72,896]{1,0:T(8,128)(2,1)S(1)}, u32[]{:S(2)}, u32[]{:S(2)}) collective-permute-start(bf16[72,896]{1,0:T(8,128)(2,1)S(1)} %collective-permute-done.8.refs_1_), channel_id=1, source_target_pairs={{0,2},{2,0},{4,6},{6,4},{8,10},{10,8},{12,14},{14,12},{1,3},{3,1},... | collective-permute-start | bytes 387080 | tf_op jit(solution)/shard_map/ppermute | solution.py:316
  24.0 9.4 %collective-permute-start.13 = (bf16[72,896]{1,0:T(8,128)(2,1)S(1)}, bf16[72,896]{1,0:T(8,128)(2,1)S(1)}, u32[]{:S(2)}, u32[]{:S(2)}) collective-permute-start(bf16[72,896]{1,0:T(8,128)(2,1)S(1)} %collective-permute-done.9.refs_2_), channel_id=1, source_target_pairs={{0,4},{2,6},{4,0},{6,2},{8,12},{10,14},{12,8},{14,10},{1,5},{3,7},... | collective-permute-start | bytes 387080 | tf_op jit(solution)/shard_map/ppermute | solution.py:316
  24.0 10.7 %collective-permute-start.14 = (bf16[72,896]{1,0:T(8,128)(2,1)S(1)}, bf16[72,896]{1,0:T(8,128)(2,1)S(1)}, u32[]{:S(2)}, u32[]{:S(2)}) collective-permute-start(bf16[72,896]{1,0:T(8,128)(2,1)S(1)} %collective-permute-done.12.refs_5_), channel_id=1, source_target_pairs={{0,2},{2,0},{4,6},{6,4},{8,10},{10,8},{12,14},{14,12},{1,3},{3,1},... | collective-permute-start | bytes 387080 | tf_op jit(solution)/shard_map/ppermute | solution.py:316
  26.8 8.0 %collective-permute-start.15 = (bf16[72,896]{1,0:T(8,128)(2,1)S(1)}, bf16[72,896]{1,0:T(8,128)(2,1)S(1)}, u32[]{:S(2)}, u32[]{:S(2)}) collective-permute-start(bf16[72,896]{1,0:T(8,128)(2,1)S(1)} %collective-permute-done.11.refs_4_), channel_id=1, source_target_pairs={{0,4},{2,6},{4,0},{6,2},{8,12},{10,14},{12,8},{14,10},{1,5},{3,7},... | collective-permute-start | bytes 387080 | tf_op jit(solution)/shard_map/ppermute | solution.py:316
  36.0 9.6 %collective-permute-start.16 = (f32[5,40,768]{2,1,0:T(8,128)S(1)}, f32[5,40,768]{2,1,0:T(8,128)S(1)}, u32[]{:S(2)}, u32[]{:S(2)}) collective-permute-start(f32[5,40,768]{2,1,0:T(8,128)S(1)} %get-tuple-element.31.refs_0_), channel_id=1, source_target_pairs={{0,1},{1,0},{2,3},{3,2},{4,5},{5,4},{6,7},{7,6},{8,9},{9,8},{10,11... | collective-permute-start | bytes 1843208 | tf_op jit(solution)/shard_map/ppermute | solution.py:363
  36.1 8.6 %collective-permute-start.1 = (bf16[72,1792]{1,0:T(8,128)(2,1)S(1)}, bf16[72,1792]{1,0:T(8,128)(2,1)S(1)}, u32[]{:S(2)}, u32[]{:S(2)}) collective-permute-start(bf16[72,1792]{1,0:T(8,128)(2,1)S(1)} %get-tuple-element.24.refs_0_), channel_id=1, source_target_pairs={{0,2},{2,0},{4,6},{6,4},{8,10},{10,8},{12,14},{14,12},{1,3},{3,1},... | collective-permute-start | bytes 774152 | tf_op jit(solution)/shard_map/ppermute | solution.py:316
  45.5 4.5 %copy-start = (s32[1,64,1]{1,2,0:T(1,128)S(1)}, s32[1,64,1]{1,2,0:T(1,128)}, u32[]{:S(2)}) copy-start(s32[1,64,1]{1,2,0:T(1,128)} %param.8) | copy-start | bytes 772
  45.5 5.9 %collective-permute-start.3 = (f32[3,40,768]{2,1,0:T(8,128)S(1)}, f32[3,40,768]{2,1,0:T(8,128)S(1)}, u32[]{:S(2)}, u32[]{:S(2)}) collective-permute-start(f32[3,40,768]{2,1,0:T(8,128)S(1)} %get-tuple-element.25.refs_0_), channel_id=1, source_target_pairs={{0,1},{1,0},{2,3},{3,2},{4,5},{5,4},{6,7},{7,6},{8,9},{9,8},{10,11... | collective-permute-start | bytes 1105928 | tf_op jit(solution)/shard_map/ppermute | solution.py:363
  46.4 6.4 %collective-permute-start.18 = (bf16[72,896]{1,0:T(8,128)(2,1)S(1)}, bf16[72,896]{1,0:T(8,128)(2,1)S(1)}, u32[]{:S(2)}, u32[]{:S(2)}) collective-permute-start(bf16[72,896]{1,0:T(8,128)(2,1)S(1)} %get-tuple-element.34), channel_id=1, source_target_pairs={{0,2},{2,0},{4,6},{6,4},{8,10},{10,8},{12,14},{14,12},{1,3},{3,1},... | collective-permute-start | bytes 387080 | tf_op jit(solution)/shard_map/ppermute | solution.py:316
  48.0 7.2 %collective-permute-start.19 = (bf16[72,896]{1,0:T(8,128)(2,1)S(1)}, bf16[72,896]{1,0:T(8,128)(2,1)S(1)}, u32[]{:S(2)}, u32[]{:S(2)}) collective-permute-start(bf16[72,896]{1,0:T(8,128)(2,1)S(1)} %get-tuple-element.35), channel_id=1, source_target_pairs={{0,4},{2,6},{4,0},{6,2},{8,12},{10,14},{12,8},{14,10},{1,5},{3,7},... | collective-permute-start | bytes 387080 | tf_op jit(solution)/shard_map/ppermute | solution.py:316
  48.0 8.3 %collective-permute-start.20 = (bf16[72,896]{1,0:T(8,128)(2,1)S(1)}, bf16[72,896]{1,0:T(8,128)(2,1)S(1)}, u32[]{:S(2)}, u32[]{:S(2)}) collective-permute-start(bf16[72,896]{1,0:T(8,128)(2,1)S(1)} %get-tuple-element.36), channel_id=1, source_target_pairs={{0,6},{2,4},{4,2},{6,0},{8,14},{10,12},{12,10},{14,8},{1,7},{3,5},... | collective-permute-start | bytes 387080 | tf_op jit(solution)/shard_map/ppermute | solution.py:316
  49.9 9.0 %collective-permute-start = (s32[1,64]{1,0:T(1,128)S(1)}, s32[1,64]{1,0:T(1,128)S(1)}, u32[]{:S(2)}, u32[]{:S(2)}) collective-permute-start(s32[1,64]{1,0:T(1,128)S(1)} %bitcast.19), channel_id=1, source_target_pairs={{0,16},{16,0},{1,17},{17,1},{2,18},{18,2},{3,19},{19,3},{4,20},{20... | collective-permute-start | bytes 776 | tf_op jit(solution)/shard_map/ppermute | solution.py:335
  52.2 11.6 %collective-permute-start.4 = (bf16[72,896]{1,0:T(8,128)(2,1)S(1)}, bf16[72,896]{1,0:T(8,128)(2,1)S(1)}, u32[]{:S(2)}, u32[]{:S(2)}) collective-permute-start(bf16[72,896]{1,0:T(8,128)(2,1)S(1)} %get-tuple-element.26), channel_id=1, source_target_pairs={{0,16},{2,18},{4,20},{6,22},{8,24},{10,26},{12,28},{14,30},{16,0},... | collective-permute-start | bytes 387080 | tf_op jit(solution)/shard_map/ppermute | solution.py:333
  52.8 16.2 %collective-permute-start.5 = (bf16[72,896]{1,0:T(8,128)(2,1)S(1)}, bf16[72,896]{1,0:T(8,128)(2,1)S(1)}, u32[]{:S(2)}, u32[]{:S(2)}) collective-permute-start(bf16[72,896]{1,0:T(8,128)(2,1)S(1)} %get-tuple-element.27), channel_id=1, source_target_pairs={{0,18},{2,16},{4,22},{6,20},{8,26},{10,24},{12,30},{14,28},{16,2},... | collective-permute-start | bytes 387080 | tf_op jit(solution)/shard_map/ppermute | solution.py:333
  55.2 13.8 %collective-permute-start.6 = (bf16[72,896]{1,0:T(8,128)(2,1)S(1)}, bf16[72,896]{1,0:T(8,128)(2,1)S(1)}, u32[]{:S(2)}, u32[]{:S(2)}) collective-permute-start(bf16[72,896]{1,0:T(8,128)(2,1)S(1)} %get-tuple-element.28), channel_id=1, source_target_pairs={{0,20},{2,22},{4,16},{6,18},{8,28},{10,30},{12,24},{14,26},{16,4},... | collective-permute-start | bytes 387080 | tf_op jit(solution)/shard_map/ppermute | solution.py:333
  56.2 12.7 %collective-permute-start.17 = (bf16[72,896]{1,0:T(8,128)(2,1)S(1)}, bf16[72,896]{1,0:T(8,128)(2,1)S(1)}, u32[]{:S(2)}, u32[]{:S(2)}) collective-permute-start(bf16[72,896]{1,0:T(8,128)(2,1)S(1)} %get-tuple-element.32), channel_id=1, source_target_pairs={{0,22},{2,20},{4,18},{6,16},{8,30},{10,28},{12,26},{14,24},{16,6},... | collective-permute-start | bytes 387080 | tf_op jit(solution)/shard_map/ppermute | solution.py:333
  58.9 10.1 %collective-permute-start.21 = (bf16[72,896]{1,0:T(8,128)(2,1)S(1)}, bf16[72,896]{1,0:T(8,128)(2,1)S(1)}, u32[]{:S(2)}, u32[]{:S(2)}) collective-permute-start(bf16[72,896]{1,0:T(8,128)(2,1)S(1)} %add_convert_fusion), channel_id=1, source_target_pairs={{0,28},{2,30},{4,24},{6,26},{8,20},{10,22},{12,16},{14,18},{16,12}... | collective-permute-start | bytes 387080 | tf_op jit(solution)/shard_map/ppermute | solution.py:333
